TPU v7x, 32 devices: a whole 2x2x4 slice. The times are simulated.
32 devices in a mesh: src: 4 (over y, x), dst: 8 (over z, core).
Axes of the slice: x: 2, y: 2, z: 4, core: 2. Of those that a mesh axis runs over, the one named last changes fastest.
Arguments:
- edge_in: bfloat16 [32768, 512], P(('src', 'dst')), may hold values from -6 to 6
- atom_in: bfloat16 [2048, 256], P(('dst', 'src')), may hold values from -6 to 6
- targets: int32 [32768], P(('src', 'dst')), may hold values from 0 to 255
- reverse: int32 [32768], P(('src', 'dst')), may hold values from 0 to 127, as said below
- counts: int32 [4, 8, 8], P('src', 'dst'), may hold values from 2 to 128, as said below
- w_in: bfloat16 [256, 512], replicated, may hold values from -0.375 to 0.375
- gains: float32 [2, 512], replicated, may hold values from 0.1 to 1.9
- w_layers: bfloat16 [2, 512, 512], replicated, may hold values from -0.25 to 0.25
- w_rev: bfloat16 [512, 512], replicated, may hold values from -0.25 to 0.25
- w_down: bfloat16 [512, 256], replicated, may hold values from -0.25 to 0.25
- w_atom: bfloat16 [256, 256], replicated, may hold values from -0.375 to 0.375
Outputs:
- edge_out: bfloat16 [32768, 512], P(('src', 'dst'))
- atom_out: bfloat16 [2048, 256], P(('dst', 'src'))
Inputs may be any that keep to these rules, and one draw needn't show every extreme that they name: In every block k of tile (i, j), reverse maps the used slots one to one onto the used slots of block j of tile (i, k), and the two maps are inverse to each other; in block j of tile (i, j) it pairs used slots and is its own inverse. Unused slots map onto unused slots. Every count is even, and counts[i, j, k] equals counts[i, k, j].
All inputs are finite; a program needn't handle non-finite values.
Results may differ from a plain program's by a relative error of at most 0.014.
Values may be sent and summed in bfloat16 or wider, within the bound.
No kernel may reach another device: no remote copies, remote signals or barrier semaphores. Data moves between devices by JAX's collectives and lax.ppermute only.
A program may use at most 128 MiB of HBM per device.

v0:
```python
import jax
import jax.numpy as jnp
from jax import lax
from jax.sharding import PartitionSpec as P


def edge_layers(base, picked, gains, w_layers):
    state = base.astype(jnp.float32) + picked.astype(jnp.float32)
    for layer in range(w_layers.shape[0]):
        scale = lax.rsqrt(jnp.mean(state * state, axis=-1, keepdims=True) + 1e-06)
        normed = (state * scale * gains[layer]).astype(jnp.bfloat16)
        state = state + jax.nn.silu(
            jnp.dot(normed, w_layers[layer], preferred_element_type=jnp.float32)
        )
    return state


def on_device(
    edge_in, atom_in, targets, reverse, counts, w_in, gains, w_layers, w_rev, w_down, w_atom
):
    slots = edge_in.shape[0]
    blocks = counts.shape[2]
    width = slots // blocks
    place = jnp.arange(slots)
    owner = place // width
    used = place % width < jnp.repeat(counts.reshape(blocks), width)
    whole = lax.all_gather(atom_in, "src", axis=0, tiled=True)
    atom_proj = jnp.dot(whole, w_in, preferred_element_type=jnp.float32).astype(jnp.bfloat16)
    picked = jnp.take(atom_proj, targets, axis=0)
    source = owner * width + reverse
    state = edge_layers(edge_in, picked, gains, w_layers)
    sent = state.astype(jnp.bfloat16)
    arrived = lax.all_to_all(sent, "dst", split_axis=0, concat_axis=0, tiled=True)
    mirrored = jnp.take(arrived, source, axis=0)
    combined = jnp.where(
        used[:, None],
        state + jnp.dot(mirrored, w_rev, preferred_element_type=jnp.float32),
        jnp.float32(0.0),
    )
    edge_out = combined.astype(jnp.bfloat16)
    contrib = jnp.where(
        used[:, None],
        jnp.dot(edge_out, w_down, preferred_element_type=jnp.float32),
        jnp.float32(0.0),
    )
    count = atom_in.shape[0] * lax.axis_size("src")
    inside = (targets >= 0) & (targets < count)
    labels = jnp.where(inside, targets, count)
    summed = jax.ops.segment_sum(contrib, labels, num_segments=count + 1)
    agg = lax.psum_scatter(
        summed[:count].astype(jnp.bfloat16), "src", scatter_dimension=0, tiled=True
    ).astype(jnp.float32)
    act = jax.nn.silu(0.3 * agg).astype(jnp.bfloat16)
    atom_out = (
        atom_in.astype(jnp.float32) + jnp.dot(act, w_atom, preferred_element_type=jnp.float32)
    ).astype(jnp.bfloat16)
    return (edge_out, atom_out)


def solution(mesh):
    placed = (
        P(("src", "dst"), None),
        P(("dst", "src"), None),
        P(("src", "dst")),
        P(("src", "dst")),
        P("src", "dst", None),
        P(),
        P(),
        P(),
        P(),
        P(),
        P(),
    )
    return jax.shard_map(
        on_device,
        mesh=mesh,
        in_specs=placed,
        out_specs=(P(("src", "dst"), None), P(("dst", "src"), None)),
        check_vma=False,
    )
```

profile of v0, /device:TPU:0, one launch (start us, length us, event | category | flops | bytes accessed | tf_op | source)
XLA Modules:
  0.0 105.7 jit_solution(10639381983829888902)
XLA Ops:
  7.2 0.0 copy-start
  7.2 0.8 and_select_fusion
  7.9 0.7 compare_and_fusion.1
  8.6 10.1 %all_gather.3 = bf16[256,256]{1,0:T(8,128)(2,1)S(1)} all-gather(bf16[64,256]{1,0:T(8,128)(2,1)} %param.12), channel_id=1, replica_groups=mesh['src'=4,'dst'=8] {'src'}, dimensions={0}, use_global_device_ids=true | all-gather | bytes 163840 | tf_op jit(solution)/shard_map/all_gather | solution.py:27
  18.8 1.2 %convolution_convert_fusion = bf16[256,512]{1,0:T(8,128)(2,1)S(1)} fusion(bf16[256,256]{1,0:T(8,128)(2,1)S(1)} %all_gather.3, bf16[256,512]{1,0:T(8,128)(2,1)} %param.16), kind=kOutput, calls=%fused_computation.12 | convolution fusion | flops 67239936 | bytes 655360 | tf_op jit(solution)/shard_map/dot_general | solution.py:28
  19.9 0.0 copy-start.2
  20.0 4.0 %gather_fusion = bf16[1024,512]{1,0:T(8,128)(2,1)S(1)} fusion(bf16[256,512]{1,0:T(8,128)(2,1)S(1)} %convolution_convert_fusion, s32[1024]{0:T(1024)S(1)} %get-tuple-element.3), kind=kCustom, calls=%fused_computation | custom fusion | bytes 2101248 | tf_op jit(solution)/shard_map/jit(_take)/gather | solution.py:29
  23.9 0.0 copy-done.2
  23.9 0.0 copy-start.6
  23.9 0.0 copy-start.8
  24.0 0.7 multiply_reduce_fusion.1
  24.7 0.0 copy-done.6
  24.7 0.5 copy-done.8
  25.2 1.5 %multiply_reduce_fusion = (f32[1024]{0:T(1024)S(1)}, f32[1024,512]{1,0:T(8,128)S(1)}) fusion(bf16[2,512,512]{2,1,0:T(8,128)(2,1)S(1)} %copy-done.8, bf16[1024,512]{1,0:T(8,128)(2,1)S(1)} %copy-done.2, f32[512]{0:T(512)S(1)} %bitcast.25, f32[1024]{0:T(1024)S(1)} %add_rsqrt_fusion.1, bf16[1024,512]{1,0:T(8,128)(2,1)S(1)} %gather_fusion, ...), kind=kOutput, calls=%fused_computation.6 | convolution fusion | flops 546307072 | bytes 6828032 | tf_op jit(solution)/shard_map/dot_general | solution.py:13
  26.7 2.8 %fusion.32 = (bf16[1024,512]{1,0:T(8,128)(2,1)}, f32[1024,512]{1,0:T(8,128)}) fusion(f32[1024,512]{1,0:T(8,128)S(1)} %get-tuple-element.7, bf16[2,512,512]{2,1,0:T(8,128)(2,1)S(1)} %copy-done.8, f32[512]{0:T(512)S(1)} %bitcast.24, f32[1024]{0:T(1024)S(1)} %add_rsqrt_fusion), kind=kOutput, calls=%fused_computation.62 | convolution fusion | flops 541589504 | bytes 7870464 | tf_op jit(solution)/shard_map/dot_general | solution.py:13
  29.5 0.0 copy-start.5
  29.5 0.0 copy-start.7
  29.5 5.0 %all-to-all-start = ((bf16[8,128,512]{2,1,0:T(8,128)(2,1)}), bf16[8,128,512]{2,1,0:T(8,128)(2,1)S(1)}, u32[]{:S(2)}, u32[]{:S(2)}) async-start(bf16[8,128,512]{2,1,0:T(8,128)(2,1)} %bitcast.6), calls=%async_computation | async-start | bytes 2097152 | tf_op jit(solution)/shard_map/all_to_all | solution.py:33
  34.5 0.0 reduce-scatter.2.cloned.1.call-start
  34.5 0.0 copy-done.5
  34.5 0.0 copy-done.7
  34.6 0.1 fusion.18
  34.6 26.4 %all-to-all-done = bf16[8,128,512]{2,1,0:T(8,128)(2,1)S(1)} async-done(((bf16[8,128,512]{2,1,0:T(8,128)(2,1)}), bf16[8,128,512]{2,1,0:T(8,128)(2,1)S(1)}, u32[]{:S(2)}, u32[]{:S(2)}) %all-to-all-start) | async-done | bytes 1048608 | tf_op jit(solution)/shard_map/all_to_all | solution.py:33
  61.1 4.0 %gather_fusion.1 = bf16[1024,512]{1,0:T(8,128)(2,1)S(1)} fusion(bf16[1024,512]{1,0:T(8,128)(2,1)S(1)} %bitcast.23, s32[1024]{0:T(1024)S(1)} %broadcast_clamp_fusion), kind=kCustom, calls=%fused_computation.1 | custom fusion | bytes 2101248 | tf_op jit(solution)/shard_map/jit(_take)/gather | solution.py:34
  65.0 0.0 copy-done
  65.0 0.0 copy-start.3
  65.0 2.7 %select_convert_fusion = bf16[1024,512]{1,0:T(8,128)(2,1)S(1)} fusion(f32[1024,512]{1,0:T(8,128)} %get-tuple-element.9, bf16[512,512]{1,0:T(8,128)(2,1)S(1)} %copy-done, bf16[1024,512]{1,0:T(8,128)(2,1)S(1)} %gather_fusion.1, pred[1024]{0:T(1024)(128)(4,1)S(1)} %get-tuple-element.11, pred[1024]{0:T(1024)(128)(4,1)S(1)} %get-tuple-element.10), kind=kOutput, calls=%fused_computation.3 | convolution fusion | flops 538968064 | bytes 4720640 | tf_op jit(solution)/shard_map/dot_general | solution.py:37
  67.7 0.0 copy-done.3
  67.7 0.0 copy-start.1
  67.8 0.0 copy-start.4
  67.8 0.0 copy-start.9
  67.8 0.4 convolution_select_fusion
  68.2 6.1 %scatter_custom_fusion = f32[257,256]{1,0:T(8,128)S(1)} fusion(s32[1024]{0:T(1024)S(1)} %get-tuple-element.2, f32[1024,256]{1,0:T(8,128)S(1)} %convolution_select_fusion, f32[]{:T(128)} %constant.71.clone.1), kind=kCustom, calls=%fused_computation.30 | custom fusion | flops 262144 | bytes 263172 | tf_op jit(solution)/shard_map/scatter-add | solution.py:49
  74.3 0.7 slice.35
  75.0 0.0 reduce-scatter.2.cloned.1.call-update
  75.0 22.3 %reduce-scatter.2.cloned.1.call-done = bf16[64,256]{1,0:T(8,128)(2,1)} async-done(((bf16[256,256]{1,0:T(8,128)(2,1)}), bf16[64,256]{1,0:T(8,128)(2,1)}) %reduce-scatter.2.cloned.1.call-update) | async-done | bytes 32784 | tf_op jit(solution)/shard_map/reduce_scatter | solution.py:50
  97.3 0.0 copy-done.4
  97.3 0.0 copy-done.9
  97.3 1.5 %fusion = bf16[64,256]{1,0:T(8,128)(2,1)} fusion(bf16[256,256]{1,0:T(8,128)(2,1)S(1)} %copy-done.9, bf16[64,256]{1,0:T(8,128)(2,1)S(1)} %copy-done.4, bf16[64,256]{1,0:T(8,128)(2,1)} %reduce-scatter.2.cloned.1.call-done), kind=kOutput, calls=%fused_computation.14 | convolution fusion | flops 8552448 | bytes 229376 | tf_op jit(solution)/shard_map/dot_general | solution.py:55
  98.8 0.0 copy-done.1
  (4 shorter events, 0.0 us)
Async XLA Ops:
  7.2 57.9 %copy-start = (bf16[512,512]{1,0:T(8,128)(2,1)S(1)}, bf16[512,512]{1,0:T(8,128)(2,1)}, u32[]{:S(2)}) copy-start(bf16[512,512]{1,0:T(8,128)(2,1)} %param.19) | copy-start | bytes 1572868
  19.9 4.0 %copy-start.2 = (bf16[1024,512]{1,0:T(8,128)(2,1)S(1)}, bf16[1024,512]{1,0:T(8,128)(2,1)}, u32[]{:S(2)}) copy-start(bf16[1024,512]{1,0:T(8,128)(2,1)} %param.11) | copy-start | bytes 3145732
  23.9 0.7 copy-start.6
  23.9 1.2 %copy-start.8 = (bf16[2,512,512]{2,1,0:T(8,128)(2,1)S(1)}, bf16[2,512,512]{2,1,0:T(8,128)(2,1)}, u32[]{:S(2)}) copy-start(bf16[2,512,512]{2,1,0:T(8,128)(2,1)} %param.18) | copy-start | bytes 3145732
  29.5 5.0 %copy-start.5 = (s32[1024]{0:T(1024)S(1)}, s32[1024]{0:T(1024)}, u32[]{:S(2)}) copy-start(s32[1024]{0:T(1024)} %param.14) | copy-start | bytes 12292
  29.5 5.1 %copy-start.7 = (s32[1,1,8]{2,1,0:T(1,128)S(1)}, s32[1,1,8]{2,1,0:T(1,128)}, u32[]{:S(2)}) copy-start(s32[1,1,8]{2,1,0:T(1,128)} %param.15) | copy-start | bytes 100
  29.5 31.6 %all-to-all-start = ((bf16[8,128,512]{2,1,0:T(8,128)(2,1)}), bf16[8,128,512]{2,1,0:T(8,128)(2,1)S(1)}, u32[]{:S(2)}, u32[]{:S(2)}) async-start(bf16[8,128,512]{2,1,0:T(8,128)(2,1)} %bitcast.6), calls=%async_computation | async-start | bytes 2097152 | tf_op jit(solution)/shard_map/all_to_all | solution.py:33
  34.5 62.8 %reduce-scatter.2.cloned.1.call-start = ((), (), s32[]{:S(2)}) async-start(), calls=%async_computation.2 | async-start | bytes 163840 | tf_op jit(solution)/shard_map/reduce_scatter | solution.py:50
  65.0 2.7 %copy-start.3 = (bf16[512,256]{1,0:T(8,128)(2,1)S(1)}, bf16[512,256]{1,0:T(8,128)(2,1)}, u32[]{:S(2)}) copy-start(bf16[512,256]{1,0:T(8,128)(2,1)} %param.20) | copy-start | bytes 786436
  67.7 31.1 %copy-start.1 = (bf16[1024,512]{1,0:T(8,128)(2,1)}, bf16[1024,512]{1,0:T(8,128)(2,1)S(1)}, u32[]{:S(2)}) copy-start(bf16[1024,512]{1,0:T(8,128)(2,1)S(1)} %select_convert_fusion) | copy-start | bytes 3145732
  67.8 29.5 %copy-start.4 = (bf16[64,256]{1,0:T(8,128)(2,1)S(1)}, bf16[64,256]{1,0:T(8,128)(2,1)}, u32[]{:S(2)}) copy-start(bf16[64,256]{1,0:T(8,128)(2,1)} %param.12) | copy-start | bytes 98308
  67.8 29.5 %copy-start.9 = (bf16[256,256]{1,0:T(8,128)(2,1)S(1)}, bf16[256,256]{1,0:T(8,128)(2,1)}, u32[]{:S(2)}) copy-start(bf16[256,256]{1,0:T(8,128)(2,1)} %param.21) | copy-start | bytes 393220
Sparse Core Ops, SparseCore 0:
  75.1 22.1 reduce-scatter.1
where the time goes:
time: 106 us
  waiting for transfers between devices  48.7 us (46%)
  between operations  14.2 us (13%)
  blocking collectives  10.1 us (10%)
  matrix products  10.1 us (10%)
  local copies, waits for them, and re-layouts  9.13 us (9%)
  other arithmetic  8.33 us (8%)
  starting transfers between devices  5.03 us (5%)
    all_to_all x1, waiting for transfers between devices, on_device(): lax.all_to_all(sent, 'dst', split_axis=0, concat_axis=0, tiled=True)  26.4 us
    reduce_scatter x1, waiting for transfers between devices, on_device(): lax.psum_scatter(summed[:count].astype(jnp.bfloat16), 'src', scatter_dime...  22.3 us
    all_gather x1, blocking collectives, on_device(): whole = lax.all_gather(atom_in, 'src', axis=0, tiled=True)  10.1 us
    scatter-add x1, other arithmetic, on_device(): summed = jax.ops.segment_sum(contrib, labels, num_segments=count + 1)  6.09 us
    all_to_all x1, starting transfers between devices, on_device(): lax.all_to_all(sent, 'dst', split_axis=0, concat_axis=0, tiled=True)  5 us
    dot_general x2, matrix products, edge_layers(): jnp.dot(normed, w_layers[layer], preferred_element_type=jnp.float32)  4.3 us
    gather x1, local copies, waits for them, and re-layouts, on_device(): picked = jnp.take(atom_proj, targets, axis=0)  3.97 us
    gather x1, local copies, waits for them, and re-layouts, on_device(): mirrored = jnp.take(arrived, source, axis=0)  3.96 us
  transfers between devices with their start and end apart: 2, of which 2 were waited for; matrix products, arithmetic and copies ran while one was open for 0% of the time, Pallas kernels for 0%

commit v1 on v0

v1 whole, which is shorter than its diff:
```python
import functools

import jax
import jax.numpy as jnp
from jax import lax
from jax.experimental import pallas as pl
from jax.experimental.pallas import tpu as pltpu
from jax.sharding import PartitionSpec as P

F32 = jnp.float32
BF16 = jnp.bfloat16
LIMIT = 16 * 2**20


def dot(a, b):
    return jnp.dot(a, b, preferred_element_type=F32)


def column(row, width):
    n = row.shape[1]
    spread = jnp.transpose(jnp.broadcast_to(row, (n, n)))
    return jnp.concatenate([spread] * (width // n), axis=1)


def relabel(row, me, share):
    return (lax.div(row, share) ^ me) * share + lax.rem(row, share)


def layers(x, gains_ref, weights, first):
    feat = x.shape[1]
    for layer in range(gains_ref.shape[0]):
        scale = lax.rsqrt(jnp.mean(x * x, axis=-1, keepdims=True) + 1e-06)
        normed = (x * scale * gains_ref[layer : layer + 1, :]).astype(BF16)
        y = dot(normed, weights[first + layer * feat : first + (layer + 1) * feat])
        x = x + y / (1.0 + jnp.exp(-y))
    return x


def edge_kernel(ds, shards, meta, *refs):
    group = len(ds)
    edges = refs[:group]
    atoms = refs[group : group + shards]
    targets, reverse, gains, weights = refs[group + shards : group + shards + 4]
    x_ref, *msgs = refs[-1 - group :]
    width = edges[0].shape[0]
    share = atoms[0].shape[0]
    me = meta[0]
    hidden, feat = atoms[0].shape[1], edges[0].shape[1]
    w_rev = hidden + gains.shape[0] * feat
    table = jnp.concatenate([a[...] for a in atoms], axis=0)
    lanes = lax.broadcasted_iota(jnp.int32, (width, table.shape[0]), 1)
    picks = []
    for g in range(group):
        row = relabel(targets[pl.ds(meta[1] ^ ds[g], 1), :], me, share)
        picks.append((column(row, table.shape[0]) == lanes).astype(BF16))
    picked = dot(jnp.concatenate(picks, axis=0), table).astype(BF16)
    proj = dot(picked, weights[:hidden]).astype(BF16).astype(F32)
    x = jnp.concatenate([e[...] for e in edges], axis=0).astype(F32) + proj
    x = layers(x, gains, weights, hidden)
    sent = x.astype(BF16)
    rows = lax.broadcasted_iota(jnp.int32, (width, width), 0)
    slots = lax.broadcasted_iota(jnp.int32, (width, x.shape[1]), 0)
    turned = []
    for g in range(group):
        k = meta[1] ^ ds[g]
        used = meta[2 + k]
        mine = slice(g * width, (g + 1) * width)
        x_ref[mine, :] = jnp.where(slots < used, x[mine], 0.0)
        swap = (rows == reverse[pl.ds(k, 1), :]) & (rows < used)
        turned.append(dot(swap.astype(BF16), sent[mine]).astype(BF16))
    msg = dot(jnp.concatenate(turned, axis=0), weights[w_rev:]).astype(BF16)
    for g in range(group):
        msgs[g][...] = msg[g * width : (g + 1) * width]


def edge_group(ds, edge_in, atoms, targets, reverse, meta, gains, weights, after):
    _, width = targets.shape
    group = len(ds)
    feat = edge_in.shape[1]
    whole = pl.BlockSpec(memory_space=pltpu.VMEM)
    picks = [
        pl.BlockSpec((width, feat), functools.partial(lambda i, m, d: (m[1] ^ d, 0), d=d))
        for d in ds
    ]
    rows = group * width
    return pl.pallas_call(
        functools.partial(edge_kernel, ds, len(atoms)),
        out_shape=[jax.ShapeDtypeStruct((rows, feat), F32)]
        + [jax.ShapeDtypeStruct((width, feat), BF16)] * group,
        grid_spec=pltpu.PrefetchScalarGridSpec(
            num_scalar_prefetch=1,
            grid=(1,),
            in_specs=picks + [whole] * (len(atoms) + 4) + [pl.BlockSpec(memory_space=pl.ANY)] * len(after),
            out_specs=[whole] * (1 + group),
        ),
        cost_estimate=pl.CostEstimate(
            flops=2 * rows * feat * feat * 4, bytes_accessed=rows * feat * 8, transcendentals=rows * feat * 4
        ),
        compiler_params=pltpu.CompilerParams(vmem_limit_bytes=LIMIT),
        name="edge_group",
    )(meta, *[edge_in] * group, *atoms, targets, reverse, gains, weights, *after)


def finish_kernel(ds, first, last, shards, meta, *refs):
    group = len(ds)
    xs, msgs = refs[:group], refs[group : 2 * group]
    targets, w_down = refs[2 * group : 2 * group + 2]
    rest = list(refs[2 * group + 2 :])
    acc = None if first else rest[0]
    out, *sums = rest[0 if first else 2 : -2]
    stage, sems = rest[-2:]
    width = msgs[0].shape[0]
    copies = []
    for g, d in enumerate(ds):
        k = meta[1] ^ d
        x = xs[g][...] + msgs[g][...].astype(F32)
        stage[pl.ds(g * width, width), :] = x.astype(BF16)
        copies.append(
            pltpu.make_async_copy(
                stage.at[pl.ds(g * width, width), :],
                out.at[pl.ds(pl.multiple_of(k * width, width), width), :],
                sems.at[g],
            )
        )
        copies[g].start()
    contrib = dot(stage[...], w_down[...]).astype(BF16)
    atoms = sums[0].shape[0] * (shards if last else 1)
    place = lax.broadcasted_iota(jnp.int32, (atoms, width), 0)
    spread = [
        (place == relabel(targets[pl.ds(meta[1] ^ d, 1), :], meta[0], atoms // shards)).astype(BF16)
        for d in ds
    ]
    total = dot(jnp.concatenate(spread, axis=1), contrib)
    if not first:
        total = total + acc[...]
    if last:
        share = atoms // shards
        for p in range(shards):
            sums[p][...] = total[p * share : (p + 1) * share].astype(sums[p].dtype)
    else:
        sums[0][...] = total
    for copy in copies:
        copy.wait()


def finish(ds, xs, msgs, targets, meta, w_down, acc, out, total_rows, atoms, shards, last):
    _, width = targets.shape
    feat, hidden = w_down.shape
    first = acc is None
    group = len(ds)
    whole = pl.BlockSpec(memory_space=pltpu.VMEM)
    far = pl.BlockSpec(memory_space=pl.ANY)
    share = atoms // shards
    if last:
        tail = [jax.ShapeDtypeStruct((share, hidden), F32)]
        tail += [jax.ShapeDtypeStruct((share, hidden), BF16)] * (shards - 1)
    else:
        tail = [jax.ShapeDtypeStruct((atoms, hidden), F32)]
    return pl.pallas_call(
        functools.partial(finish_kernel, ds, first, last, shards),
        out_shape=[jax.ShapeDtypeStruct((total_rows, feat), BF16)] + tail,
        grid_spec=pltpu.PrefetchScalarGridSpec(
            num_scalar_prefetch=1,
            grid=(1,),
            in_specs=[
                pl.BlockSpec((width, feat), functools.partial(lambda i, m, at: (at, 0), at=at))
                for _, at in xs
            ]
            + [whole] * (group + 2)
            + ([] if first else [whole, far]),
            out_specs=[far] + [whole] * len(tail),
            scratch_shapes=[
                pltpu.VMEM((group * width, feat), BF16),
                pltpu.SemaphoreType.DMA((group,)),
            ],
        ),
        input_output_aliases={} if first else {2 * group + 4: 0},
        cost_estimate=pl.CostEstimate(
            flops=4 * group * width * feat * hidden,
            bytes_accessed=group * width * feat * 8,
            transcendentals=0,
        ),
        compiler_params=pltpu.CompilerParams(vmem_limit_bytes=LIMIT),
        name="finish",
    )(meta, *[x for x, _ in xs], *msgs, targets, w_down, *([] if first else [acc, out]))


def atom_kernel(atom_in, w_atom, *refs):
    *parts, out = refs
    agg = parts[0][...]
    for part in parts[1:]:
        agg = agg + part[...].astype(F32)
    v = 0.3 * agg
    act = (v / (1.0 + jnp.exp(-v))).astype(BF16)
    out[...] = (atom_in[...].astype(F32) + dot(act, w_atom[...])).astype(BF16)


def edge_order(blocks):
    half = blocks // 2
    near = [[d, d + 1] for d in range(2, half, 2)]
    far = [[d, d + 1] for d in range(half + 2, blocks, 2)]
    return [[half], [half + 1]] + near + far + [[1, 0]]


def on_device(
    edge_in, atom_in, targets, reverse, counts, w_in, gains, w_layers, w_rev, w_down, w_atom
):
    slots, feat = edge_in.shape
    blocks = counts.shape[2]
    width = slots // blocks
    shards = lax.axis_size("src")
    atoms = atom_in.shape[0] * shards
    me, part = lax.axis_index("src"), lax.axis_index("dst")
    meta = jnp.concatenate([jnp.stack([me, part]).astype(jnp.int32), counts.reshape(blocks)])
    targets = targets.reshape(blocks, width)
    reverse = reverse.reshape(blocks, width)

    def over(size, d):
        return [(s, s ^ d) for s in range(size)]

    held = [atom_in]
    for p in range(1, shards):
        held.append(lax.ppermute(atom_in, "src", over(shards, p)))
    weights = jnp.concatenate([w_in, w_layers.reshape(-1, feat), w_rev], axis=0)
    xs, msgs, after = {}, {}, []
    for ds in edge_order(blocks):
        x, *sent = edge_group(ds, edge_in, held, targets, reverse, meta, gains, weights, after)
        after = [x]
        for g, d in enumerate(ds):
            xs[d] = (x, g)
            msgs[d] = sent[g]
            if d:
                msgs[d] = lax.ppermute(sent[g], "dst", over(blocks, d))
    acc = out = None
    half = blocks // 2
    for at in [0, half] + list(range(2, half, 2)) + list(range(half + 2, blocks, 2)):
        ds = [at, at + 1]
        last = at + 2 == blocks
        out, *sums = finish(
            ds, [xs[d] for d in ds], [msgs[d] for d in ds], targets, meta,
            w_down, acc, out, slots, atoms, shards, last,
        )
        acc = sums[0]
    parts = [sums[0]]
    for p in range(1, shards):
        parts.append(lax.ppermute(sums[p], "src", over(shards, p)))
    atom_out = pl.pallas_call(
        atom_kernel,
        out_shape=jax.ShapeDtypeStruct(atom_in.shape, BF16),
        compiler_params=pltpu.CompilerParams(vmem_limit_bytes=LIMIT),
        name="atom_update",
    )(atom_in, w_atom, *parts)
    return (out, atom_out)


def solution(mesh):
    placed = (
        P(("src", "dst"), None),
        P(("dst", "src"), None),
        P(("src", "dst")),
        P(("src", "dst")),
        P("src", "dst", None),
        P(),
        P(),
        P(),
        P(),
        P(),
        P(),
    )
    return jax.shard_map(
        on_device,
        mesh=mesh,
        in_specs=placed,
        out_specs=(P(("src", "dst"), None), P(("dst", "src"), None)),
        check_vma=False,
    )
```

time: 106 us -> 49.9 us (0.47)
  waiting for transfers between devices: 48.7 us -> 14.3 us
  Pallas kernels: 0 us -> 16.1 us
  between operations: 14.2 us -> 0.8 us
  starting transfers between devices: 5.03 us -> 16.7 us
  matrix products: 10.1 us -> 0 us
  blocking collectives: 10.1 us -> 0 us
  local copies, waits for them, and re-layouts: 9.13 us -> 0.04 us
  other arithmetic: 8.33 us -> 1.71 us
    all_to_all x1 -> x0, waiting for transfers between devices: 26.4 us -> none  [on_device(): lax.all_to_all(sent, 'dst', split_axis=0, concat_axis=0, tiled=True)]
    reduce_scatter x1 -> x0, waiting for transfers between devices: 22.3 us -> none  [on_device(): lax.psum_scatter(summed[:count].astype(jnp.bfloat16), 'src', scatter_dime...]
    ppermute x0 -> x13, starting transfers between devices: none -> 16.7 us  [the longest x7 8.58 us: on_device(): msgs[d] = lax.ppermute(sent[g], 'dst', over(blocks, d))]
    pallas_call x0 -> x10, Pallas kernels: none -> 16.1 us  [the longest x5 10.1 us: edge_group(): pl.pallas_call(functools.partial(edge_kernel, ds, len(atoms)), out_shape=...]
    ppermute x0 -> x13, waiting for transfers between devices: none -> 14.3 us  [the longest x7 8.73 us: on_device(): msgs[d] = lax.ppermute(sent[g], 'dst', over(blocks, d))]
    dot_general x6 -> x0, matrix products: 10.1 us -> none  [the longest x2 4.3 us: edge_layers(): jnp.dot(normed, w_layers[layer], preferred_element_type=jnp.float32)]
    all_gather x1 -> x0, blocking collectives: 10.1 us -> none  [on_device(): whole = lax.all_gather(atom_in, 'src', axis=0, tiled=True)]
    gather x2 -> x0, local copies, waits for them, and re-layouts: 7.92 us -> none  [the longest x1 3.97 us: on_device(): picked = jnp.take(atom_proj, targets, axis=0)]
  transfers between devices with their start and end apart: 2 -> 13, of which waited for: 2 -> 9; matrix products, arithmetic and copies ran while one was open for 0% -> 3% of each run, Pallas kernels for 0% -> 24%
where the time goes in v1:
time: 49.9 us; the launch traced here: 49.7 us
  starting transfers between devices  16.7 us (33%)
  Pallas kernels  16.1 us (32%)
  waiting for transfers between devices  14.3 us (29%)
  other arithmetic  1.71 us (3%)
  between operations  0.8 us (2%)
    pallas_call x5, Pallas kernels, edge_group(): pl.pallas_call(functools.partial(edge_kernel, ds, len(atoms)), out_shape=...  10.1 us
    ppermute x7, waiting for transfers between devices, on_device(): msgs[d] = lax.ppermute(sent[g], 'dst', over(blocks, d))  8.73 us
    ppermute x7, starting transfers between devices, on_device(): msgs[d] = lax.ppermute(sent[g], 'dst', over(blocks, d))  8.58 us
    pallas_call x4, Pallas kernels, finish(): pl.pallas_call(functools.partial(finish_kernel, ds, first, last, shards),...  5.2 us
    ppermute x3, starting transfers between devices, on_device(): held.append(lax.ppermute(atom_in, 'src', over(shards, p)))  4.57 us
    ppermute x3, starting transfers between devices, on_device(): parts.append(lax.ppermute(sums[p], 'src', over(shards, p)))  3.55 us
    ppermute x3, waiting for transfers between devices, on_device(): held.append(lax.ppermute(atom_in, 'src', over(shards, p)))  3.25 us
    ppermute x3, waiting for transfers between devices, on_device(): parts.append(lax.ppermute(sums[p], 'src', over(shards, p)))  2.37 us
  transfers between devices with their start and end apart: 13, of which 9 were waited for; matrix products, arithmetic and copies ran while one was open for 3% of the time, Pallas kernels for 24%

profile of v1, /device:TPU:0, one launch (start us, length us, event | category | flops | bytes accessed | tf_op | source)
XLA Modules:
  0.0 49.7 jit_solution(4990068465496509682)
XLA Ops:
  0.6 3.0 %collective-permute-start = (bf16[64,256]{1,0:T(8,128)(2,1)}, bf16[64,256]{1,0:T(8,128)(2,1)S(1)}, u32[]{:S(2)}, u32[]{:S(2)}) collective-permute-start(bf16[64,256]{1,0:T(8,128)(2,1)} %atom_in.1), channel_id=1, source_target_pairs={{0,8},{8,0},{16,24},{24,16},{1,9},{9,1},{17,25},{25,17},{2,10},{10... | collective-permute-start | bytes 98312 | tf_op jit(solution)/shard_map/ppermute | solution.py:223
  3.7 1.5 %collective-permute-start.1 = (bf16[64,256]{1,0:T(8,128)(2,1)}, bf16[64,256]{1,0:T(8,128)(2,1)S(1)}, u32[]{:S(2)}, u32[]{:S(2)}) collective-permute-start(bf16[64,256]{1,0:T(8,128)(2,1)} %atom_in.1), channel_id=1, source_target_pairs={{0,16},{8,24},{16,0},{24,8},{1,17},{9,25},{17,1},{25,9},{2,18},{10... | collective-permute-start | bytes 98312 | tf_op jit(solution)/shard_map/ppermute | solution.py:223
  5.2 0.0 collective-permute-start.2
  5.2 0.0 copy-start.7
  5.2 0.0 copy-start
  5.2 0.0 copy-start.2
  5.2 0.0 copy-start.3
  5.2 0.0 copy-start.5
  5.2 0.0 copy-start.6
  5.2 1.6 %pad_maximum_fusion.refs_8_.refs_9_ = bf16[1792,512]{1,0:T(8,128)(2,1)S(1)} fusion(bf16[512,512]{1,0:T(8,128)(2,1)} %param.19, bf16[1024,512]{1,0:T(8,128)(2,1)} %bitcast.20, bf16[256,512]{1,0:T(8,128)(2,1)} %param.16), kind=kLoop, calls=%fused_computation | loop fusion | flops 5505024 | bytes 3670016 | tf_op jit(solution)/shard_map/concatenate | solution.py:224
  6.9 0.0 copy-done.7
  6.9 0.1 pad_add_fusion.meta
  7.0 0.0 collective-permute-done.refs_2_.refs_3_
  7.0 0.8 %collective-permute-done.1.refs_3_.refs_4_ = bf16[64,256]{1,0:T(8,128)(2,1)S(1)} collective-permute-done((bf16[64,256]{1,0:T(8,128)(2,1)}, bf16[64,256]{1,0:T(8,128)(2,1)S(1)}, u32[]{:S(2)}, u32[]{:S(2)}) %collective-permute-start.1) | collective-permute-done | bytes 32800 | tf_op jit(solution)/shard_map/ppermute | solution.py:223
  7.8 2.4 %collective-permute-done.2.refs_4_.refs_5_ = bf16[64,256]{1,0:T(8,128)(2,1)S(1)} collective-permute-done((bf16[64,256]{1,0:T(8,128)(2,1)}, bf16[64,256]{1,0:T(8,128)(2,1)S(1)}, u32[]{:S(2)}, u32[]{:S(2)}) %collective-permute-start.2) | collective-permute-done | bytes 32800 | tf_op jit(solution)/shard_map/ppermute | solution.py:223
  10.2 0.0 copy-done
  10.2 0.0 copy-done.2
  10.2 0.0 copy-done.3
  10.2 0.0 copy-done.5
  10.2 0.0 copy-done.6
  10.2 1.8 %edge_group.5 = (f32[128,512]{1,0:T(8,128)S(1)}, bf16[128,512]{1,0:T(8,128)(2,1)S(1)}) custom-call(s32[10]{0:T(128)S(1)} %pad_add_fusion.meta, bf16[1024,512]{1,0:T(8,128)(2,1)S(1)} %copy-done, bf16[64,256]{1,0:T(8,128)(2,1)S(1)} %copy-done.2, bf16[64,256]{1,0:T(8,128)(2,1)S(1)} %collective-permute-done.refs_2_.refs_3_, ...), custom_call_target="tpu_custom_call" | custom-call | flops 268435456 | bytes 524288 | tf_op jit(solution)/shard_map/edge_group/pallas_call | solution.py:86
  12.1 2.7 %collective-permute-start.7 = (bf16[128,512]{1,0:T(8,128)(2,1)S(1)}, bf16[128,512]{1,0:T(8,128)(2,1)S(1)}, u32[]{:S(2)}, u32[]{:S(2)}) collective-permute-start(bf16[128,512]{1,0:T(8,128)(2,1)S(1)} %get-tuple-element.34), channel_id=1, source_target_pairs={{0,4},{1,5},{2,6},{3,7},{4,0},{5,1},{6,2},{7,3},{8,12},{9,13},{10,... | collective-permute-start | bytes 393224 | tf_op jit(solution)/shard_map/ppermute | solution.py:233
  14.8 1.8 %edge_group.6 = (f32[128,512]{1,0:T(8,128)S(1)}, bf16[128,512]{1,0:T(8,128)(2,1)S(1)}) custom-call(s32[10]{0:T(128)S(1)} %pad_add_fusion.meta, bf16[1024,512]{1,0:T(8,128)(2,1)S(1)} %copy-done, bf16[64,256]{1,0:T(8,128)(2,1)S(1)} %copy-done.2, bf16[64,256]{1,0:T(8,128)(2,1)S(1)} %collective-permute-done.refs_2_.refs_3_, ...), custom_call_target="tpu_custom_call" | custom-call | flops 268435456 | bytes 524288 | tf_op jit(solution)/shard_map/edge_group/pallas_call | solution.py:86
  16.6 2.1 %edge_group.7 = (f32[256,512]{1,0:T(8,128)S(1)}, bf16[128,512]{1,0:T(8,128)(2,1)S(1)}, bf16[128,512]{1,0:T(8,128)(2,1)S(1)}) custom-call(s32[10]{0:T(128)S(1)} %pad_add_fusion.meta, bf16[1024,512]{1,0:T(8,128)(2,1)S(1)} %copy-done, bf16[1024,512]{1,0:T(8,128)(2,1)S(1)} %copy-done, bf16[64,256]{1,0:T(8,128)(2,1)S(1)} %copy-done.2, ...), custom_call_target="tpu_custom_call" | custom-call | flops 536870912 | bytes 1048576 | tf_op jit(solution)/shard_map/edge_group/pallas_call | solution.py:86
  18.8 2.1 %edge_group.8 = (f32[256,512]{1,0:T(8,128)S(1)}, bf16[128,512]{1,0:T(8,128)(2,1)S(1)}, bf16[128,512]{1,0:T(8,128)(2,1)S(1)}) custom-call(s32[10]{0:T(128)S(1)} %pad_add_fusion.meta, bf16[1024,512]{1,0:T(8,128)(2,1)S(1)} %copy-done, bf16[1024,512]{1,0:T(8,128)(2,1)S(1)} %copy-done, bf16[64,256]{1,0:T(8,128)(2,1)S(1)} %copy-done.2, ...), custom_call_target="tpu_custom_call" | custom-call | flops 536870912 | bytes 1048576 | tf_op jit(solution)/shard_map/edge_group/pallas_call | solution.py:86
  20.9 0.0 copy-start.1
  20.9 2.1 %edge_group.9 = (f32[256,512]{1,0:T(8,128)S(1)}, bf16[128,512]{1,0:T(8,128)(2,1)S(1)}, bf16[128,512]{1,0:T(8,128)(2,1)S(1)}) custom-call(s32[10]{0:T(128)S(1)} %pad_add_fusion.meta, bf16[1024,512]{1,0:T(8,128)(2,1)S(1)} %copy-done, bf16[1024,512]{1,0:T(8,128)(2,1)S(1)} %copy-done, bf16[64,256]{1,0:T(8,128)(2,1)S(1)} %copy-done.2, ...), custom_call_target="tpu_custom_call" | custom-call | flops 536870912 | bytes 1048576 | tf_op jit(solution)/shard_map/edge_group/pallas_call | solution.py:86
  23.1 0.1 collective-permute-start.9
  23.1 0.4 collective-permute-start.8
  23.6 1.6 %collective-permute-start.5 = (bf16[128,512]{1,0:T(8,128)(2,1)S(1)}, bf16[128,512]{1,0:T(8,128)(2,1)S(1)}, u32[]{:S(2)}, u32[]{:S(2)}) collective-permute-start(bf16[128,512]{1,0:T(8,128)(2,1)S(1)} %get-tuple-element.32), channel_id=1, source_target_pairs={{0,2},{1,3},{2,0},{3,1},{4,6},{5,7},{6,4},{7,5},{8,10},{9,11},{10,... | collective-permute-start | bytes 393224 | tf_op jit(solution)/shard_map/ppermute | solution.py:233
  25.2 0.0 collective-permute-start.6
  25.2 0.0 collective-permute-done.7.refs_2_
  25.2 3.4 %collective-permute-start.3 = (bf16[128,512]{1,0:T(8,128)(2,1)S(1)}, bf16[128,512]{1,0:T(8,128)(2,1)S(1)}, u32[]{:S(2)}, u32[]{:S(2)}) collective-permute-start(bf16[128,512]{1,0:T(8,128)(2,1)S(1)} %get-tuple-element.30), channel_id=1, source_target_pairs={{0,6},{1,7},{2,4},{3,5},{4,2},{5,3},{6,0},{7,1},{8,14},{9,15},{10,... | collective-permute-start | bytes 393224 | tf_op jit(solution)/shard_map/ppermute | solution.py:233
  28.6 0.0 collective-permute-done.9.refs_3_
  28.6 0.4 collective-permute-start.4
  29.0 0.0 copy-done.1
  29.0 1.3 %finish.4 = (bf16[1024,512]{1,0:T(8,128)(2,1)}, f32[256,256]{1,0:T(8,128)S(1)}) custom-call(s32[10]{0:T(128)S(1)} %pad_add_fusion.meta, f32[256,512]{1,0:T(8,128)S(1)} %get-tuple-element.36.refs_0_.refs_1_, f32[256,512]{1,0:T(8,128)S(1)} %get-tuple-element.36.refs_0_.refs_1_, bf16[128,512]{1,0:T(8,128)(2,1)S(1)} %get-tuple-element.37.refs_2_, ...), custom_call_target="tpu_custom_call" | custom-call | flops 134217728 | bytes 1048576 | tf_op jit(solution)/shard_map/finish/pallas_call | solution.py:159
  30.3 1.9 %collective-permute-done.8.refs_3_ = bf16[128,512]{1,0:T(8,128)(2,1)S(1)} collective-permute-done((bf16[128,512]{1,0:T(8,128)(2,1)S(1)}, bf16[128,512]{1,0:T(8,128)(2,1)S(1)}, u32[]{:S(2)}, u32[]{:S(2)}) %collective-permute-start.8) | collective-permute-done | bytes 131104 | tf_op jit(solution)/shard_map/ppermute | solution.py:233
  32.2 1.3 %finish.5 = (bf16[1024,512]{1,0:T(8,128)(2,1)}, f32[256,256]{1,0:T(8,128)S(1)}) custom-call(s32[10]{0:T(128)S(1)} %pad_add_fusion.meta, f32[128,512]{1,0:T(8,128)S(1)} %get-tuple-element.26.refs_9_.refs_0_, f32[128,512]{1,0:T(8,128)S(1)} %get-tuple-element.27.refs_10_.refs_1_, ...), custom_call_target="tpu_custom_call", output_to_operand_aliasing={{0}: (8, {})} | custom-call | flops 134217728 | bytes 1048576 | tf_op jit(solution)/shard_map/finish/pallas_call | solution.py:159
  33.6 0.0 collective-permute-done.5.refs_2_
  33.6 0.2 collective-permute-done.6.refs_3_
  33.8 1.3 %finish.6 = (bf16[1024,512]{1,0:T(8,128)(2,1)}, f32[256,256]{1,0:T(8,128)S(1)}) custom-call(s32[10]{0:T(128)S(1)} %pad_add_fusion.meta, f32[256,512]{1,0:T(8,128)S(1)} %get-tuple-element.28.refs_10_.refs_0_.refs_1_, f32[256,512]{1,0:T(8,128)S(1)} %get-tuple-element.28.refs_10_.refs_0_.refs_1_, ...), custom_call_target="tpu_custom_call", output_to_operand_aliasing={{0}: (8, {})} | custom-call | flops 134217728 | bytes 1048576 | tf_op jit(solution)/shard_map/finish/pallas_call | solution.py:159
  35.1 0.0 copy-start.4
  35.1 5.0 %collective-permute-done.3.refs_2_ = bf16[128,512]{1,0:T(8,128)(2,1)S(1)} collective-permute-done((bf16[128,512]{1,0:T(8,128)(2,1)S(1)}, bf16[128,512]{1,0:T(8,128)(2,1)S(1)}, u32[]{:S(2)}, u32[]{:S(2)}) %collective-permute-start.3) | collective-permute-done | bytes 131104 | tf_op jit(solution)/shard_map/ppermute | solution.py:233
  40.1 1.6 %collective-permute-done.4.refs_3_ = bf16[128,512]{1,0:T(8,128)(2,1)S(1)} collective-permute-done((bf16[128,512]{1,0:T(8,128)(2,1)S(1)}, bf16[128,512]{1,0:T(8,128)(2,1)S(1)}, u32[]{:S(2)}, u32[]{:S(2)}) %collective-permute-start.4) | collective-permute-done | bytes 131104 | tf_op jit(solution)/shard_map/ppermute | solution.py:233
  41.7 1.3 %finish.7 = (bf16[1024,512]{1,0:T(8,128)(2,1)}, f32[64,256]{1,0:T(8,128)S(1)}, bf16[64,256]{1,0:T(8,128)(2,1)S(1)}, bf16[64,256]{1,0:T(8,128)(2,1)S(1)}, bf16[64,256]{1,0:T(8,128)(2,1)S(1)}) custom-call(s32[10]{0:T(128)S(1)} %pad_add_fusion.meta, f32[256,512]{1,0:T(8,128)S(1)} %get-tuple-element.29.refs_10_.refs_0_.refs_1_, ...), custom_call_target="tpu_custom_call", output_to_operand_aliasing={{0}: (8, {})} | custom-call | flops 134217728 | bytes 1048576 | tf_op jit(solution)/shard_map/finish/pallas_call | solution.py:159
  43.0 0.6 %collective-permute-start.10 = (bf16[64,256]{1,0:T(8,128)(2,1)S(1)}, bf16[64,256]{1,0:T(8,128)(2,1)S(1)}, u32[]{:S(2)}, u32[]{:S(2)}) collective-permute-start(bf16[64,256]{1,0:T(8,128)(2,1)S(1)} %get-tuple-element.47), channel_id=1, source_target_pairs={{0,8},{8,0},{16,24},{24,16},{1,9},{9,1},{17,25},{25,17},{2,10},{10... | collective-permute-start | bytes 98312 | tf_op jit(solution)/shard_map/ppermute | solution.py:246
  43.6 0.5 %collective-permute-start.11 = (bf16[64,256]{1,0:T(8,128)(2,1)S(1)}, bf16[64,256]{1,0:T(8,128)(2,1)S(1)}, u32[]{:S(2)}, u32[]{:S(2)}) collective-permute-start(bf16[64,256]{1,0:T(8,128)(2,1)S(1)} %get-tuple-element.48), channel_id=1, source_target_pairs={{0,16},{8,24},{16,0},{24,8},{1,17},{9,25},{17,1},{25,9},{2,18},{10... | collective-permute-start | bytes 98312 | tf_op jit(solution)/shard_map/ppermute | solution.py:246
  44.1 2.4 %collective-permute-start.12 = (bf16[64,256]{1,0:T(8,128)(2,1)S(1)}, bf16[64,256]{1,0:T(8,128)(2,1)S(1)}, u32[]{:S(2)}, u32[]{:S(2)}) collective-permute-start(bf16[64,256]{1,0:T(8,128)(2,1)S(1)} %get-tuple-element.49), channel_id=1, source_target_pairs={{0,24},{8,16},{16,8},{24,0},{1,25},{9,17},{17,9},{25,1},{2,26},{10... | collective-permute-start | bytes 98312 | tf_op jit(solution)/shard_map/ppermute | solution.py:246
  46.5 0.4 collective-permute-done.10.refs_1_
  47.0 0.6 %collective-permute-done.11.refs_2_ = bf16[64,256]{1,0:T(8,128)(2,1)S(1)} collective-permute-done((bf16[64,256]{1,0:T(8,128)(2,1)S(1)}, bf16[64,256]{1,0:T(8,128)(2,1)S(1)}, u32[]{:S(2)}, u32[]{:S(2)}) %collective-permute-start.11) | collective-permute-done | bytes 32800 | tf_op jit(solution)/shard_map/ppermute | solution.py:246
  47.5 1.4 %collective-permute-done.12.refs_3_ = bf16[64,256]{1,0:T(8,128)(2,1)S(1)} collective-permute-done((bf16[64,256]{1,0:T(8,128)(2,1)S(1)}, bf16[64,256]{1,0:T(8,128)(2,1)S(1)}, u32[]{:S(2)}, u32[]{:S(2)}) %collective-permute-start.12) | collective-permute-done | bytes 32800 | tf_op jit(solution)/shard_map/ppermute | solution.py:246
  48.9 0.0 copy-done.4
  48.9 0.8 %atom_update.1 = bf16[64,256]{1,0:T(8,128)(2,1)} custom-call(bf16[64,256]{1,0:T(8,128)(2,1)S(1)} %copy-done.2, bf16[256,256]{1,0:T(8,128)(2,1)S(1)} %copy-done.4, f32[64,256]{1,0:T(8,128)S(1)} %get-tuple-element.46.refs_0_, bf16[64,256]{1,0:T(8,128)(2,1)S(1)} %collective-permute-done.10.refs_1_, bf16[64,256]{1,0:T(8,128)(2,1)S(1)} %collective-permute-done.11.refs_2_, ...), custom_call_target="tpu_custom_call" | custom-call | tf_op jit(solution)/shard_map/atom_update/pallas_call | solution.py:247
Async XLA Ops:
  0.6 6.3 %collective-permute-start = (bf16[64,256]{1,0:T(8,128)(2,1)}, bf16[64,256]{1,0:T(8,128)(2,1)S(1)}, u32[]{:S(2)}, u32[]{:S(2)}) collective-permute-start(bf16[64,256]{1,0:T(8,128)(2,1)} %atom_in.1), channel_id=1, source_target_pairs={{0,8},{8,0},{16,24},{24,16},{1,9},{9,1},{17,25},{25,17},{2,10},{10... | collective-permute-start | bytes 98312 | tf_op jit(solution)/shard_map/ppermute | solution.py:223
  3.7 4.1 %collective-permute-start.1 = (bf16[64,256]{1,0:T(8,128)(2,1)}, bf16[64,256]{1,0:T(8,128)(2,1)S(1)}, u32[]{:S(2)}, u32[]{:S(2)}) collective-permute-start(bf16[64,256]{1,0:T(8,128)(2,1)} %atom_in.1), channel_id=1, source_target_pairs={{0,16},{8,24},{16,0},{24,8},{1,17},{9,25},{17,1},{25,9},{2,18},{10... | collective-permute-start | bytes 98312 | tf_op jit(solution)/shard_map/ppermute | solution.py:223
  5.2 5.0 %collective-permute-start.2 = (bf16[64,256]{1,0:T(8,128)(2,1)}, bf16[64,256]{1,0:T(8,128)(2,1)S(1)}, u32[]{:S(2)}, u32[]{:S(2)}) collective-permute-start(bf16[64,256]{1,0:T(8,128)(2,1)} %atom_in.1), channel_id=1, source_target_pairs={{0,24},{8,16},{16,8},{24,0},{1,25},{9,17},{17,9},{25,1},{2,26},{10... | collective-permute-start | bytes 98312 | tf_op jit(solution)/shard_map/ppermute | solution.py:223
  5.2 1.7 %copy-start.7 = (s32[1,1,8]{2,1,0:T(1,128)S(1)}, s32[1,1,8]{2,1,0:T(1,128)}, u32[]{:S(2)}) copy-start(s32[1,1,8]{2,1,0:T(1,128)} %param.15) | copy-start | bytes 100
  5.2 5.0 %copy-start = (bf16[1024,512]{1,0:T(8,128)(2,1)S(1)}, bf16[1024,512]{1,0:T(8,128)(2,1)}, u32[]{:S(2)}) copy-start(bf16[1024,512]{1,0:T(8,128)(2,1)} %refs_1_.9) | copy-start | bytes 3145732
  5.2 5.0 %copy-start.2 = (bf16[64,256]{1,0:T(8,128)(2,1)S(1)}, bf16[64,256]{1,0:T(8,128)(2,1)}, u32[]{:S(2)}) copy-start(bf16[64,256]{1,0:T(8,128)(2,1)} %atom_in.1) | copy-start | bytes 98308
  5.2 5.0 %copy-start.3 = (s32[1024]{0:T(1024)S(1)}, s32[1024]{0:T(1024)}, u32[]{:S(2)}) copy-start(s32[1024]{0:T(1024)} %param.13) | copy-start | bytes 12292
  5.2 5.0 %copy-start.5 = (s32[1024]{0:T(1024)S(1)}, s32[1024]{0:T(1024)}, u32[]{:S(2)}) copy-start(s32[1024]{0:T(1024)} %param.14) | copy-start | bytes 12292
  5.2 5.0 %copy-start.6 = (f32[2,512]{1,0:T(2,128)S(1)}, f32[2,512]{1,0:T(2,128)}, u32[]{:S(2)}) copy-start(f32[2,512]{1,0:T(2,128)} %refs_8_.5) | copy-start | bytes 12292
  12.1 13.1 %collective-permute-start.7 = (bf16[128,512]{1,0:T(8,128)(2,1)S(1)}, bf16[128,512]{1,0:T(8,128)(2,1)S(1)}, u32[]{:S(2)}, u32[]{:S(2)}) collective-permute-start(bf16[128,512]{1,0:T(8,128)(2,1)S(1)} %get-tuple-element.34), channel_id=1, source_target_pairs={{0,4},{1,5},{2,6},{3,7},{4,0},{5,1},{6,2},{7,3},{8,12},{9,13},{10,... | collective-permute-start | bytes 393224 | tf_op jit(solution)/shard_map/ppermute | solution.py:233
  20.9 8.1 %copy-start.1 = (bf16[512,256]{1,0:T(8,128)(2,1)S(1)}, bf16[512,256]{1,0:T(8,128)(2,1)}, u32[]{:S(2)}) copy-start(bf16[512,256]{1,0:T(8,128)(2,1)} %refs_5_.7) | copy-start | bytes 786436
  23.1 5.5 %collective-permute-start.9 = (bf16[128,512]{1,0:T(8,128)(2,1)S(1)}, bf16[128,512]{1,0:T(8,128)(2,1)S(1)}, u32[]{:S(2)}, u32[]{:S(2)}) collective-permute-start(bf16[128,512]{1,0:T(8,128)(2,1)S(1)} %get-tuple-element.38), channel_id=1, source_target_pairs={{0,1},{1,0},{2,3},{3,2},{4,5},{5,4},{6,7},{7,6},{8,9},{9,8},{10,11... | collective-permute-start | bytes 393224 | tf_op jit(solution)/shard_map/ppermute | solution.py:233
  23.1 9.1 %collective-permute-start.8 = (bf16[128,512]{1,0:T(8,128)(2,1)S(1)}, bf16[128,512]{1,0:T(8,128)(2,1)S(1)}, u32[]{:S(2)}, u32[]{:S(2)}) collective-permute-start(bf16[128,512]{1,0:T(8,128)(2,1)S(1)} %get-tuple-element.35), channel_id=1, source_target_pairs={{0,5},{1,4},{2,7},{3,6},{4,1},{5,0},{6,3},{7,2},{8,13},{9,12},{10,... | collective-permute-start | bytes 393224 | tf_op jit(solution)/shard_map/ppermute | solution.py:233
  23.6 10.0 %collective-permute-start.5 = (bf16[128,512]{1,0:T(8,128)(2,1)S(1)}, bf16[128,512]{1,0:T(8,128)(2,1)S(1)}, u32[]{:S(2)}, u32[]{:S(2)}) collective-permute-start(bf16[128,512]{1,0:T(8,128)(2,1)S(1)} %get-tuple-element.32), channel_id=1, source_target_pairs={{0,2},{1,3},{2,0},{3,1},{4,6},{5,7},{6,4},{7,5},{8,10},{9,11},{10,... | collective-permute-start | bytes 393224 | tf_op jit(solution)/shard_map/ppermute | solution.py:233
  25.2 8.6 %collective-permute-start.6 = (bf16[128,512]{1,0:T(8,128)(2,1)S(1)}, bf16[128,512]{1,0:T(8,128)(2,1)S(1)}, u32[]{:S(2)}, u32[]{:S(2)}) collective-permute-start(bf16[128,512]{1,0:T(8,128)(2,1)S(1)} %get-tuple-element.33), channel_id=1, source_target_pairs={{0,3},{1,2},{2,1},{3,0},{4,7},{5,6},{6,5},{7,4},{8,11},{9,10},{10,... | collective-permute-start | bytes 393224 | tf_op jit(solution)/shard_map/ppermute | solution.py:233
  25.2 14.9 %collective-permute-start.3 = (bf16[128,512]{1,0:T(8,128)(2,1)S(1)}, bf16[128,512]{1,0:T(8,128)(2,1)S(1)}, u32[]{:S(2)}, u32[]{:S(2)}) collective-permute-start(bf16[128,512]{1,0:T(8,128)(2,1)S(1)} %get-tuple-element.30), channel_id=1, source_target_pairs={{0,6},{1,7},{2,4},{3,5},{4,2},{5,3},{6,0},{7,1},{8,14},{9,15},{10,... | collective-permute-start | bytes 393224 | tf_op jit(solution)/shard_map/ppermute | solution.py:233
  28.6 13.1 %collective-permute-start.4 = (bf16[128,512]{1,0:T(8,128)(2,1)S(1)}, bf16[128,512]{1,0:T(8,128)(2,1)S(1)}, u32[]{:S(2)}, u32[]{:S(2)}) collective-permute-start(bf16[128,512]{1,0:T(8,128)(2,1)S(1)} %get-tuple-element.31), channel_id=1, source_target_pairs={{0,7},{1,6},{2,5},{3,4},{4,3},{5,2},{6,1},{7,0},{8,15},{9,14},{10,... | collective-permute-start | bytes 393224 | tf_op jit(solution)/shard_map/ppermute | solution.py:233
  35.1 13.8 %copy-start.4 = (bf16[256,256]{1,0:T(8,128)(2,1)S(1)}, bf16[256,256]{1,0:T(8,128)(2,1)}, u32[]{:S(2)}) copy-start(bf16[256,256]{1,0:T(8,128)(2,1)} %w_atom.1) | copy-start | bytes 393220
  43.0 4.0 %collective-permute-start.10 = (bf16[64,256]{1,0:T(8,128)(2,1)S(1)}, bf16[64,256]{1,0:T(8,128)(2,1)S(1)}, u32[]{:S(2)}, u32[]{:S(2)}) collective-permute-start(bf16[64,256]{1,0:T(8,128)(2,1)S(1)} %get-tuple-element.47), channel_id=1, source_target_pairs={{0,8},{8,0},{16,24},{24,16},{1,9},{9,1},{17,25},{25,17},{2,10},{10... | collective-permute-start | bytes 98312 | tf_op jit(solution)/shard_map/ppermute | solution.py:246
  43.6 3.9 %collective-permute-start.11 = (bf16[64,256]{1,0:T(8,128)(2,1)S(1)}, bf16[64,256]{1,0:T(8,128)(2,1)S(1)}, u32[]{:S(2)}, u32[]{:S(2)}) collective-permute-start(bf16[64,256]{1,0:T(8,128)(2,1)S(1)} %get-tuple-element.48), channel_id=1, source_target_pairs={{0,16},{8,24},{16,0},{24,8},{1,17},{9,25},{17,1},{25,9},{2,18},{10... | collective-permute-start | bytes 98312 | tf_op jit(solution)/shard_map/ppermute | solution.py:246
  44.1 4.8 %collective-permute-start.12 = (bf16[64,256]{1,0:T(8,128)(2,1)S(1)}, bf16[64,256]{1,0:T(8,128)(2,1)S(1)}, u32[]{:S(2)}, u32[]{:S(2)}) collective-permute-start(bf16[64,256]{1,0:T(8,128)(2,1)S(1)} %get-tuple-element.49), channel_id=1, source_target_pairs={{0,24},{8,16},{16,8},{24,0},{1,25},{9,17},{17,9},{25,1},{2,26},{10... | collective-permute-start | bytes 98312 | tf_op jit(solution)/shard_map/ppermute | solution.py:246

commit v2 on v1

--- a/solution.py
+++ b/solution.py
@@ -38,14 +38,13 @@
 
 def edge_kernel(ds, shards, meta, *refs):
     group = len(ds)
-    edges = refs[:group]
-    atoms = refs[group : group + shards]
-    targets, reverse, gains, weights = refs[group + shards : group + shards + 4]
+    edge_in, *atoms = refs[: 1 + shards]
+    targets, reverse, gains, weights = refs[1 + shards : 5 + shards]
     x_ref, *msgs = refs[-1 - group :]
-    width = edges[0].shape[0]
+    width = targets.shape[1]
     share = atoms[0].shape[0]
     me = meta[0]
-    hidden, feat = atoms[0].shape[1], edges[0].shape[1]
+    hidden, feat = atoms[0].shape[1], edge_in.shape[1]
     w_rev = hidden + gains.shape[0] * feat
     table = jnp.concatenate([a[...] for a in atoms], axis=0)
     lanes = lax.broadcasted_iota(jnp.int32, (width, table.shape[0]), 1)
@@ -55,7 +54,9 @@
         picks.append((column(row, table.shape[0]) == lanes).astype(BF16))
     picked = dot(jnp.concatenate(picks, axis=0), table).astype(BF16)
     proj = dot(picked, weights[:hidden]).astype(BF16).astype(F32)
-    x = jnp.concatenate([e[...] for e in edges], axis=0).astype(F32) + proj
+    starts = [pl.multiple_of((meta[1] ^ d) * width, width) for d in ds]
+    x = jnp.concatenate([edge_in[pl.ds(start, width), :] for start in starts], axis=0)
+    x = x.astype(F32) + proj
     x = layers(x, gains, weights, hidden)
     sent = x.astype(BF16)
     rows = lax.broadcasted_iota(jnp.int32, (width, width), 0)
@@ -78,10 +79,6 @@
     group = len(ds)
     feat = edge_in.shape[1]
     whole = pl.BlockSpec(memory_space=pltpu.VMEM)
-    picks = [
-        pl.BlockSpec((width, feat), functools.partial(lambda i, m, d: (m[1] ^ d, 0), d=d))
-        for d in ds
-    ]
     rows = group * width
     return pl.pallas_call(
         functools.partial(edge_kernel, ds, len(atoms)),
@@ -90,7 +87,7 @@
         grid_spec=pltpu.PrefetchScalarGridSpec(
             num_scalar_prefetch=1,
             grid=(1,),
-            in_specs=picks + [whole] * (len(atoms) + 4) + [pl.BlockSpec(memory_space=pl.ANY)] * len(after),
+            in_specs=[whole] * (len(atoms) + 5) + [pl.BlockSpec(memory_space=pl.ANY)] * len(after),
             out_specs=[whole] * (1 + group),
         ),
         cost_estimate=pl.CostEstimate(
@@ -98,10 +95,10 @@
         ),
         compiler_params=pltpu.CompilerParams(vmem_limit_bytes=LIMIT),
         name="edge_group",
-    )(meta, *[edge_in] * group, *atoms, targets, reverse, gains, weights, *after)
-
-
-def finish_kernel(ds, first, last, shards, meta, *refs):
+    )(meta, edge_in, *atoms, targets, reverse, gains, weights, *after)
+
+
+def finish_kernel(ds, ats, first, last, shards, meta, *refs):
     group = len(ds)
     xs, msgs = refs[:group], refs[group : 2 * group]
     targets, w_down = refs[2 * group : 2 * group + 2]
@@ -113,7 +110,7 @@
     copies = []
     for g, d in enumerate(ds):
         k = meta[1] ^ d
-        x = xs[g][...] + msgs[g][...].astype(F32)
+        x = xs[g][pl.ds(ats[g] * width, width), :] + msgs[g][...].astype(F32)
         stage[pl.ds(g * width, width), :] = x.astype(BF16)
         copies.append(
             pltpu.make_async_copy(
@@ -157,16 +154,12 @@
     else:
         tail = [jax.ShapeDtypeStruct((atoms, hidden), F32)]
     return pl.pallas_call(
-        functools.partial(finish_kernel, ds, first, last, shards),
+        functools.partial(finish_kernel, ds, [at for _, at in xs], first, last, shards),
         out_shape=[jax.ShapeDtypeStruct((total_rows, feat), BF16)] + tail,
         grid_spec=pltpu.PrefetchScalarGridSpec(
             num_scalar_prefetch=1,
             grid=(1,),
-            in_specs=[
-                pl.BlockSpec((width, feat), functools.partial(lambda i, m, at: (at, 0), at=at))
-                for _, at in xs
-            ]
-            + [whole] * (group + 2)
+            in_specs=[whole] * (2 * group + 2)
             + ([] if first else [whole, far]),
             out_specs=[far] + [whole] * len(tail),
             scratch_shapes=[
@@ -199,7 +192,7 @@
     half = blocks // 2
     near = [[d, d + 1] for d in range(2, half, 2)]
     far = [[d, d + 1] for d in range(half + 2, blocks, 2)]
-    return [[half], [half + 1]] + near + far + [[1, 0]]
+    return [[half, half + 1]] + near + far + [[1, 0]]
 
 
 def on_device(
@@ -233,9 +226,11 @@
                 msgs[d] = lax.ppermute(sent[g], "dst", over(blocks, d))
     acc = out = None
     half = blocks // 2
-    for at in [0, half] + list(range(2, half, 2)) + list(range(half + 2, blocks, 2)):
-        ds = [at, at + 1]
-        last = at + 2 == blocks
+    groups = [[0, 1, half, half + 1]]
+    rest = list(range(2, half)) + list(range(half + 2, blocks))
+    groups += [rest[n : n + 4] for n in range(0, len(rest), 4)]
+    for ds in groups:
+        last = ds is groups[-1]
         out, *sums = finish(
             ds, [xs[d] for d in ds], [msgs[d] for d in ds], targets, meta,
             w_down, acc, out, slots, atoms, shards, last,

time: 49.9 us -> 45.5 us (0.912)
  Pallas kernels: 16.1 us -> 12.2 us
  waiting for transfers between devices: 14.3 us -> 13 us
  starting transfers between devices: 16.7 us -> 17.7 us
    pallas_call x4 -> x2, Pallas kernels: 5.2 us -> 2.84 us  [finish(): pl.pallas_call(functools.partial(finish_kernel, ds, [at for _, at in xs],...]
    pallas_call x5 -> x4, Pallas kernels: 10.1 us -> 8.55 us  [edge_group(): pl.pallas_call(functools.partial(edge_kernel, ds, len(atoms)), out_shape=...]
    ppermute x7, waiting for transfers between devices: 8.73 us -> 7.38 us  [on_device(): msgs[d] = lax.ppermute(sent[g], 'dst', over(blocks, d))]
    ppermute x3, waiting for transfers between devices: 3.25 us -> 2.23 us  [on_device(): held.append(lax.ppermute(atom_in, 'src', over(shards, p)))]
    ppermute x3, waiting for transfers between devices: 2.37 us -> 3.38 us  [on_device(): parts.append(lax.ppermute(sums[p], 'src', over(shards, p)))]
    ppermute x7, starting transfers between devices: 8.58 us -> 9.49 us  [on_device(): msgs[d] = lax.ppermute(sent[g], 'dst', over(blocks, d))]
  transfers between devices with their start and end apart: 13 -> 13, of which waited for: 9 -> 8; matrix products, arithmetic and copies ran while one was open for 3% -> 4% of each run, Pallas kernels for 24% -> 17%
where the time goes in v2:
time: 45.5 us; the launch traced here: 45.4 us
  starting transfers between devices  17.7 us (39%)
  waiting for transfers between devices  13 us (29%)
  Pallas kernels  12.2 us (27%)
  other arithmetic  1.71 us (4%)
  between operations  0.76 us (2%)
    ppermute x7, starting transfers between devices, on_device(): msgs[d] = lax.ppermute(sent[g], 'dst', over(blocks, d))  9.49 us
    pallas_call x4, Pallas kernels, edge_group(): pl.pallas_call(functools.partial(edge_kernel, ds, len(atoms)), out_shape=...  8.55 us
    ppermute x7, waiting for transfers between devices, on_device(): msgs[d] = lax.ppermute(sent[g], 'dst', over(blocks, d))  7.38 us
    ppermute x3, starting transfers between devices, on_device(): held.append(lax.ppermute(atom_in, 'src', over(shards, p)))  4.63 us
    ppermute x3, starting transfers between devices, on_device(): parts.append(lax.ppermute(sums[p], 'src', over(shards, p)))  3.55 us
    ppermute x3, waiting for transfers between devices, on_device(): parts.append(lax.ppermute(sums[p], 'src', over(shards, p)))  3.38 us
    pallas_call x2, Pallas kernels, finish(): pl.pallas_call(functools.partial(finish_kernel, ds, [at for _, at in xs],...  2.84 us
    ppermute x3, waiting for transfers between devices, on_device(): held.append(lax.ppermute(atom_in, 'src', over(shards, p)))  2.23 us
  transfers between devices with their start and end apart: 13, of which 8 were waited for; matrix products, arithmetic and copies ran while one was open for 4% of the time, Pallas kernels for 17%

profile of v2, /device:TPU:0, one launch (start us, length us, event | category | flops | bytes accessed | tf_op | source)
XLA Modules:
  0.0 45.4 jit_solution(15304909588568788990)
XLA Ops:
  0.6 4.0 %collective-permute-start.2 = (bf16[64,256]{1,0:T(8,128)(2,1)}, bf16[64,256]{1,0:T(8,128)(2,1)S(1)}, u32[]{:S(2)}, u32[]{:S(2)}) collective-permute-start(bf16[64,256]{1,0:T(8,128)(2,1)} %atom_in.1), channel_id=1, source_target_pairs={{0,24},{8,16},{16,8},{24,0},{1,25},{9,17},{17,9},{25,1},{2,26},{10... | collective-permute-start | bytes 98312 | tf_op jit(solution)/shard_map/ppermute | solution.py:216
  4.6 0.5 %collective-permute-start.1 = (bf16[64,256]{1,0:T(8,128)(2,1)}, bf16[64,256]{1,0:T(8,128)(2,1)S(1)}, u32[]{:S(2)}, u32[]{:S(2)}) collective-permute-start(bf16[64,256]{1,0:T(8,128)(2,1)} %atom_in.1), channel_id=1, source_target_pairs={{0,16},{8,24},{16,0},{24,8},{1,17},{9,25},{17,1},{25,9},{2,18},{10... | collective-permute-start | bytes 98312 | tf_op jit(solution)/shard_map/ppermute | solution.py:216
  5.1 0.1 collective-permute-start
  5.3 0.0 copy-start.7
  5.3 0.0 copy-start
  5.3 0.0 copy-start.2
  5.3 0.0 copy-start.3
  5.3 0.0 copy-start.5
  5.3 0.0 copy-start.6
  5.3 1.6 %pad_maximum_fusion.refs_8_ = bf16[1792,512]{1,0:T(8,128)(2,1)S(1)} fusion(bf16[512,512]{1,0:T(8,128)(2,1)} %param.19, bf16[1024,512]{1,0:T(8,128)(2,1)} %bitcast.16, bf16[256,512]{1,0:T(8,128)(2,1)} %param.16), kind=kLoop, calls=%fused_computation | loop fusion | flops 5505024 | bytes 3670016 | tf_op jit(solution)/shard_map/concatenate | solution.py:217
  6.9 0.0 copy-done.7
  6.9 0.1 pad_add_fusion.meta
  7.0 0.0 collective-permute-done.2.refs_4_
  7.0 1.7 %collective-permute-done.1.refs_3_ = bf16[64,256]{1,0:T(8,128)(2,1)S(1)} collective-permute-done((bf16[64,256]{1,0:T(8,128)(2,1)}, bf16[64,256]{1,0:T(8,128)(2,1)S(1)}, u32[]{:S(2)}, u32[]{:S(2)}) %collective-permute-start.1) | collective-permute-done | bytes 32800 | tf_op jit(solution)/shard_map/ppermute | solution.py:216
  8.7 0.5 %collective-permute-done.refs_2_ = bf16[64,256]{1,0:T(8,128)(2,1)S(1)} collective-permute-done((bf16[64,256]{1,0:T(8,128)(2,1)}, bf16[64,256]{1,0:T(8,128)(2,1)S(1)}, u32[]{:S(2)}, u32[]{:S(2)}) %collective-permute-start) | collective-permute-done | bytes 32800 | tf_op jit(solution)/shard_map/ppermute | solution.py:216
  9.3 0.0 copy-done
  9.3 0.0 copy-done.2
  9.3 0.0 copy-done.3
  9.3 0.0 copy-done.5
  9.3 0.0 copy-done.6
  9.3 2.1 %edge_group.4 = (f32[256,512]{1,0:T(8,128)S(1)}, bf16[128,512]{1,0:T(8,128)(2,1)S(1)}, bf16[128,512]{1,0:T(8,128)(2,1)S(1)}) custom-call(s32[10]{0:T(128)S(1)} %pad_add_fusion.meta, bf16[1024,512]{1,0:T(8,128)(2,1)S(1)} %copy-done, bf16[64,256]{1,0:T(8,128)(2,1)S(1)} %copy-done.2, bf16[64,256]{1,0:T(8,128)(2,1)S(1)} %collective-permute-done.refs_2_, ...), custom_call_target="tpu_custom_call" | custom-call | flops 536870912 | bytes 1048576 | tf_op jit(solution)/shard_map/edge_group/pallas_call | solution.py:83
  11.4 2.6 %collective-permute-start.8 = (bf16[128,512]{1,0:T(8,128)(2,1)S(1)}, bf16[128,512]{1,0:T(8,128)(2,1)S(1)}, u32[]{:S(2)}, u32[]{:S(2)}) collective-permute-start(bf16[128,512]{1,0:T(8,128)(2,1)S(1)} %get-tuple-element.31), channel_id=1, source_target_pairs={{0,4},{1,5},{2,6},{3,7},{4,0},{5,1},{6,2},{7,3},{8,12},{9,13},{10,... | collective-permute-start | bytes 393224 | tf_op jit(solution)/shard_map/ppermute | solution.py:226
  14.1 0.0 collective-permute-start.9
  14.1 2.1 %edge_group.5 = (f32[256,512]{1,0:T(8,128)S(1)}, bf16[128,512]{1,0:T(8,128)(2,1)S(1)}, bf16[128,512]{1,0:T(8,128)(2,1)S(1)}) custom-call(s32[10]{0:T(128)S(1)} %pad_add_fusion.meta, bf16[1024,512]{1,0:T(8,128)(2,1)S(1)} %copy-done, bf16[64,256]{1,0:T(8,128)(2,1)S(1)} %copy-done.2, bf16[64,256]{1,0:T(8,128)(2,1)S(1)} %collective-permute-done.refs_2_, ...), custom_call_target="tpu_custom_call" | custom-call | flops 536870912 | bytes 1048576 | tf_op jit(solution)/shard_map/edge_group/pallas_call | solution.py:83
  16.2 2.1 %edge_group.6 = (f32[256,512]{1,0:T(8,128)S(1)}, bf16[128,512]{1,0:T(8,128)(2,1)S(1)}, bf16[128,512]{1,0:T(8,128)(2,1)S(1)}) custom-call(s32[10]{0:T(128)S(1)} %pad_add_fusion.meta, bf16[1024,512]{1,0:T(8,128)(2,1)S(1)} %copy-done, bf16[64,256]{1,0:T(8,128)(2,1)S(1)} %copy-done.2, bf16[64,256]{1,0:T(8,128)(2,1)S(1)} %collective-permute-done.refs_2_, ...), custom_call_target="tpu_custom_call" | custom-call | flops 536870912 | bytes 1048576 | tf_op jit(solution)/shard_map/edge_group/pallas_call | solution.py:83
  18.4 0.0 copy-start.1
  18.4 2.1 %edge_group.7 = (f32[256,512]{1,0:T(8,128)S(1)}, bf16[128,512]{1,0:T(8,128)(2,1)S(1)}, bf16[128,512]{1,0:T(8,128)(2,1)S(1)}) custom-call(s32[10]{0:T(128)S(1)} %pad_add_fusion.meta, bf16[1024,512]{1,0:T(8,128)(2,1)S(1)} %copy-done, bf16[64,256]{1,0:T(8,128)(2,1)S(1)} %copy-done.2, bf16[64,256]{1,0:T(8,128)(2,1)S(1)} %collective-permute-done.refs_2_, ...), custom_call_target="tpu_custom_call" | custom-call | flops 536870912 | bytes 1048576 | tf_op jit(solution)/shard_map/edge_group/pallas_call | solution.py:83
  20.5 0.5 %collective-permute-start.7 = (bf16[128,512]{1,0:T(8,128)(2,1)S(1)}, bf16[128,512]{1,0:T(8,128)(2,1)S(1)}, u32[]{:S(2)}, u32[]{:S(2)}) collective-permute-start(bf16[128,512]{1,0:T(8,128)(2,1)S(1)} %get-tuple-element.30), channel_id=1, source_target_pairs={{0,1},{1,0},{2,3},{3,2},{4,5},{5,4},{6,7},{7,6},{8,9},{9,8},{10,11... | collective-permute-start | bytes 393224 | tf_op jit(solution)/shard_map/ppermute | solution.py:226
  21.1 1.6 %collective-permute-start.3 = (bf16[128,512]{1,0:T(8,128)(2,1)S(1)}, bf16[128,512]{1,0:T(8,128)(2,1)S(1)}, u32[]{:S(2)}, u32[]{:S(2)}) collective-permute-start(bf16[128,512]{1,0:T(8,128)(2,1)S(1)} %get-tuple-element.24), channel_id=1, source_target_pairs={{0,2},{1,3},{2,0},{3,1},{4,6},{5,7},{6,4},{7,5},{8,10},{9,11},{10,... | collective-permute-start | bytes 393224 | tf_op jit(solution)/shard_map/ppermute | solution.py:226
  22.6 0.0 collective-permute-start.4
  22.6 0.0 collective-permute-done.8.refs_6_
  22.6 3.7 %collective-permute-start.5 = (bf16[128,512]{1,0:T(8,128)(2,1)S(1)}, bf16[128,512]{1,0:T(8,128)(2,1)S(1)}, u32[]{:S(2)}, u32[]{:S(2)}) collective-permute-start(bf16[128,512]{1,0:T(8,128)(2,1)S(1)} %get-tuple-element.26), channel_id=1, source_target_pairs={{0,6},{1,7},{2,4},{3,5},{4,2},{5,3},{6,0},{7,1},{8,14},{9,15},{10,... | collective-permute-start | bytes 393224 | tf_op jit(solution)/shard_map/ppermute | solution.py:226
  26.3 0.0 collective-permute-done.9.refs_7_
  26.3 1.0 %collective-permute-start.6 = (bf16[128,512]{1,0:T(8,128)(2,1)S(1)}, bf16[128,512]{1,0:T(8,128)(2,1)S(1)}, u32[]{:S(2)}, u32[]{:S(2)}) collective-permute-start(bf16[128,512]{1,0:T(8,128)(2,1)S(1)} %get-tuple-element.27), channel_id=1, source_target_pairs={{0,7},{1,6},{2,5},{3,4},{4,3},{5,2},{6,1},{7,0},{8,15},{9,14},{10,... | collective-permute-start | bytes 393224 | tf_op jit(solution)/shard_map/ppermute | solution.py:226
  27.4 0.0 collective-permute-done.7.refs_5_
  27.4 0.0 copy-done.1
  27.4 1.4 %finish.2 = (bf16[1024,512]{1,0:T(8,128)(2,1)}, f32[256,256]{1,0:T(8,128)S(1)}) custom-call(s32[10]{0:T(128)S(1)} %pad_add_fusion.meta, f32[256,512]{1,0:T(8,128)S(1)} %get-tuple-element.28.refs_0_.refs_1_, f32[256,512]{1,0:T(8,128)S(1)} %get-tuple-element.28.refs_0_.refs_1_, f32[256,512]{1,0:T(8,128)S(1)} %get-tuple-element.21.refs_9_.refs_2_.refs_3_, ...), custom_call_target="tpu_custom_call" | custom-call | flops 268435456 | bytes 2097152 | tf_op jit(solution)/shard_map/finish/pallas_call | solution.py:156
  28.8 0.0 collective-permute-done.3.refs_4_
  28.8 1.0 %collective-permute-done.4.refs_5_ = bf16[128,512]{1,0:T(8,128)(2,1)S(1)} collective-permute-done((bf16[128,512]{1,0:T(8,128)(2,1)S(1)}, bf16[128,512]{1,0:T(8,128)(2,1)S(1)}, u32[]{:S(2)}, u32[]{:S(2)}) %collective-permute-start.4) | collective-permute-done | bytes 131104 | tf_op jit(solution)/shard_map/ppermute | solution.py:226
  29.8 5.4 %collective-permute-done.5.refs_6_ = bf16[128,512]{1,0:T(8,128)(2,1)S(1)} collective-permute-done((bf16[128,512]{1,0:T(8,128)(2,1)S(1)}, bf16[128,512]{1,0:T(8,128)(2,1)S(1)}, u32[]{:S(2)}, u32[]{:S(2)}) %collective-permute-start.5) | collective-permute-done | bytes 131104 | tf_op jit(solution)/shard_map/ppermute | solution.py:226
  35.2 1.0 %collective-permute-done.6.refs_7_ = bf16[128,512]{1,0:T(8,128)(2,1)S(1)} collective-permute-done((bf16[128,512]{1,0:T(8,128)(2,1)S(1)}, bf16[128,512]{1,0:T(8,128)(2,1)S(1)}, u32[]{:S(2)}, u32[]{:S(2)}) %collective-permute-start.6) | collective-permute-done | bytes 131104 | tf_op jit(solution)/shard_map/ppermute | solution.py:226
  36.2 0.0 copy-start.4
  36.2 1.4 %finish.3 = (bf16[1024,512]{1,0:T(8,128)(2,1)}, f32[64,256]{1,0:T(8,128)S(1)}, bf16[64,256]{1,0:T(8,128)(2,1)S(1)}, bf16[64,256]{1,0:T(8,128)(2,1)S(1)}, bf16[64,256]{1,0:T(8,128)(2,1)S(1)}) custom-call(s32[10]{0:T(128)S(1)} %pad_add_fusion.meta, f32[256,512]{1,0:T(8,128)S(1)} %get-tuple-element.22.refs_9_.refs_0_.refs_1_, ...), custom_call_target="tpu_custom_call", output_to_operand_aliasing={{0}: (12, {})} | custom-call | flops 268435456 | bytes 2097152 | tf_op jit(solution)/shard_map/finish/pallas_call | solution.py:156
  37.6 0.6 %collective-permute-start.10 = (bf16[64,256]{1,0:T(8,128)(2,1)S(1)}, bf16[64,256]{1,0:T(8,128)(2,1)S(1)}, u32[]{:S(2)}, u32[]{:S(2)}) collective-permute-start(bf16[64,256]{1,0:T(8,128)(2,1)S(1)} %get-tuple-element.37), channel_id=1, source_target_pairs={{0,8},{8,0},{16,24},{24,16},{1,9},{9,1},{17,25},{25,17},{2,10},{10... | collective-permute-start | bytes 98312 | tf_op jit(solution)/shard_map/ppermute | solution.py:241
  38.2 1.5 %collective-permute-start.11 = (bf16[64,256]{1,0:T(8,128)(2,1)S(1)}, bf16[64,256]{1,0:T(8,128)(2,1)S(1)}, u32[]{:S(2)}, u32[]{:S(2)}) collective-permute-start(bf16[64,256]{1,0:T(8,128)(2,1)S(1)} %get-tuple-element.38), channel_id=1, source_target_pairs={{0,16},{8,24},{16,0},{24,8},{1,17},{9,25},{17,1},{25,9},{2,18},{10... | collective-permute-start | bytes 98312 | tf_op jit(solution)/shard_map/ppermute | solution.py:241
  39.7 1.4 %collective-permute-start.12 = (bf16[64,256]{1,0:T(8,128)(2,1)S(1)}, bf16[64,256]{1,0:T(8,128)(2,1)S(1)}, u32[]{:S(2)}, u32[]{:S(2)}) collective-permute-start(bf16[64,256]{1,0:T(8,128)(2,1)S(1)} %get-tuple-element.39), channel_id=1, source_target_pairs={{0,24},{8,16},{16,8},{24,0},{1,25},{9,17},{17,9},{25,1},{2,26},{10... | collective-permute-start | bytes 98312 | tf_op jit(solution)/shard_map/ppermute | solution.py:241
  41.2 0.5 %collective-permute-done.10.refs_1_ = bf16[64,256]{1,0:T(8,128)(2,1)S(1)} collective-permute-done((bf16[64,256]{1,0:T(8,128)(2,1)S(1)}, bf16[64,256]{1,0:T(8,128)(2,1)S(1)}, u32[]{:S(2)}, u32[]{:S(2)}) %collective-permute-start.10) | collective-permute-done | bytes 32800 | tf_op jit(solution)/shard_map/ppermute | solution.py:241
  41.7 0.4 collective-permute-done.11.refs_2_
  42.1 2.4 %collective-permute-done.12.refs_3_ = bf16[64,256]{1,0:T(8,128)(2,1)S(1)} collective-permute-done((bf16[64,256]{1,0:T(8,128)(2,1)S(1)}, bf16[64,256]{1,0:T(8,128)(2,1)S(1)}, u32[]{:S(2)}, u32[]{:S(2)}) %collective-permute-start.12) | collective-permute-done | bytes 32800 | tf_op jit(solution)/shard_map/ppermute | solution.py:241
  44.6 0.0 copy-done.4
  44.6 0.8 %atom_update.1 = bf16[64,256]{1,0:T(8,128)(2,1)} custom-call(bf16[64,256]{1,0:T(8,128)(2,1)S(1)} %copy-done.2, bf16[256,256]{1,0:T(8,128)(2,1)S(1)} %copy-done.4, f32[64,256]{1,0:T(8,128)S(1)} %get-tuple-element.36.refs_0_, bf16[64,256]{1,0:T(8,128)(2,1)S(1)} %collective-permute-done.10.refs_1_, bf16[64,256]{1,0:T(8,128)(2,1)S(1)} %collective-permute-done.11.refs_2_, ...), custom_call_target="tpu_custom_call" | custom-call | tf_op jit(solution)/shard_map/atom_update/pallas_call | solution.py:242
Async XLA Ops:
  0.6 6.4 %collective-permute-start.2 = (bf16[64,256]{1,0:T(8,128)(2,1)}, bf16[64,256]{1,0:T(8,128)(2,1)S(1)}, u32[]{:S(2)}, u32[]{:S(2)}) collective-permute-start(bf16[64,256]{1,0:T(8,128)(2,1)} %atom_in.1), channel_id=1, source_target_pairs={{0,24},{8,16},{16,8},{24,0},{1,25},{9,17},{17,9},{25,1},{2,26},{10... | collective-permute-start | bytes 98312 | tf_op jit(solution)/shard_map/ppermute | solution.py:216
  4.6 4.1 %collective-permute-start.1 = (bf16[64,256]{1,0:T(8,128)(2,1)}, bf16[64,256]{1,0:T(8,128)(2,1)S(1)}, u32[]{:S(2)}, u32[]{:S(2)}) collective-permute-start(bf16[64,256]{1,0:T(8,128)(2,1)} %atom_in.1), channel_id=1, source_target_pairs={{0,16},{8,24},{16,0},{24,8},{1,17},{9,25},{17,1},{25,9},{2,18},{10... | collective-permute-start | bytes 98312 | tf_op jit(solution)/shard_map/ppermute | solution.py:216
  5.1 4.1 %collective-permute-start = (bf16[64,256]{1,0:T(8,128)(2,1)}, bf16[64,256]{1,0:T(8,128)(2,1)S(1)}, u32[]{:S(2)}, u32[]{:S(2)}) collective-permute-start(bf16[64,256]{1,0:T(8,128)(2,1)} %atom_in.1), channel_id=1, source_target_pairs={{0,8},{8,0},{16,24},{24,16},{1,9},{9,1},{17,25},{25,17},{2,10},{10... | collective-permute-start | bytes 98312 | tf_op jit(solution)/shard_map/ppermute | solution.py:216
  5.3 1.7 %copy-start.7 = (s32[1,1,8]{2,1,0:T(1,128)S(1)}, s32[1,1,8]{2,1,0:T(1,128)}, u32[]{:S(2)}) copy-start(s32[1,1,8]{2,1,0:T(1,128)} %param.15) | copy-start | bytes 100
  5.3 4.0 %copy-start = (bf16[1024,512]{1,0:T(8,128)(2,1)S(1)}, bf16[1024,512]{1,0:T(8,128)(2,1)}, u32[]{:S(2)}) copy-start(bf16[1024,512]{1,0:T(8,128)(2,1)} %refs_0_.7) | copy-start | bytes 3145732
  5.3 4.0 %copy-start.2 = (bf16[64,256]{1,0:T(8,128)(2,1)S(1)}, bf16[64,256]{1,0:T(8,128)(2,1)}, u32[]{:S(2)}) copy-start(bf16[64,256]{1,0:T(8,128)(2,1)} %atom_in.1) | copy-start | bytes 98308
  5.3 4.0 %copy-start.3 = (s32[1024]{0:T(1024)S(1)}, s32[1024]{0:T(1024)}, u32[]{:S(2)}) copy-start(s32[1024]{0:T(1024)} %param.13) | copy-start | bytes 12292
  5.3 4.0 %copy-start.5 = (s32[1024]{0:T(1024)S(1)}, s32[1024]{0:T(1024)}, u32[]{:S(2)}) copy-start(s32[1024]{0:T(1024)} %param.14) | copy-start | bytes 12292
  5.3 4.0 %copy-start.6 = (f32[2,512]{1,0:T(2,128)S(1)}, f32[2,512]{1,0:T(2,128)}, u32[]{:S(2)}) copy-start(f32[2,512]{1,0:T(2,128)} %refs_7_.7) | copy-start | bytes 12292
  11.4 11.2 %collective-permute-start.8 = (bf16[128,512]{1,0:T(8,128)(2,1)S(1)}, bf16[128,512]{1,0:T(8,128)(2,1)S(1)}, u32[]{:S(2)}, u32[]{:S(2)}) collective-permute-start(bf16[128,512]{1,0:T(8,128)(2,1)S(1)} %get-tuple-element.31), channel_id=1, source_target_pairs={{0,4},{1,5},{2,6},{3,7},{4,0},{5,1},{6,2},{7,3},{8,12},{9,13},{10,... | collective-permute-start | bytes 393224 | tf_op jit(solution)/shard_map/ppermute | solution.py:226
  14.1 12.2 %collective-permute-start.9 = (bf16[128,512]{1,0:T(8,128)(2,1)S(1)}, bf16[128,512]{1,0:T(8,128)(2,1)S(1)}, u32[]{:S(2)}, u32[]{:S(2)}) collective-permute-start(bf16[128,512]{1,0:T(8,128)(2,1)S(1)} %get-tuple-element.32), channel_id=1, source_target_pairs={{0,5},{1,4},{2,7},{3,6},{4,1},{5,0},{6,3},{7,2},{8,13},{9,12},{10,... | collective-permute-start | bytes 393224 | tf_op jit(solution)/shard_map/ppermute | solution.py:226
  18.4 9.0 %copy-start.1 = (bf16[512,256]{1,0:T(8,128)(2,1)S(1)}, bf16[512,256]{1,0:T(8,128)(2,1)}, u32[]{:S(2)}) copy-start(bf16[512,256]{1,0:T(8,128)(2,1)} %refs_9_.3) | copy-start | bytes 786436
  20.5 6.8 %collective-permute-start.7 = (bf16[128,512]{1,0:T(8,128)(2,1)S(1)}, bf16[128,512]{1,0:T(8,128)(2,1)S(1)}, u32[]{:S(2)}, u32[]{:S(2)}) collective-permute-start(bf16[128,512]{1,0:T(8,128)(2,1)S(1)} %get-tuple-element.30), channel_id=1, source_target_pairs={{0,1},{1,0},{2,3},{3,2},{4,5},{5,4},{6,7},{7,6},{8,9},{9,8},{10,11... | collective-permute-start | bytes 393224 | tf_op jit(solution)/shard_map/ppermute | solution.py:226
  21.1 7.8 %collective-permute-start.3 = (bf16[128,512]{1,0:T(8,128)(2,1)S(1)}, bf16[128,512]{1,0:T(8,128)(2,1)S(1)}, u32[]{:S(2)}, u32[]{:S(2)}) collective-permute-start(bf16[128,512]{1,0:T(8,128)(2,1)S(1)} %get-tuple-element.24), channel_id=1, source_target_pairs={{0,2},{1,3},{2,0},{3,1},{4,6},{5,7},{6,4},{7,5},{8,10},{9,11},{10,... | collective-permute-start | bytes 393224 | tf_op jit(solution)/shard_map/ppermute | solution.py:226
  22.6 7.2 %collective-permute-start.4 = (bf16[128,512]{1,0:T(8,128)(2,1)S(1)}, bf16[128,512]{1,0:T(8,128)(2,1)S(1)}, u32[]{:S(2)}, u32[]{:S(2)}) collective-permute-start(bf16[128,512]{1,0:T(8,128)(2,1)S(1)} %get-tuple-element.25), channel_id=1, source_target_pairs={{0,3},{1,2},{2,1},{3,0},{4,7},{5,6},{6,5},{7,4},{8,11},{9,10},{10,... | collective-permute-start | bytes 393224 | tf_op jit(solution)/shard_map/ppermute | solution.py:226
  22.6 12.5 %collective-permute-start.5 = (bf16[128,512]{1,0:T(8,128)(2,1)S(1)}, bf16[128,512]{1,0:T(8,128)(2,1)S(1)}, u32[]{:S(2)}, u32[]{:S(2)}) collective-permute-start(bf16[128,512]{1,0:T(8,128)(2,1)S(1)} %get-tuple-element.26), channel_id=1, source_target_pairs={{0,6},{1,7},{2,4},{3,5},{4,2},{5,3},{6,0},{7,1},{8,14},{9,15},{10,... | collective-permute-start | bytes 393224 | tf_op jit(solution)/shard_map/ppermute | solution.py:226
  26.3 9.9 %collective-permute-start.6 = (bf16[128,512]{1,0:T(8,128)(2,1)S(1)}, bf16[128,512]{1,0:T(8,128)(2,1)S(1)}, u32[]{:S(2)}, u32[]{:S(2)}) collective-permute-start(bf16[128,512]{1,0:T(8,128)(2,1)S(1)} %get-tuple-element.27), channel_id=1, source_target_pairs={{0,7},{1,6},{2,5},{3,4},{4,3},{5,2},{6,1},{7,0},{8,15},{9,14},{10,... | collective-permute-start | bytes 393224 | tf_op jit(solution)/shard_map/ppermute | solution.py:226
  36.2 8.4 %copy-start.4 = (bf16[256,256]{1,0:T(8,128)(2,1)S(1)}, bf16[256,256]{1,0:T(8,128)(2,1)}, u32[]{:S(2)}) copy-start(bf16[256,256]{1,0:T(8,128)(2,1)} %w_atom.1) | copy-start | bytes 393220
  37.6 4.1 %collective-permute-start.10 = (bf16[64,256]{1,0:T(8,128)(2,1)S(1)}, bf16[64,256]{1,0:T(8,128)(2,1)S(1)}, u32[]{:S(2)}, u32[]{:S(2)}) collective-permute-start(bf16[64,256]{1,0:T(8,128)(2,1)S(1)} %get-tuple-element.37), channel_id=1, source_target_pairs={{0,8},{8,0},{16,24},{24,16},{1,9},{9,1},{17,25},{25,17},{2,10},{10... | collective-permute-start | bytes 98312 | tf_op jit(solution)/shard_map/ppermute | solution.py:241
  38.2 3.9 %collective-permute-start.11 = (bf16[64,256]{1,0:T(8,128)(2,1)S(1)}, bf16[64,256]{1,0:T(8,128)(2,1)S(1)}, u32[]{:S(2)}, u32[]{:S(2)}) collective-permute-start(bf16[64,256]{1,0:T(8,128)(2,1)S(1)} %get-tuple-element.38), channel_id=1, source_target_pairs={{0,16},{8,24},{16,0},{24,8},{1,17},{9,25},{17,1},{25,9},{2,18},{10... | collective-permute-start | bytes 98312 | tf_op jit(solution)/shard_map/ppermute | solution.py:241
  39.7 4.8 %collective-permute-start.12 = (bf16[64,256]{1,0:T(8,128)(2,1)S(1)}, bf16[64,256]{1,0:T(8,128)(2,1)S(1)}, u32[]{:S(2)}, u32[]{:S(2)}) collective-permute-start(bf16[64,256]{1,0:T(8,128)(2,1)S(1)} %get-tuple-element.39), channel_id=1, source_target_pairs={{0,24},{8,16},{16,8},{24,0},{1,25},{9,17},{17,9},{25,1},{2,26},{10... | collective-permute-start | bytes 98312 | tf_op jit(solution)/shard_map/ppermute | solution.py:241

commit v3 on v2

v3 whole, which is shorter than its diff:
```python
import functools

import jax
import jax.numpy as jnp
from jax import lax
from jax.experimental import pallas as pl
from jax.experimental.pallas import tpu as pltpu
from jax.sharding import PartitionSpec as P

F32 = jnp.float32
BF16 = jnp.bfloat16
LIMIT = 16 * 2**20


def dot(a, b):
    return jnp.dot(a, b, preferred_element_type=F32)


def column(row, width):
    n = row.shape[1]
    spread = jnp.transpose(jnp.broadcast_to(row, (n, n)))
    return jnp.concatenate([spread] * (width // n), axis=1)


def relabel(row, me, share):
    return (lax.div(row, share) ^ me) * share + lax.rem(row, share)


def silu(v):
    half = 0.5 * v
    return half + half * jnp.tanh(half)


def layers(x, gains_ref, weights, first):
    feat = x.shape[1]
    for layer in range(gains_ref.shape[0]):
        scale = lax.rsqrt(jnp.mean(x * x, axis=-1, keepdims=True) + 1e-06)
        normed = (x * scale * gains_ref[layer : layer + 1, :]).astype(BF16)
        y = dot(normed, weights[first + layer * feat : first + (layer + 1) * feat])
        x = x + silu(y)
    return x


def edge_kernel(ds, shards, *refs):
    group = len(ds)
    me, part = lax.axis_index("src"), lax.axis_index("dst")
    edge_in, *atoms = refs[: 1 + shards]
    targets, reverse, counts, gains, weights = refs[1 + shards : 6 + shards]
    x_ref, *msgs = refs[-1 - group :]
    width = targets.shape[1]
    share = atoms[0].shape[0]
    hidden, feat = atoms[0].shape[1], edge_in.shape[1]
    w_rev = hidden + gains.shape[0] * feat
    table = jnp.concatenate([a[...] for a in atoms], axis=0)
    lanes = lax.broadcasted_iota(jnp.int32, (width, table.shape[0]), 1)
    picks = []
    for g in range(group):
        row = relabel(targets[pl.ds(part ^ ds[g], 1), :], me, share)
        picks.append((column(row, table.shape[0]) == lanes).astype(BF16))
    picked = dot(jnp.concatenate(picks, axis=0), table).astype(BF16)
    proj = dot(picked, weights[:hidden]).astype(BF16).astype(F32)
    starts = [pl.multiple_of((part ^ d) * width, width) for d in ds]
    x = jnp.concatenate([edge_in[pl.ds(start, width), :] for start in starts], axis=0)
    x = x.astype(F32) + proj
    x = layers(x, gains, weights, hidden)
    sent = x.astype(BF16)
    rows = lax.broadcasted_iota(jnp.int32, (width, width), 0)
    slots = lax.broadcasted_iota(jnp.int32, (width, x.shape[1]), 0)
    turned = []
    for g in range(group):
        k = part ^ ds[g]
        lanes = lax.broadcasted_iota(jnp.int32, counts.shape, 1)
        used = jnp.sum(jnp.where(lanes == k, counts[...], 0), axis=1, keepdims=True)
        mine = slice(g * width, (g + 1) * width)
        x_ref[mine, :] = jnp.where(slots < used, x[mine], 0.0)
        swap = (rows == reverse[pl.ds(k, 1), :]) & (rows < used)
        turned.append(dot(swap.astype(BF16), sent[mine]).astype(BF16))
    msg = dot(jnp.concatenate(turned, axis=0), weights[w_rev:]).astype(BF16)
    for g in range(group):
        msgs[g][...] = msg[g * width : (g + 1) * width]


def edge_group(ds, edge_in, atoms, targets, reverse, counts, gains, weights, after):
    _, width = targets.shape
    group = len(ds)
    feat = edge_in.shape[1]
    whole = pl.BlockSpec(memory_space=pltpu.VMEM)
    rows = group * width
    return pl.pallas_call(
        functools.partial(edge_kernel, ds, len(atoms)),
        out_shape=[jax.ShapeDtypeStruct((rows, feat), F32)]
        + [jax.ShapeDtypeStruct((width, feat), BF16)] * group,
        in_specs=[whole] * (len(atoms) + 6) + [pl.BlockSpec(memory_space=pl.ANY)] * len(after),
        out_specs=[whole] * (1 + group),
        cost_estimate=pl.CostEstimate(
            flops=2 * rows * feat * feat * 4, bytes_accessed=rows * feat * 8, transcendentals=rows * feat * 4
        ),
        compiler_params=pltpu.CompilerParams(vmem_limit_bytes=LIMIT),
        name="edge_group",
    )(edge_in, *atoms, targets, reverse, counts, gains, weights, *after)


def block_copy(stage, g, out, k, width, sems):
    return pltpu.make_async_copy(
        stage.at[pl.ds(g * width, width), :],
        out.at[pl.ds(pl.multiple_of(k * width, width), width), :],
        sems.at[g],
    )


def store_kernel(ds, width, stage, old, out, sems):
    part = lax.axis_index("dst")
    copies = [block_copy(stage, g, out, part ^ d, width, sems) for g, d in enumerate(ds)]
    for copy in copies:
        copy.start()
    for copy in copies:
        copy.wait()


def store(ds, width, stage, out):
    far = pl.BlockSpec(memory_space=pl.ANY)
    return pl.pallas_call(
        functools.partial(store_kernel, ds, width),
        out_shape=jax.ShapeDtypeStruct(out.shape, out.dtype),
        in_specs=[pl.BlockSpec(memory_space=pltpu.VMEM), far],
        out_specs=far,
        scratch_shapes=[pltpu.SemaphoreType.DMA((len(ds),))],
        input_output_aliases={1: 0},
        cost_estimate=pl.CostEstimate(flops=10**8, bytes_accessed=stage.size * 4, transcendentals=0),
        compiler_params=pltpu.CompilerParams(vmem_limit_bytes=LIMIT),
        name="store",
    )(stage, out)


def finish_kernel(ds, ats, first, last, shards, *refs):
    group = len(ds)
    me, part = lax.axis_index("src"), lax.axis_index("dst")
    xs, msgs = refs[:group], refs[group : 2 * group]
    targets, w_down = refs[2 * group : 2 * group + 2]
    rest = list(refs[2 * group + 2 :])
    acc = None if first else rest[0]
    if last:
        stage, *sums = rest[1:]
    else:
        out, *sums = rest[0 if first else 2 : -2]
        stage, sems = rest[-2:]
    width = msgs[0].shape[0]
    copies = []
    for g, d in enumerate(ds):
        x = xs[g][pl.ds(ats[g] * width, width), :] + msgs[g][...].astype(F32)
        stage[pl.ds(g * width, width), :] = x.astype(BF16)
        if not last:
            copies.append(block_copy(stage, g, out, part ^ d, width, sems))
            copies[g].start()
    contrib = dot(stage[...], w_down[...]).astype(BF16)
    atoms = sums[0].shape[0] * (shards if last else 1)
    place = lax.broadcasted_iota(jnp.int32, (atoms, width), 0)
    spread = [
        (place == relabel(targets[pl.ds(part ^ d, 1), :], me, atoms // shards)).astype(BF16)
        for d in ds
    ]
    total = dot(jnp.concatenate(spread, axis=1), contrib)
    if not first:
        total = total + acc[...]
    if last:
        share = atoms // shards
        for p in range(shards):
            sums[p][...] = total[p * share : (p + 1) * share].astype(sums[p].dtype)
    else:
        sums[0][...] = total
    for copy in copies:
        copy.wait()


def finish(ds, xs, msgs, targets, w_down, acc, out, total_rows, atoms, shards, last):
    _, width = targets.shape
    feat, hidden = w_down.shape
    first = acc is None
    assert not (first and last)
    group = len(ds)
    whole = pl.BlockSpec(memory_space=pltpu.VMEM)
    far = pl.BlockSpec(memory_space=pl.ANY)
    share = atoms // shards
    if last:
        tail = [jax.ShapeDtypeStruct((share, hidden), F32)]
        tail += [jax.ShapeDtypeStruct((share, hidden), BF16)] * (shards - 1)
    else:
        tail = [jax.ShapeDtypeStruct((atoms, hidden), F32)]
    return pl.pallas_call(
        functools.partial(finish_kernel, ds, [at for _, at in xs], first, last, shards),
        out_shape=[jax.ShapeDtypeStruct((group * width if last else total_rows, feat), BF16)] + tail,
        in_specs=[whole] * (2 * group + 2) + ([] if first else [whole] if last else [whole, far]),
        out_specs=[whole if last else far] + [whole] * len(tail),
        scratch_shapes=[]
        if last
        else [
            pltpu.VMEM((group * width, feat), BF16),
            pltpu.SemaphoreType.DMA((group,)),
        ],
        input_output_aliases={} if first or last else {2 * group + 3: 0},
        cost_estimate=pl.CostEstimate(
            flops=4 * group * width * feat * hidden,
            bytes_accessed=group * width * feat * 8,
            transcendentals=0,
        ),
        compiler_params=pltpu.CompilerParams(vmem_limit_bytes=LIMIT),
        name="finish",
    )(*[x for x, _ in xs], *msgs, targets, w_down, *([] if first else [acc] if last else [acc, out]))


def atom_kernel(atom_in, w_atom, *refs):
    *parts, out = refs
    agg = parts[0][...]
    for part in parts[1:]:
        agg = agg + part[...].astype(F32)
    v = 0.3 * agg
    act = silu(v).astype(BF16)
    out[...] = (atom_in[...].astype(F32) + dot(act, w_atom[...])).astype(BF16)


def edge_order(blocks):
    half = blocks // 2
    near = [[d, d + 1] for d in range(2, half, 2)]
    far = [[d, d + 1] for d in range(half + 2, blocks, 2)]
    return [[half, half + 1]] + near + far + [[1, 0]]


def on_device(
    edge_in, atom_in, targets, reverse, counts, w_in, gains, w_layers, w_rev, w_down, w_atom
):
    slots, feat = edge_in.shape
    blocks = counts.shape[2]
    width = slots // blocks
    shards = lax.axis_size("src")
    atoms = atom_in.shape[0] * shards
    counts = counts.reshape(1, blocks)
    targets = targets.reshape(blocks, width)
    reverse = reverse.reshape(blocks, width)

    def over(size, d):
        return [(s, s ^ d) for s in range(size)]

    held = [atom_in]
    for p in range(1, shards):
        held.append(lax.ppermute(atom_in, "src", over(shards, p)))
    weights = jnp.concatenate([w_in, w_layers.reshape(-1, feat), w_rev], axis=0)
    xs, msgs, after = {}, {}, []
    for ds in edge_order(blocks):
        x, *sent = edge_group(ds, edge_in, held, targets, reverse, counts, gains, weights, after)
        after = [x]
        for g, d in enumerate(ds):
            xs[d] = (x, g)
            msgs[d] = sent[g]
            if d:
                msgs[d] = lax.ppermute(sent[g], "dst", over(blocks, d))
    acc = out = None
    half = blocks // 2
    groups = [[0, 1, half, half + 1]]
    rest = list(range(2, half)) + list(range(half + 2, blocks))
    groups += [rest[n : n + 4] for n in range(0, len(rest), 4)]
    for ds in groups:
        last = ds is groups[-1]
        rows, *sums = finish(
            ds, [xs[d] for d in ds], [msgs[d] for d in ds], targets,
            w_down, acc, out, slots, atoms, shards, last,
        )
        acc = sums[0]
        if not last:
            out = rows
    parts = [sums[0]]
    for p in range(1, shards):
        parts.append(lax.ppermute(sums[p], "src", over(shards, p)))
    out = store(groups[-1], width, rows, out)
    atom_out = pl.pallas_call(
        atom_kernel,
        out_shape=jax.ShapeDtypeStruct(atom_in.shape, BF16),
        compiler_params=pltpu.CompilerParams(vmem_limit_bytes=LIMIT),
        name="atom_update",
    )(atom_in, w_atom, *parts)
    return (out, atom_out)


def solution(mesh):
    placed = (
        P(("src", "dst"), None),
        P(("dst", "src"), None),
        P(("src", "dst")),
        P(("src", "dst")),
        P("src", "dst", None),
        P(),
        P(),
        P(),
        P(),
        P(),
        P(),
    )
    return jax.shard_map(
        on_device,
        mesh=mesh,
        in_specs=placed,
        out_specs=(P(("src", "dst"), None), P(("dst", "src"), None)),
        check_vma=False,
    )
```

time: 45.5 us -> 43.6 us (0.958)
  Pallas kernels: 12.2 us -> 9.37 us
  starting transfers between devices: 17.7 us -> 18.7 us
    pallas_call x4, Pallas kernels: 8.55 us -> 6.33 us  [edge_group(): pl.pallas_call(functools.partial(edge_kernel, ds, len(atoms)), out_shape=...]
    pallas_call x2, Pallas kernels: 2.84 us -> 1.44 us  [finish(): pl.pallas_call(functools.partial(finish_kernel, ds, [at for _, at in xs],...]
    ppermute x7, starting transfers between devices: 9.49 us -> 10.5 us  [on_device(): msgs[d] = lax.ppermute(sent[g], 'dst', over(blocks, d))]
    pallas_call x0 -> x1, Pallas kernels: none -> 0.82 us  [store(): pl.pallas_call(functools.partial(store_kernel, ds, width), out_shape=jax....]
    ppermute x3, waiting for transfers between devices: 3.38 us -> 2.74 us  [on_device(): parts.append(lax.ppermute(sums[p], 'src', over(shards, p)))]
    ppermute x7, waiting for transfers between devices: 7.38 us -> 7.91 us  [on_device(): msgs[d] = lax.ppermute(sent[g], 'dst', over(blocks, d))]
  transfers between devices with their start and end apart: 13 -> 13, of which waited for: 8 -> 6; matrix products, arithmetic and copies ran while one was open for 4% -> 4% of each run, Pallas kernels for 17% -> 15%
where the time goes in v3:
time: 43.6 us; the launch traced here: 43.5 us
  starting transfers between devices  18.7 us (43%)
  waiting for transfers between devices  13 us (30%)
  Pallas kernels  9.37 us (21%)
  other arithmetic  1.63 us (4%)
  between operations  0.79 us (2%)
    ppermute x7, starting transfers between devices, on_device(): msgs[d] = lax.ppermute(sent[g], 'dst', over(blocks, d))  10.5 us
    ppermute x7, waiting for transfers between devices, on_device(): msgs[d] = lax.ppermute(sent[g], 'dst', over(blocks, d))  7.91 us
    pallas_call x4, Pallas kernels, edge_group(): pl.pallas_call(functools.partial(edge_kernel, ds, len(atoms)), out_shape=...  6.33 us
    ppermute x3, starting transfers between devices, on_device(): held.append(lax.ppermute(atom_in, 'src', over(shards, p)))  4.63 us
    ppermute x3, starting transfers between devices, on_device(): parts.append(lax.ppermute(sums[p], 'src', over(shards, p)))  3.55 us
    ppermute x3, waiting for transfers between devices, on_device(): parts.append(lax.ppermute(sums[p], 'src', over(shards, p)))  2.74 us
    ppermute x3, waiting for transfers between devices, on_device(): held.append(lax.ppermute(atom_in, 'src', over(shards, p)))  2.32 us
    concatenate x1, other arithmetic, on_device(): weights = jnp.concatenate([w_in, w_layers.reshape(-1, feat), w_rev], axis=0)  1.63 us
  transfers between devices with their start and end apart: 13, of which 6 were waited for; matrix products, arithmetic and copies ran while one was open for 4% of the time, Pallas kernels for 15%

profile of v3, /device:TPU:0, one launch (start us, length us, event | category | flops | bytes accessed | tf_op | source)
XLA Modules:
  0.0 43.5 jit_solution(10868779609808665767)
XLA Ops:
  0.6 4.0 %collective-permute-start.2 = (bf16[64,256]{1,0:T(8,128)(2,1)}, bf16[64,256]{1,0:T(8,128)(2,1)S(1)}, u32[]{:S(2)}, u32[]{:S(2)}) collective-permute-start(bf16[64,256]{1,0:T(8,128)(2,1)} %atom_in.1), channel_id=1, source_target_pairs={{0,24},{8,16},{16,8},{24,0},{1,25},{9,17},{17,9},{25,1},{2,26},{10... | collective-permute-start | bytes 98312 | tf_op jit(solution)/shard_map/ppermute | solution.py:245
  4.6 0.5 %collective-permute-start.1 = (bf16[64,256]{1,0:T(8,128)(2,1)}, bf16[64,256]{1,0:T(8,128)(2,1)S(1)}, u32[]{:S(2)}, u32[]{:S(2)}) collective-permute-start(bf16[64,256]{1,0:T(8,128)(2,1)} %atom_in.1), channel_id=1, source_target_pairs={{0,16},{8,24},{16,0},{24,8},{1,17},{9,25},{17,1},{25,9},{2,18},{10... | collective-permute-start | bytes 98312 | tf_op jit(solution)/shard_map/ppermute | solution.py:245
  5.1 0.1 collective-permute-start
  5.3 0.0 copy-start
  5.3 0.0 copy-start.2
  5.3 0.0 copy-start.3
  5.3 0.0 copy-start.5
  5.3 0.0 copy-start.6
  5.3 0.0 copy-start.7
  5.3 1.6 %pad_maximum_fusion.refs_9_ = bf16[1792,512]{1,0:T(8,128)(2,1)S(1)} fusion(bf16[512,512]{1,0:T(8,128)(2,1)} %param.19, bf16[1024,512]{1,0:T(8,128)(2,1)} %bitcast.18, bf16[256,512]{1,0:T(8,128)(2,1)} %param.16), kind=kLoop, calls=%fused_computation | loop fusion | flops 5505024 | bytes 3670016 | tf_op jit(solution)/shard_map/concatenate | solution.py:246
  6.9 0.0 collective-permute-done.2.refs_4_
  6.9 1.8 %collective-permute-done.1.refs_3_ = bf16[64,256]{1,0:T(8,128)(2,1)S(1)} collective-permute-done((bf16[64,256]{1,0:T(8,128)(2,1)}, bf16[64,256]{1,0:T(8,128)(2,1)S(1)}, u32[]{:S(2)}, u32[]{:S(2)}) %collective-permute-start.1) | collective-permute-done | bytes 32800 | tf_op jit(solution)/shard_map/ppermute | solution.py:245
  8.7 0.5 %collective-permute-done.refs_2_ = bf16[64,256]{1,0:T(8,128)(2,1)S(1)} collective-permute-done((bf16[64,256]{1,0:T(8,128)(2,1)}, bf16[64,256]{1,0:T(8,128)(2,1)S(1)}, u32[]{:S(2)}, u32[]{:S(2)}) %collective-permute-start) | collective-permute-done | bytes 32800 | tf_op jit(solution)/shard_map/ppermute | solution.py:245
  9.3 0.0 copy-done
  9.3 0.0 copy-done.2
  9.3 0.0 copy-done.3
  9.3 0.0 copy-done.5
  9.3 0.0 copy-done.6
  9.3 0.0 copy-done.7
  9.3 1.6 %edge_group.4 = (f32[256,512]{1,0:T(8,128)S(1)}, bf16[128,512]{1,0:T(8,128)(2,1)S(1)}, bf16[128,512]{1,0:T(8,128)(2,1)S(1)}) custom-call(bf16[1024,512]{1,0:T(8,128)(2,1)S(1)} %copy-done, bf16[64,256]{1,0:T(8,128)(2,1)S(1)} %copy-done.2, bf16[64,256]{1,0:T(8,128)(2,1)S(1)} %collective-permute-done.refs_2_, ...), custom_call_target="tpu_custom_call" | custom-call | flops 536870912 | bytes 1048576 | tf_op jit(solution)/shard_map/edge_group/pallas_call | solution.py:89
  10.9 2.7 %collective-permute-start.8 = (bf16[128,512]{1,0:T(8,128)(2,1)S(1)}, bf16[128,512]{1,0:T(8,128)(2,1)S(1)}, u32[]{:S(2)}, u32[]{:S(2)}) collective-permute-start(bf16[128,512]{1,0:T(8,128)(2,1)S(1)} %get-tuple-element.31), channel_id=1, source_target_pairs={{0,4},{1,5},{2,6},{3,7},{4,0},{5,1},{6,2},{7,3},{8,12},{9,13},{10,... | collective-permute-start | bytes 393224 | tf_op jit(solution)/shard_map/ppermute | solution.py:255
  13.5 0.0 collective-permute-start.9
  13.5 1.6 %edge_group.5 = (f32[256,512]{1,0:T(8,128)S(1)}, bf16[128,512]{1,0:T(8,128)(2,1)S(1)}, bf16[128,512]{1,0:T(8,128)(2,1)S(1)}) custom-call(bf16[1024,512]{1,0:T(8,128)(2,1)S(1)} %copy-done, bf16[64,256]{1,0:T(8,128)(2,1)S(1)} %copy-done.2, bf16[64,256]{1,0:T(8,128)(2,1)S(1)} %collective-permute-done.refs_2_, ...), custom_call_target="tpu_custom_call" | custom-call | flops 536870912 | bytes 1048576 | tf_op jit(solution)/shard_map/edge_group/pallas_call | solution.py:89
  15.1 1.6 %edge_group.6 = (f32[256,512]{1,0:T(8,128)S(1)}, bf16[128,512]{1,0:T(8,128)(2,1)S(1)}, bf16[128,512]{1,0:T(8,128)(2,1)S(1)}) custom-call(bf16[1024,512]{1,0:T(8,128)(2,1)S(1)} %copy-done, bf16[64,256]{1,0:T(8,128)(2,1)S(1)} %copy-done.2, bf16[64,256]{1,0:T(8,128)(2,1)S(1)} %collective-permute-done.refs_2_, ...), custom_call_target="tpu_custom_call" | custom-call | flops 536870912 | bytes 1048576 | tf_op jit(solution)/shard_map/edge_group/pallas_call | solution.py:89
  16.7 0.0 copy-start.1
  16.7 1.6 %edge_group.7 = (f32[256,512]{1,0:T(8,128)S(1)}, bf16[128,512]{1,0:T(8,128)(2,1)S(1)}, bf16[128,512]{1,0:T(8,128)(2,1)S(1)}) custom-call(bf16[1024,512]{1,0:T(8,128)(2,1)S(1)} %copy-done, bf16[64,256]{1,0:T(8,128)(2,1)S(1)} %copy-done.2, bf16[64,256]{1,0:T(8,128)(2,1)S(1)} %collective-permute-done.refs_2_, ...), custom_call_target="tpu_custom_call" | custom-call | flops 536870912 | bytes 1048576 | tf_op jit(solution)/shard_map/edge_group/pallas_call | solution.py:89
  18.3 0.5 %collective-permute-start.7 = (bf16[128,512]{1,0:T(8,128)(2,1)S(1)}, bf16[128,512]{1,0:T(8,128)(2,1)S(1)}, u32[]{:S(2)}, u32[]{:S(2)}) collective-permute-start(bf16[128,512]{1,0:T(8,128)(2,1)S(1)} %get-tuple-element.30), channel_id=1, source_target_pairs={{0,1},{1,0},{2,3},{3,2},{4,5},{5,4},{6,7},{7,6},{8,9},{9,8},{10,11... | collective-permute-start | bytes 393224 | tf_op jit(solution)/shard_map/ppermute | solution.py:255
  18.8 1.6 %collective-permute-start.3 = (bf16[128,512]{1,0:T(8,128)(2,1)S(1)}, bf16[128,512]{1,0:T(8,128)(2,1)S(1)}, u32[]{:S(2)}, u32[]{:S(2)}) collective-permute-start(bf16[128,512]{1,0:T(8,128)(2,1)S(1)} %get-tuple-element.24), channel_id=1, source_target_pairs={{0,2},{1,3},{2,0},{3,1},{4,6},{5,7},{6,4},{7,5},{8,10},{9,11},{10,... | collective-permute-start | bytes 393224 | tf_op jit(solution)/shard_map/ppermute | solution.py:255
  20.4 0.0 collective-permute-start.4
  20.4 0.9 %collective-permute-done.8.refs_6_ = bf16[128,512]{1,0:T(8,128)(2,1)S(1)} collective-permute-done((bf16[128,512]{1,0:T(8,128)(2,1)S(1)}, bf16[128,512]{1,0:T(8,128)(2,1)S(1)}, u32[]{:S(2)}, u32[]{:S(2)}) %collective-permute-start.8) | collective-permute-done | bytes 131104 | tf_op jit(solution)/shard_map/ppermute | solution.py:255
  21.3 4.5 %collective-permute-start.5 = (bf16[128,512]{1,0:T(8,128)(2,1)S(1)}, bf16[128,512]{1,0:T(8,128)(2,1)S(1)}, u32[]{:S(2)}, u32[]{:S(2)}) collective-permute-start(bf16[128,512]{1,0:T(8,128)(2,1)S(1)} %get-tuple-element.26), channel_id=1, source_target_pairs={{0,6},{1,7},{2,4},{3,5},{4,2},{5,3},{6,0},{7,1},{8,14},{9,15},{10,... | collective-permute-start | bytes 393224 | tf_op jit(solution)/shard_map/ppermute | solution.py:255
  25.8 0.0 collective-permute-done.9.refs_7_
  25.9 1.3 %collective-permute-start.6 = (bf16[128,512]{1,0:T(8,128)(2,1)S(1)}, bf16[128,512]{1,0:T(8,128)(2,1)S(1)}, u32[]{:S(2)}, u32[]{:S(2)}) collective-permute-start(bf16[128,512]{1,0:T(8,128)(2,1)S(1)} %get-tuple-element.27), channel_id=1, source_target_pairs={{0,7},{1,6},{2,5},{3,4},{4,3},{5,2},{6,1},{7,0},{8,15},{9,14},{10,... | collective-permute-start | bytes 393224 | tf_op jit(solution)/shard_map/ppermute | solution.py:255
  27.1 0.0 collective-permute-done.7.refs_5_
  27.1 0.0 copy-done.1
  27.1 0.9 %finish.2 = (bf16[1024,512]{1,0:T(8,128)(2,1)}, f32[256,256]{1,0:T(8,128)S(1)}) custom-call(f32[256,512]{1,0:T(8,128)S(1)} %get-tuple-element.28.refs_0_.refs_1_, f32[256,512]{1,0:T(8,128)S(1)} %get-tuple-element.28.refs_0_.refs_1_, f32[256,512]{1,0:T(8,128)S(1)} %get-tuple-element.21.refs_10_.refs_2_.refs_3_, ...), custom_call_target="tpu_custom_call" | custom-call | flops 268435456 | bytes 2097152 | tf_op jit(solution)/shard_map/finish/pallas_call | solution.py:189
  28.0 0.0 collective-permute-done.3.refs_4_
  28.0 7.0 %collective-permute-done.4.refs_5_ = bf16[128,512]{1,0:T(8,128)(2,1)S(1)} collective-permute-done((bf16[128,512]{1,0:T(8,128)(2,1)S(1)}, bf16[128,512]{1,0:T(8,128)(2,1)S(1)}, u32[]{:S(2)}, u32[]{:S(2)}) %collective-permute-start.4) | collective-permute-done | bytes 131104 | tf_op jit(solution)/shard_map/ppermute | solution.py:255
  35.0 0.0 collective-permute-done.5.refs_6_
  35.0 0.0 collective-permute-done.6.refs_7_
  35.0 0.6 %finish.3 = (bf16[512,512]{1,0:T(8,128)(2,1)S(1)}, f32[64,256]{1,0:T(8,128)S(1)}, bf16[64,256]{1,0:T(8,128)(2,1)S(1)}, bf16[64,256]{1,0:T(8,128)(2,1)S(1)}, bf16[64,256]{1,0:T(8,128)(2,1)S(1)}) custom-call(f32[256,512]{1,0:T(8,128)S(1)} %get-tuple-element.22.refs_10_.refs_0_.refs_1_, f32[256,512]{1,0:T(8,128)S(1)} %get-tuple-element.22.refs_10_.refs_0_.refs_1_, ...), custom_call_target="tpu_custom_call" | custom-call | flops 268435456 | bytes 2097152 | tf_op jit(solution)/shard_map/finish/pallas_call | solution.py:189
  35.6 0.0 copy-start.4
  35.6 0.6 %collective-permute-start.10 = (bf16[64,256]{1,0:T(8,128)(2,1)S(1)}, bf16[64,256]{1,0:T(8,128)(2,1)S(1)}, u32[]{:S(2)}, u32[]{:S(2)}) collective-permute-start(bf16[64,256]{1,0:T(8,128)(2,1)S(1)} %get-tuple-element.37), channel_id=1, source_target_pairs={{0,8},{8,0},{16,24},{24,16},{1,9},{9,1},{17,25},{25,17},{2,10},{10... | collective-permute-start | bytes 98312 | tf_op jit(solution)/shard_map/ppermute | solution.py:272
  36.2 1.7 %collective-permute-start.11 = (bf16[64,256]{1,0:T(8,128)(2,1)S(1)}, bf16[64,256]{1,0:T(8,128)(2,1)S(1)}, u32[]{:S(2)}, u32[]{:S(2)}) collective-permute-start(bf16[64,256]{1,0:T(8,128)(2,1)S(1)} %get-tuple-element.38), channel_id=1, source_target_pairs={{0,16},{8,24},{16,0},{24,8},{1,17},{9,25},{17,1},{25,9},{2,18},{10... | collective-permute-start | bytes 98312 | tf_op jit(solution)/shard_map/ppermute | solution.py:272
  37.9 1.2 %collective-permute-start.12 = (bf16[64,256]{1,0:T(8,128)(2,1)S(1)}, bf16[64,256]{1,0:T(8,128)(2,1)S(1)}, u32[]{:S(2)}, u32[]{:S(2)}) collective-permute-start(bf16[64,256]{1,0:T(8,128)(2,1)S(1)} %get-tuple-element.39), channel_id=1, source_target_pairs={{0,24},{8,16},{16,8},{24,0},{1,25},{9,17},{17,9},{25,1},{2,26},{10... | collective-permute-start | bytes 98312 | tf_op jit(solution)/shard_map/ppermute | solution.py:272
  39.1 0.8 %store.1 = bf16[1024,512]{1,0:T(8,128)(2,1)} custom-call(bf16[512,512]{1,0:T(8,128)(2,1)S(1)} %get-tuple-element.34.stage, bf16[1024,512]{1,0:T(8,128)(2,1)} %get-tuple-element.35.old), custom_call_target="tpu_custom_call", output_to_operand_aliasing={{}: (1, {})} | custom-call | flops 100000000 | bytes 1048576 | tf_op jit(solution)/shard_map/store/pallas_call | solution.py:122
  40.0 0.0 collective-permute-done.10.refs_1_
  40.0 0.1 collective-permute-done.11.refs_2_
  40.1 2.6 %collective-permute-done.12.refs_3_ = bf16[64,256]{1,0:T(8,128)(2,1)S(1)} collective-permute-done((bf16[64,256]{1,0:T(8,128)(2,1)S(1)}, bf16[64,256]{1,0:T(8,128)(2,1)S(1)}, u32[]{:S(2)}, u32[]{:S(2)}) %collective-permute-start.12) | collective-permute-done | bytes 32800 | tf_op jit(solution)/shard_map/ppermute | solution.py:272
  42.7 0.0 copy-done.4
  42.7 0.8 %atom_update.1 = bf16[64,256]{1,0:T(8,128)(2,1)} custom-call(bf16[64,256]{1,0:T(8,128)(2,1)S(1)} %copy-done.2, bf16[256,256]{1,0:T(8,128)(2,1)S(1)} %copy-done.4, f32[64,256]{1,0:T(8,128)S(1)} %get-tuple-element.36.refs_0_, bf16[64,256]{1,0:T(8,128)(2,1)S(1)} %collective-permute-done.10.refs_1_, bf16[64,256]{1,0:T(8,128)(2,1)S(1)} %collective-permute-done.11.refs_2_, ...), custom_call_target="tpu_custom_call" | custom-call | tf_op jit(solution)/shard_map/atom_update/pallas_call | solution.py:274
Async XLA Ops:
  0.6 6.3 %collective-permute-start.2 = (bf16[64,256]{1,0:T(8,128)(2,1)}, bf16[64,256]{1,0:T(8,128)(2,1)S(1)}, u32[]{:S(2)}, u32[]{:S(2)}) collective-permute-start(bf16[64,256]{1,0:T(8,128)(2,1)} %atom_in.1), channel_id=1, source_target_pairs={{0,24},{8,16},{16,8},{24,0},{1,25},{9,17},{17,9},{25,1},{2,26},{10... | collective-permute-start | bytes 98312 | tf_op jit(solution)/shard_map/ppermute | solution.py:245
  4.6 4.1 %collective-permute-start.1 = (bf16[64,256]{1,0:T(8,128)(2,1)}, bf16[64,256]{1,0:T(8,128)(2,1)S(1)}, u32[]{:S(2)}, u32[]{:S(2)}) collective-permute-start(bf16[64,256]{1,0:T(8,128)(2,1)} %atom_in.1), channel_id=1, source_target_pairs={{0,16},{8,24},{16,0},{24,8},{1,17},{9,25},{17,1},{25,9},{2,18},{10... | collective-permute-start | bytes 98312 | tf_op jit(solution)/shard_map/ppermute | solution.py:245
  5.1 4.1 %collective-permute-start = (bf16[64,256]{1,0:T(8,128)(2,1)}, bf16[64,256]{1,0:T(8,128)(2,1)S(1)}, u32[]{:S(2)}, u32[]{:S(2)}) collective-permute-start(bf16[64,256]{1,0:T(8,128)(2,1)} %atom_in.1), channel_id=1, source_target_pairs={{0,8},{8,0},{16,24},{24,16},{1,9},{9,1},{17,25},{25,17},{2,10},{10... | collective-permute-start | bytes 98312 | tf_op jit(solution)/shard_map/ppermute | solution.py:245
  5.3 4.0 %copy-start = (bf16[1024,512]{1,0:T(8,128)(2,1)S(1)}, bf16[1024,512]{1,0:T(8,128)(2,1)}, u32[]{:S(2)}) copy-start(bf16[1024,512]{1,0:T(8,128)(2,1)} %refs_0_.7) | copy-start | bytes 3145732
  5.3 4.0 %copy-start.2 = (bf16[64,256]{1,0:T(8,128)(2,1)S(1)}, bf16[64,256]{1,0:T(8,128)(2,1)}, u32[]{:S(2)}) copy-start(bf16[64,256]{1,0:T(8,128)(2,1)} %atom_in.1) | copy-start | bytes 98308
  5.3 4.0 %copy-start.3 = (s32[1024]{0:T(1024)S(1)}, s32[1024]{0:T(1024)}, u32[]{:S(2)}) copy-start(s32[1024]{0:T(1024)} %param.13) | copy-start | bytes 12292
  5.3 4.0 %copy-start.5 = (s32[1024]{0:T(1024)S(1)}, s32[1024]{0:T(1024)}, u32[]{:S(2)}) copy-start(s32[1024]{0:T(1024)} %param.14) | copy-start | bytes 12292
  5.3 4.0 %copy-start.6 = (f32[2,512]{1,0:T(2,128)S(1)}, f32[2,512]{1,0:T(2,128)}, u32[]{:S(2)}) copy-start(f32[2,512]{1,0:T(2,128)} %refs_8_.7) | copy-start | bytes 12292
  5.3 4.0 %copy-start.7 = (s32[1,1,8]{2,1,0:T(1,128)S(1)}, s32[1,1,8]{2,1,0:T(1,128)}, u32[]{:S(2)}) copy-start(s32[1,1,8]{2,1,0:T(1,128)} %param.15) | copy-start | bytes 100
  10.9 10.5 %collective-permute-start.8 = (bf16[128,512]{1,0:T(8,128)(2,1)S(1)}, bf16[128,512]{1,0:T(8,128)(2,1)S(1)}, u32[]{:S(2)}, u32[]{:S(2)}) collective-permute-start(bf16[128,512]{1,0:T(8,128)(2,1)S(1)} %get-tuple-element.31), channel_id=1, source_target_pairs={{0,4},{1,5},{2,6},{3,7},{4,0},{5,1},{6,2},{7,3},{8,12},{9,13},{10,... | collective-permute-start | bytes 393224 | tf_op jit(solution)/shard_map/ppermute | solution.py:255
  13.5 12.3 %collective-permute-start.9 = (bf16[128,512]{1,0:T(8,128)(2,1)S(1)}, bf16[128,512]{1,0:T(8,128)(2,1)S(1)}, u32[]{:S(2)}, u32[]{:S(2)}) collective-permute-start(bf16[128,512]{1,0:T(8,128)(2,1)S(1)} %get-tuple-element.32), channel_id=1, source_target_pairs={{0,5},{1,4},{2,7},{3,6},{4,1},{5,0},{6,3},{7,2},{8,13},{9,12},{10,... | collective-permute-start | bytes 393224 | tf_op jit(solution)/shard_map/ppermute | solution.py:255
  16.7 10.4 %copy-start.1 = (bf16[512,256]{1,0:T(8,128)(2,1)S(1)}, bf16[512,256]{1,0:T(8,128)(2,1)}, u32[]{:S(2)}) copy-start(bf16[512,256]{1,0:T(8,128)(2,1)} %refs_9_.3) | copy-start | bytes 786436
  18.3 8.8 %collective-permute-start.7 = (bf16[128,512]{1,0:T(8,128)(2,1)S(1)}, bf16[128,512]{1,0:T(8,128)(2,1)S(1)}, u32[]{:S(2)}, u32[]{:S(2)}) collective-permute-start(bf16[128,512]{1,0:T(8,128)(2,1)S(1)} %get-tuple-element.30), channel_id=1, source_target_pairs={{0,1},{1,0},{2,3},{3,2},{4,5},{5,4},{6,7},{7,6},{8,9},{9,8},{10,11... | collective-permute-start | bytes 393224 | tf_op jit(solution)/shard_map/ppermute | solution.py:255
  18.8 9.2 %collective-permute-start.3 = (bf16[128,512]{1,0:T(8,128)(2,1)S(1)}, bf16[128,512]{1,0:T(8,128)(2,1)S(1)}, u32[]{:S(2)}, u32[]{:S(2)}) collective-permute-start(bf16[128,512]{1,0:T(8,128)(2,1)S(1)} %get-tuple-element.24), channel_id=1, source_target_pairs={{0,2},{1,3},{2,0},{3,1},{4,6},{5,7},{6,4},{7,5},{8,10},{9,11},{10,... | collective-permute-start | bytes 393224 | tf_op jit(solution)/shard_map/ppermute | solution.py:255
  20.4 14.6 %collective-permute-start.4 = (bf16[128,512]{1,0:T(8,128)(2,1)S(1)}, bf16[128,512]{1,0:T(8,128)(2,1)S(1)}, u32[]{:S(2)}, u32[]{:S(2)}) collective-permute-start(bf16[128,512]{1,0:T(8,128)(2,1)S(1)} %get-tuple-element.25), channel_id=1, source_target_pairs={{0,3},{1,2},{2,1},{3,0},{4,7},{5,6},{6,5},{7,4},{8,11},{9,10},{10,... | collective-permute-start | bytes 393224 | tf_op jit(solution)/shard_map/ppermute | solution.py:255
  21.3 13.7 %collective-permute-start.5 = (bf16[128,512]{1,0:T(8,128)(2,1)S(1)}, bf16[128,512]{1,0:T(8,128)(2,1)S(1)}, u32[]{:S(2)}, u32[]{:S(2)}) collective-permute-start(bf16[128,512]{1,0:T(8,128)(2,1)S(1)} %get-tuple-element.26), channel_id=1, source_target_pairs={{0,6},{1,7},{2,4},{3,5},{4,2},{5,3},{6,0},{7,1},{8,14},{9,15},{10,... | collective-permute-start | bytes 393224 | tf_op jit(solution)/shard_map/ppermute | solution.py:255
  25.9 9.2 %collective-permute-start.6 = (bf16[128,512]{1,0:T(8,128)(2,1)S(1)}, bf16[128,512]{1,0:T(8,128)(2,1)S(1)}, u32[]{:S(2)}, u32[]{:S(2)}) collective-permute-start(bf16[128,512]{1,0:T(8,128)(2,1)S(1)} %get-tuple-element.27), channel_id=1, source_target_pairs={{0,7},{1,6},{2,5},{3,4},{4,3},{5,2},{6,1},{7,0},{8,15},{9,14},{10,... | collective-permute-start | bytes 393224 | tf_op jit(solution)/shard_map/ppermute | solution.py:255
  35.6 7.1 %copy-start.4 = (bf16[256,256]{1,0:T(8,128)(2,1)S(1)}, bf16[256,256]{1,0:T(8,128)(2,1)}, u32[]{:S(2)}) copy-start(bf16[256,256]{1,0:T(8,128)(2,1)} %w_atom.1) | copy-start | bytes 393220
  35.6 4.4 %collective-permute-start.10 = (bf16[64,256]{1,0:T(8,128)(2,1)S(1)}, bf16[64,256]{1,0:T(8,128)(2,1)S(1)}, u32[]{:S(2)}, u32[]{:S(2)}) collective-permute-start(bf16[64,256]{1,0:T(8,128)(2,1)S(1)} %get-tuple-element.37), channel_id=1, source_target_pairs={{0,8},{8,0},{16,24},{24,16},{1,9},{9,1},{17,25},{25,17},{2,10},{10... | collective-permute-start | bytes 98312 | tf_op jit(solution)/shard_map/ppermute | solution.py:272
  36.2 3.9 %collective-permute-start.11 = (bf16[64,256]{1,0:T(8,128)(2,1)S(1)}, bf16[64,256]{1,0:T(8,128)(2,1)S(1)}, u32[]{:S(2)}, u32[]{:S(2)}) collective-permute-start(bf16[64,256]{1,0:T(8,128)(2,1)S(1)} %get-tuple-element.38), channel_id=1, source_target_pairs={{0,16},{8,24},{16,0},{24,8},{1,17},{9,25},{17,1},{25,9},{2,18},{10... | collective-permute-start | bytes 98312 | tf_op jit(solution)/shard_map/ppermute | solution.py:272
  37.9 4.8 %collective-permute-start.12 = (bf16[64,256]{1,0:T(8,128)(2,1)S(1)}, bf16[64,256]{1,0:T(8,128)(2,1)S(1)}, u32[]{:S(2)}, u32[]{:S(2)}) collective-permute-start(bf16[64,256]{1,0:T(8,128)(2,1)S(1)} %get-tuple-element.39), channel_id=1, source_target_pairs={{0,24},{8,16},{16,8},{24,0},{1,25},{9,17},{17,9},{25,1},{2,26},{10... | collective-permute-start | bytes 98312 | tf_op jit(solution)/shard_map/ppermute | solution.py:272

commit v4 on v3

--- a/solution.py
+++ b/solution.py
@@ -35,8 +35,8 @@
     feat = x.shape[1]
     for layer in range(gains_ref.shape[0]):
         scale = lax.rsqrt(jnp.mean(x * x, axis=-1, keepdims=True) + 1e-06)
-        normed = (x * scale * gains_ref[layer : layer + 1, :]).astype(BF16)
-        y = dot(normed, weights[first + layer * feat : first + (layer + 1) * feat])
+        scaled = (x * gains_ref[layer : layer + 1, :]).astype(BF16)
+        y = scale * dot(scaled, weights[first + layer * feat : first + (layer + 1) * feat])
         x = x + silu(y)
     return x
 
@@ -256,8 +256,8 @@
     acc = out = None
     half = blocks // 2
     groups = [[0, 1, half, half + 1]]
-    rest = list(range(2, half)) + list(range(half + 2, blocks))
-    groups += [rest[n : n + 4] for n in range(0, len(rest), 4)]
+    for rest in (list(range(2, half)), list(range(half + 2, blocks))):
+        groups += [rest[n : n + 4] for n in range(0, len(rest), 4)]
     for ds in groups:
         last = ds is groups[-1]
         rows, *sums = finish(

time: 43.6 us -> 44.2 us (1.014)
  starting transfers between devices: 18.7 us -> 19.2 us
    pallas_call x2 -> x3, Pallas kernels: 1.44 us -> 2.09 us  [finish(): pl.pallas_call(functools.partial(finish_kernel, ds, [at for _, at in xs],...]
    pallas_call x4, Pallas kernels: 6.33 us -> 5.7 us  [edge_group(): pl.pallas_call(functools.partial(edge_kernel, ds, len(atoms)), out_shape=...]
    ppermute x7, starting transfers between devices: 10.5 us -> 11 us  [on_device(): msgs[d] = lax.ppermute(sent[g], 'dst', over(blocks, d))]
where the time goes in v4:
time: 44.2 us; the launch traced here: 44 us
  starting transfers between devices  19.2 us (43%)
  waiting for transfers between devices  13.1 us (30%)
  Pallas kernels  9.28 us (21%)
  other arithmetic  1.63 us (4%)
  between operations  0.81 us (2%)
    ppermute x7, starting transfers between devices, on_device(): msgs[d] = lax.ppermute(sent[g], 'dst', over(blocks, d))  11 us
    ppermute x7, waiting for transfers between devices, on_device(): msgs[d] = lax.ppermute(sent[g], 'dst', over(blocks, d))  7.93 us
    pallas_call x4, Pallas kernels, edge_group(): pl.pallas_call(functools.partial(edge_kernel, ds, len(atoms)), out_shape=...  5.7 us
    ppermute x3, starting transfers between devices, on_device(): held.append(lax.ppermute(atom_in, 'src', over(shards, p)))  4.63 us
    ppermute x3, starting transfers between devices, on_device(): parts.append(lax.ppermute(sums[p], 'src', over(shards, p)))  3.55 us
    ppermute x3, waiting for transfers between devices, on_device(): parts.append(lax.ppermute(sums[p], 'src', over(shards, p)))  2.85 us
    ppermute x3, waiting for transfers between devices, on_device(): held.append(lax.ppermute(atom_in, 'src', over(shards, p)))  2.32 us
    pallas_call x3, Pallas kernels, finish(): pl.pallas_call(functools.partial(finish_kernel, ds, [at for _, at in xs],...  2.09 us
  transfers between devices with their start and end apart: 13, of which 6 were waited for; matrix products, arithmetic and copies ran while one was open for 4% of the time, Pallas kernels for 15%

profile of v4, /device:TPU:0, one launch (start us, length us, event | category | flops | bytes accessed | tf_op | source)
XLA Modules:
  0.0 44.0 jit_solution(263632216311728473)
XLA Ops:
  0.6 4.0 %collective-permute-start.2 = (bf16[64,256]{1,0:T(8,128)(2,1)}, bf16[64,256]{1,0:T(8,128)(2,1)S(1)}, u32[]{:S(2)}, u32[]{:S(2)}) collective-permute-start(bf16[64,256]{1,0:T(8,128)(2,1)} %atom_in.1), channel_id=1, source_target_pairs={{0,24},{8,16},{16,8},{24,0},{1,25},{9,17},{17,9},{25,1},{2,26},{10... | collective-permute-start | bytes 98312 | tf_op jit(solution)/shard_map/ppermute | solution.py:245
  4.6 0.5 %collective-permute-start.1 = (bf16[64,256]{1,0:T(8,128)(2,1)}, bf16[64,256]{1,0:T(8,128)(2,1)S(1)}, u32[]{:S(2)}, u32[]{:S(2)}) collective-permute-start(bf16[64,256]{1,0:T(8,128)(2,1)} %atom_in.1), channel_id=1, source_target_pairs={{0,16},{8,24},{16,0},{24,8},{1,17},{9,25},{17,1},{25,9},{2,18},{10... | collective-permute-start | bytes 98312 | tf_op jit(solution)/shard_map/ppermute | solution.py:245
  5.1 0.1 collective-permute-start
  5.3 0.0 copy-start
  5.3 0.0 copy-start.2
  5.3 0.0 copy-start.3
  5.3 0.0 copy-start.5
  5.3 0.0 copy-start.6
  5.3 0.0 copy-start.7
  5.3 1.6 %pad_maximum_fusion.refs_9_ = bf16[1792,512]{1,0:T(8,128)(2,1)S(1)} fusion(bf16[512,512]{1,0:T(8,128)(2,1)} %param.19, bf16[1024,512]{1,0:T(8,128)(2,1)} %bitcast.19, bf16[256,512]{1,0:T(8,128)(2,1)} %param.16), kind=kLoop, calls=%fused_computation | loop fusion | flops 5505024 | bytes 3670016 | tf_op jit(solution)/shard_map/concatenate | solution.py:246
  6.9 0.0 collective-permute-done.2.refs_4_
  6.9 1.8 %collective-permute-done.1.refs_3_ = bf16[64,256]{1,0:T(8,128)(2,1)S(1)} collective-permute-done((bf16[64,256]{1,0:T(8,128)(2,1)}, bf16[64,256]{1,0:T(8,128)(2,1)S(1)}, u32[]{:S(2)}, u32[]{:S(2)}) %collective-permute-start.1) | collective-permute-done | bytes 32800 | tf_op jit(solution)/shard_map/ppermute | solution.py:245
  8.7 0.5 %collective-permute-done.refs_2_ = bf16[64,256]{1,0:T(8,128)(2,1)S(1)} collective-permute-done((bf16[64,256]{1,0:T(8,128)(2,1)}, bf16[64,256]{1,0:T(8,128)(2,1)S(1)}, u32[]{:S(2)}, u32[]{:S(2)}) %collective-permute-start) | collective-permute-done | bytes 32800 | tf_op jit(solution)/shard_map/ppermute | solution.py:245
  9.3 0.0 copy-done
  9.3 0.0 copy-done.2
  9.3 0.0 copy-done.3
  9.3 0.0 copy-done.5
  9.3 0.0 copy-done.6
  9.3 0.0 copy-done.7
  9.3 1.4 %edge_group.4 = (f32[256,512]{1,0:T(8,128)S(1)}, bf16[128,512]{1,0:T(8,128)(2,1)S(1)}, bf16[128,512]{1,0:T(8,128)(2,1)S(1)}) custom-call(bf16[1024,512]{1,0:T(8,128)(2,1)S(1)} %copy-done, bf16[64,256]{1,0:T(8,128)(2,1)S(1)} %copy-done.2, bf16[64,256]{1,0:T(8,128)(2,1)S(1)} %collective-permute-done.refs_2_, ...), custom_call_target="tpu_custom_call" | custom-call | flops 536870912 | bytes 1048576 | tf_op jit(solution)/shard_map/edge_group/pallas_call | solution.py:89
  10.7 2.6 %collective-permute-start.8 = (bf16[128,512]{1,0:T(8,128)(2,1)S(1)}, bf16[128,512]{1,0:T(8,128)(2,1)S(1)}, u32[]{:S(2)}, u32[]{:S(2)}) collective-permute-start(bf16[128,512]{1,0:T(8,128)(2,1)S(1)} %get-tuple-element.33), channel_id=1, source_target_pairs={{0,4},{1,5},{2,6},{3,7},{4,0},{5,1},{6,2},{7,3},{8,12},{9,13},{10,... | collective-permute-start | bytes 393224 | tf_op jit(solution)/shard_map/ppermute | solution.py:255
  13.4 0.0 collective-permute-start.9
  13.4 1.4 %edge_group.5 = (f32[256,512]{1,0:T(8,128)S(1)}, bf16[128,512]{1,0:T(8,128)(2,1)S(1)}, bf16[128,512]{1,0:T(8,128)(2,1)S(1)}) custom-call(bf16[1024,512]{1,0:T(8,128)(2,1)S(1)} %copy-done, bf16[64,256]{1,0:T(8,128)(2,1)S(1)} %copy-done.2, bf16[64,256]{1,0:T(8,128)(2,1)S(1)} %collective-permute-done.refs_2_, ...), custom_call_target="tpu_custom_call" | custom-call | flops 536870912 | bytes 1048576 | tf_op jit(solution)/shard_map/edge_group/pallas_call | solution.py:89
  14.8 1.4 %edge_group.6 = (f32[256,512]{1,0:T(8,128)S(1)}, bf16[128,512]{1,0:T(8,128)(2,1)S(1)}, bf16[128,512]{1,0:T(8,128)(2,1)S(1)}) custom-call(bf16[1024,512]{1,0:T(8,128)(2,1)S(1)} %copy-done, bf16[64,256]{1,0:T(8,128)(2,1)S(1)} %copy-done.2, bf16[64,256]{1,0:T(8,128)(2,1)S(1)} %collective-permute-done.refs_2_, ...), custom_call_target="tpu_custom_call" | custom-call | flops 536870912 | bytes 1048576 | tf_op jit(solution)/shard_map/edge_group/pallas_call | solution.py:89
  16.2 0.0 copy-start.1
  16.3 1.4 %edge_group.7 = (f32[256,512]{1,0:T(8,128)S(1)}, bf16[128,512]{1,0:T(8,128)(2,1)S(1)}, bf16[128,512]{1,0:T(8,128)(2,1)S(1)}) custom-call(bf16[1024,512]{1,0:T(8,128)(2,1)S(1)} %copy-done, bf16[64,256]{1,0:T(8,128)(2,1)S(1)} %copy-done.2, bf16[64,256]{1,0:T(8,128)(2,1)S(1)} %collective-permute-done.refs_2_, ...), custom_call_target="tpu_custom_call" | custom-call | flops 536870912 | bytes 1048576 | tf_op jit(solution)/shard_map/edge_group/pallas_call | solution.py:89
  17.7 0.5 %collective-permute-start.7 = (bf16[128,512]{1,0:T(8,128)(2,1)S(1)}, bf16[128,512]{1,0:T(8,128)(2,1)S(1)}, u32[]{:S(2)}, u32[]{:S(2)}) collective-permute-start(bf16[128,512]{1,0:T(8,128)(2,1)S(1)} %get-tuple-element.32), channel_id=1, source_target_pairs={{0,1},{1,0},{2,3},{3,2},{4,5},{5,4},{6,7},{7,6},{8,9},{9,8},{10,11... | collective-permute-start | bytes 393224 | tf_op jit(solution)/shard_map/ppermute | solution.py:255
  18.2 1.6 %collective-permute-start.5 = (bf16[128,512]{1,0:T(8,128)(2,1)S(1)}, bf16[128,512]{1,0:T(8,128)(2,1)S(1)}, u32[]{:S(2)}, u32[]{:S(2)}) collective-permute-start(bf16[128,512]{1,0:T(8,128)(2,1)S(1)} %get-tuple-element.28), channel_id=1, source_target_pairs={{0,2},{1,3},{2,0},{3,1},{4,6},{5,7},{6,4},{7,5},{8,10},{9,11},{10,... | collective-permute-start | bytes 393224 | tf_op jit(solution)/shard_map/ppermute | solution.py:255
  19.8 0.0 collective-permute-start.6
  19.8 1.4 %collective-permute-done.8.refs_6_ = bf16[128,512]{1,0:T(8,128)(2,1)S(1)} collective-permute-done((bf16[128,512]{1,0:T(8,128)(2,1)S(1)}, bf16[128,512]{1,0:T(8,128)(2,1)S(1)}, u32[]{:S(2)}, u32[]{:S(2)}) %collective-permute-start.8) | collective-permute-done | bytes 131104 | tf_op jit(solution)/shard_map/ppermute | solution.py:255
  21.2 4.5 %collective-permute-start.3 = (bf16[128,512]{1,0:T(8,128)(2,1)S(1)}, bf16[128,512]{1,0:T(8,128)(2,1)S(1)}, u32[]{:S(2)}, u32[]{:S(2)}) collective-permute-start(bf16[128,512]{1,0:T(8,128)(2,1)S(1)} %get-tuple-element.26), channel_id=1, source_target_pairs={{0,6},{1,7},{2,4},{3,5},{4,2},{5,3},{6,0},{7,1},{8,14},{9,15},{10,... | collective-permute-start | bytes 393224 | tf_op jit(solution)/shard_map/ppermute | solution.py:255
  25.7 0.0 collective-permute-done.9.refs_7_
  25.7 1.7 %collective-permute-start.4 = (bf16[128,512]{1,0:T(8,128)(2,1)S(1)}, bf16[128,512]{1,0:T(8,128)(2,1)S(1)}, u32[]{:S(2)}, u32[]{:S(2)}) collective-permute-start(bf16[128,512]{1,0:T(8,128)(2,1)S(1)} %get-tuple-element.27), channel_id=1, source_target_pairs={{0,7},{1,6},{2,5},{3,4},{4,3},{5,2},{6,1},{7,0},{8,15},{9,14},{10,... | collective-permute-start | bytes 393224 | tf_op jit(solution)/shard_map/ppermute | solution.py:255
  27.4 0.0 collective-permute-done.7.refs_5_
  27.5 0.0 copy-done.1
  27.5 0.9 %finish.3 = (bf16[1024,512]{1,0:T(8,128)(2,1)}, f32[256,256]{1,0:T(8,128)S(1)}) custom-call(f32[256,512]{1,0:T(8,128)S(1)} %get-tuple-element.30.refs_0_.refs_1_, f32[256,512]{1,0:T(8,128)S(1)} %get-tuple-element.30.refs_0_.refs_1_, f32[256,512]{1,0:T(8,128)S(1)} %get-tuple-element.23.refs_10_.refs_2_.refs_3_, ...), custom_call_target="tpu_custom_call" | custom-call | flops 268435456 | bytes 2097152 | tf_op jit(solution)/shard_map/finish/pallas_call | solution.py:189
  28.3 0.0 collective-permute-done.5.refs_2_
  28.4 6.5 %collective-permute-done.6.refs_3_ = bf16[128,512]{1,0:T(8,128)(2,1)S(1)} collective-permute-done((bf16[128,512]{1,0:T(8,128)(2,1)S(1)}, bf16[128,512]{1,0:T(8,128)(2,1)S(1)}, u32[]{:S(2)}, u32[]{:S(2)}) %collective-permute-start.6) | collective-permute-done | bytes 131104 | tf_op jit(solution)/shard_map/ppermute | solution.py:255
  34.8 0.8 %finish.4 = (bf16[1024,512]{1,0:T(8,128)(2,1)}, f32[256,256]{1,0:T(8,128)S(1)}) custom-call(f32[256,512]{1,0:T(8,128)S(1)} %get-tuple-element.24.refs_10_.refs_0_.refs_1_, f32[256,512]{1,0:T(8,128)S(1)} %get-tuple-element.24.refs_10_.refs_0_.refs_1_, bf16[128,512]{1,0:T(8,128)(2,1)S(1)} %collective-permute-done.5.refs_2_, ...), custom_call_target="tpu_custom_call", output_to_operand_aliasing={{0}: (7, {})} | custom-call | flops 134217728 | bytes 1048576 | tf_op jit(solution)/shard_map/finish/pallas_call | solution.py:189
  35.6 0.0 collective-permute-done.3.refs_2_
  35.6 0.0 collective-permute-done.4.refs_3_
  35.6 0.0 copy-start.4
  35.7 0.4 %finish.5 = (bf16[256,512]{1,0:T(8,128)(2,1)S(1)}, f32[64,256]{1,0:T(8,128)S(1)}, bf16[64,256]{1,0:T(8,128)(2,1)S(1)}, bf16[64,256]{1,0:T(8,128)(2,1)S(1)}, bf16[64,256]{1,0:T(8,128)(2,1)S(1)}) custom-call(f32[256,512]{1,0:T(8,128)S(1)} %get-tuple-element.25.refs_10_.refs_0_.refs_1_, f32[256,512]{1,0:T(8,128)S(1)} %get-tuple-element.25.refs_10_.refs_0_.refs_1_, ...), custom_call_target="tpu_custom_call" | custom-call | flops 134217728 | bytes 1048576 | tf_op jit(solution)/shard_map/finish/pallas_call | solution.py:189
  36.1 0.6 %collective-permute-start.10 = (bf16[64,256]{1,0:T(8,128)(2,1)S(1)}, bf16[64,256]{1,0:T(8,128)(2,1)S(1)}, u32[]{:S(2)}, u32[]{:S(2)}) collective-permute-start(bf16[64,256]{1,0:T(8,128)(2,1)S(1)} %get-tuple-element.41), channel_id=1, source_target_pairs={{0,8},{8,0},{16,24},{24,16},{1,9},{9,1},{17,25},{25,17},{2,10},{10... | collective-permute-start | bytes 98312 | tf_op jit(solution)/shard_map/ppermute | solution.py:272
  36.7 1.7 %collective-permute-start.11 = (bf16[64,256]{1,0:T(8,128)(2,1)S(1)}, bf16[64,256]{1,0:T(8,128)(2,1)S(1)}, u32[]{:S(2)}, u32[]{:S(2)}) collective-permute-start(bf16[64,256]{1,0:T(8,128)(2,1)S(1)} %get-tuple-element.42), channel_id=1, source_target_pairs={{0,16},{8,24},{16,0},{24,8},{1,17},{9,25},{17,1},{25,9},{2,18},{10... | collective-permute-start | bytes 98312 | tf_op jit(solution)/shard_map/ppermute | solution.py:272
  38.4 1.2 %collective-permute-start.12 = (bf16[64,256]{1,0:T(8,128)(2,1)S(1)}, bf16[64,256]{1,0:T(8,128)(2,1)S(1)}, u32[]{:S(2)}, u32[]{:S(2)}) collective-permute-start(bf16[64,256]{1,0:T(8,128)(2,1)S(1)} %get-tuple-element.43), channel_id=1, source_target_pairs={{0,24},{8,16},{16,8},{24,0},{1,25},{9,17},{17,9},{25,1},{2,26},{10... | collective-permute-start | bytes 98312 | tf_op jit(solution)/shard_map/ppermute | solution.py:272
  39.7 0.7 %store.1 = bf16[1024,512]{1,0:T(8,128)(2,1)} custom-call(bf16[256,512]{1,0:T(8,128)(2,1)S(1)} %get-tuple-element.38.stage, bf16[1024,512]{1,0:T(8,128)(2,1)} %get-tuple-element.39.old), custom_call_target="tpu_custom_call", output_to_operand_aliasing={{}: (1, {})} | custom-call | flops 100000000 | bytes 524288 | tf_op jit(solution)/shard_map/store/pallas_call | solution.py:122
  40.4 0.0 collective-permute-done.10.refs_1_
  40.4 0.2 collective-permute-done.11.refs_2_
  40.6 2.6 %collective-permute-done.12.refs_3_ = bf16[64,256]{1,0:T(8,128)(2,1)S(1)} collective-permute-done((bf16[64,256]{1,0:T(8,128)(2,1)S(1)}, bf16[64,256]{1,0:T(8,128)(2,1)S(1)}, u32[]{:S(2)}, u32[]{:S(2)}) %collective-permute-start.12) | collective-permute-done | bytes 32800 | tf_op jit(solution)/shard_map/ppermute | solution.py:272
  43.2 0.0 copy-done.4
  43.2 0.8 %atom_update.1 = bf16[64,256]{1,0:T(8,128)(2,1)} custom-call(bf16[64,256]{1,0:T(8,128)(2,1)S(1)} %copy-done.2, bf16[256,256]{1,0:T(8,128)(2,1)S(1)} %copy-done.4, f32[64,256]{1,0:T(8,128)S(1)} %get-tuple-element.40.refs_0_, bf16[64,256]{1,0:T(8,128)(2,1)S(1)} %collective-permute-done.10.refs_1_, bf16[64,256]{1,0:T(8,128)(2,1)S(1)} %collective-permute-done.11.refs_2_, ...), custom_call_target="tpu_custom_call" | custom-call | tf_op jit(solution)/shard_map/atom_update/pallas_call | solution.py:274
Async XLA Ops:
  0.6 6.3 %collective-permute-start.2 = (bf16[64,256]{1,0:T(8,128)(2,1)}, bf16[64,256]{1,0:T(8,128)(2,1)S(1)}, u32[]{:S(2)}, u32[]{:S(2)}) collective-permute-start(bf16[64,256]{1,0:T(8,128)(2,1)} %atom_in.1), channel_id=1, source_target_pairs={{0,24},{8,16},{16,8},{24,0},{1,25},{9,17},{17,9},{25,1},{2,26},{10... | collective-permute-start | bytes 98312 | tf_op jit(solution)/shard_map/ppermute | solution.py:245
  4.6 4.1 %collective-permute-start.1 = (bf16[64,256]{1,0:T(8,128)(2,1)}, bf16[64,256]{1,0:T(8,128)(2,1)S(1)}, u32[]{:S(2)}, u32[]{:S(2)}) collective-permute-start(bf16[64,256]{1,0:T(8,128)(2,1)} %atom_in.1), channel_id=1, source_target_pairs={{0,16},{8,24},{16,0},{24,8},{1,17},{9,25},{17,1},{25,9},{2,18},{10... | collective-permute-start | bytes 98312 | tf_op jit(solution)/shard_map/ppermute | solution.py:245
  5.1 4.1 %collective-permute-start = (bf16[64,256]{1,0:T(8,128)(2,1)}, bf16[64,256]{1,0:T(8,128)(2,1)S(1)}, u32[]{:S(2)}, u32[]{:S(2)}) collective-permute-start(bf16[64,256]{1,0:T(8,128)(2,1)} %atom_in.1), channel_id=1, source_target_pairs={{0,8},{8,0},{16,24},{24,16},{1,9},{9,1},{17,25},{25,17},{2,10},{10... | collective-permute-start | bytes 98312 | tf_op jit(solution)/shard_map/ppermute | solution.py:245
  5.3 4.0 %copy-start = (bf16[1024,512]{1,0:T(8,128)(2,1)S(1)}, bf16[1024,512]{1,0:T(8,128)(2,1)}, u32[]{:S(2)}) copy-start(bf16[1024,512]{1,0:T(8,128)(2,1)} %refs_0_.7) | copy-start | bytes 3145732
  5.3 4.0 %copy-start.2 = (bf16[64,256]{1,0:T(8,128)(2,1)S(1)}, bf16[64,256]{1,0:T(8,128)(2,1)}, u32[]{:S(2)}) copy-start(bf16[64,256]{1,0:T(8,128)(2,1)} %atom_in.1) | copy-start | bytes 98308
  5.3 4.0 %copy-start.3 = (s32[1024]{0:T(1024)S(1)}, s32[1024]{0:T(1024)}, u32[]{:S(2)}) copy-start(s32[1024]{0:T(1024)} %param.13) | copy-start | bytes 12292
  5.3 4.0 %copy-start.5 = (s32[1024]{0:T(1024)S(1)}, s32[1024]{0:T(1024)}, u32[]{:S(2)}) copy-start(s32[1024]{0:T(1024)} %param.14) | copy-start | bytes 12292
  5.3 4.0 %copy-start.6 = (f32[2,512]{1,0:T(2,128)S(1)}, f32[2,512]{1,0:T(2,128)}, u32[]{:S(2)}) copy-start(f32[2,512]{1,0:T(2,128)} %refs_8_.7) | copy-start | bytes 12292
  5.3 4.0 %copy-start.7 = (s32[1,1,8]{2,1,0:T(1,128)S(1)}, s32[1,1,8]{2,1,0:T(1,128)}, u32[]{:S(2)}) copy-start(s32[1,1,8]{2,1,0:T(1,128)} %param.15) | copy-start | bytes 100
  10.7 10.5 %collective-permute-start.8 = (bf16[128,512]{1,0:T(8,128)(2,1)S(1)}, bf16[128,512]{1,0:T(8,128)(2,1)S(1)}, u32[]{:S(2)}, u32[]{:S(2)}) collective-permute-start(bf16[128,512]{1,0:T(8,128)(2,1)S(1)} %get-tuple-element.33), channel_id=1, source_target_pairs={{0,4},{1,5},{2,6},{3,7},{4,0},{5,1},{6,2},{7,3},{8,12},{9,13},{10,... | collective-permute-start | bytes 393224 | tf_op jit(solution)/shard_map/ppermute | solution.py:255
  13.4 12.4 %collective-permute-start.9 = (bf16[128,512]{1,0:T(8,128)(2,1)S(1)}, bf16[128,512]{1,0:T(8,128)(2,1)S(1)}, u32[]{:S(2)}, u32[]{:S(2)}) collective-permute-start(bf16[128,512]{1,0:T(8,128)(2,1)S(1)} %get-tuple-element.34), channel_id=1, source_target_pairs={{0,5},{1,4},{2,7},{3,6},{4,1},{5,0},{6,3},{7,2},{8,13},{9,12},{10,... | collective-permute-start | bytes 393224 | tf_op jit(solution)/shard_map/ppermute | solution.py:255
  16.2 11.2 %copy-start.1 = (bf16[512,256]{1,0:T(8,128)(2,1)S(1)}, bf16[512,256]{1,0:T(8,128)(2,1)}, u32[]{:S(2)}) copy-start(bf16[512,256]{1,0:T(8,128)(2,1)} %refs_5_.3) | copy-start | bytes 786436
  17.7 9.8 %collective-permute-start.7 = (bf16[128,512]{1,0:T(8,128)(2,1)S(1)}, bf16[128,512]{1,0:T(8,128)(2,1)S(1)}, u32[]{:S(2)}, u32[]{:S(2)}) collective-permute-start(bf16[128,512]{1,0:T(8,128)(2,1)S(1)} %get-tuple-element.32), channel_id=1, source_target_pairs={{0,1},{1,0},{2,3},{3,2},{4,5},{5,4},{6,7},{7,6},{8,9},{9,8},{10,11... | collective-permute-start | bytes 393224 | tf_op jit(solution)/shard_map/ppermute | solution.py:255
  18.2 10.1 %collective-permute-start.5 = (bf16[128,512]{1,0:T(8,128)(2,1)S(1)}, bf16[128,512]{1,0:T(8,128)(2,1)S(1)}, u32[]{:S(2)}, u32[]{:S(2)}) collective-permute-start(bf16[128,512]{1,0:T(8,128)(2,1)S(1)} %get-tuple-element.28), channel_id=1, source_target_pairs={{0,2},{1,3},{2,0},{3,1},{4,6},{5,7},{6,4},{7,5},{8,10},{9,11},{10,... | collective-permute-start | bytes 393224 | tf_op jit(solution)/shard_map/ppermute | solution.py:255
  19.8 15.1 %collective-permute-start.6 = (bf16[128,512]{1,0:T(8,128)(2,1)S(1)}, bf16[128,512]{1,0:T(8,128)(2,1)S(1)}, u32[]{:S(2)}, u32[]{:S(2)}) collective-permute-start(bf16[128,512]{1,0:T(8,128)(2,1)S(1)} %get-tuple-element.29), channel_id=1, source_target_pairs={{0,3},{1,2},{2,1},{3,0},{4,7},{5,6},{6,5},{7,4},{8,11},{9,10},{10,... | collective-permute-start | bytes 393224 | tf_op jit(solution)/shard_map/ppermute | solution.py:255
  21.2 14.4 %collective-permute-start.3 = (bf16[128,512]{1,0:T(8,128)(2,1)S(1)}, bf16[128,512]{1,0:T(8,128)(2,1)S(1)}, u32[]{:S(2)}, u32[]{:S(2)}) collective-permute-start(bf16[128,512]{1,0:T(8,128)(2,1)S(1)} %get-tuple-element.26), channel_id=1, source_target_pairs={{0,6},{1,7},{2,4},{3,5},{4,2},{5,3},{6,0},{7,1},{8,14},{9,15},{10,... | collective-permute-start | bytes 393224 | tf_op jit(solution)/shard_map/ppermute | solution.py:255
  25.7 9.9 %collective-permute-start.4 = (bf16[128,512]{1,0:T(8,128)(2,1)S(1)}, bf16[128,512]{1,0:T(8,128)(2,1)S(1)}, u32[]{:S(2)}, u32[]{:S(2)}) collective-permute-start(bf16[128,512]{1,0:T(8,128)(2,1)S(1)} %get-tuple-element.27), channel_id=1, source_target_pairs={{0,7},{1,6},{2,5},{3,4},{4,3},{5,2},{6,1},{7,0},{8,15},{9,14},{10,... | collective-permute-start | bytes 393224 | tf_op jit(solution)/shard_map/ppermute | solution.py:255
  35.6 7.6 %copy-start.4 = (bf16[256,256]{1,0:T(8,128)(2,1)S(1)}, bf16[256,256]{1,0:T(8,128)(2,1)}, u32[]{:S(2)}) copy-start(bf16[256,256]{1,0:T(8,128)(2,1)} %w_atom.1) | copy-start | bytes 393220
  36.1 4.3 %collective-permute-start.10 = (bf16[64,256]{1,0:T(8,128)(2,1)S(1)}, bf16[64,256]{1,0:T(8,128)(2,1)S(1)}, u32[]{:S(2)}, u32[]{:S(2)}) collective-permute-start(bf16[64,256]{1,0:T(8,128)(2,1)S(1)} %get-tuple-element.41), channel_id=1, source_target_pairs={{0,8},{8,0},{16,24},{24,16},{1,9},{9,1},{17,25},{25,17},{2,10},{10... | collective-permute-start | bytes 98312 | tf_op jit(solution)/shard_map/ppermute | solution.py:272
  36.7 3.9 %collective-permute-start.11 = (bf16[64,256]{1,0:T(8,128)(2,1)S(1)}, bf16[64,256]{1,0:T(8,128)(2,1)S(1)}, u32[]{:S(2)}, u32[]{:S(2)}) collective-permute-start(bf16[64,256]{1,0:T(8,128)(2,1)S(1)} %get-tuple-element.42), channel_id=1, source_target_pairs={{0,16},{8,24},{16,0},{24,8},{1,17},{9,25},{17,1},{25,9},{2,18},{10... | collective-permute-start | bytes 98312 | tf_op jit(solution)/shard_map/ppermute | solution.py:272
  38.4 4.8 %collective-permute-start.12 = (bf16[64,256]{1,0:T(8,128)(2,1)S(1)}, bf16[64,256]{1,0:T(8,128)(2,1)S(1)}, u32[]{:S(2)}, u32[]{:S(2)}) collective-permute-start(bf16[64,256]{1,0:T(8,128)(2,1)S(1)} %get-tuple-element.43), channel_id=1, source_target_pairs={{0,24},{8,16},{16,8},{24,0},{1,25},{9,17},{17,9},{25,1},{2,26},{10... | collective-permute-start | bytes 98312 | tf_op jit(solution)/shard_map/ppermute | solution.py:272

commit v5 on v4

--- a/solution.py
+++ b/solution.py
@@ -57,8 +57,8 @@
     for g in range(group):
         row = relabel(targets[pl.ds(part ^ ds[g], 1), :], me, share)
         picks.append((column(row, table.shape[0]) == lanes).astype(BF16))
-    picked = dot(jnp.concatenate(picks, axis=0), table).astype(BF16)
-    proj = dot(picked, weights[:hidden]).astype(BF16).astype(F32)
+    ready = dot(table, weights[:hidden]).astype(BF16)
+    proj = dot(jnp.concatenate(picks, axis=0), ready)
     starts = [pl.multiple_of((part ^ d) * width, width) for d in ds]
     x = jnp.concatenate([edge_in[pl.ds(start, width), :] for start in starts], axis=0)
     x = x.astype(F32) + proj
@@ -222,7 +222,7 @@
     half = blocks // 2
     near = [[d, d + 1] for d in range(2, half, 2)]
     far = [[d, d + 1] for d in range(half + 2, blocks, 2)]
-    return [[half, half + 1]] + near + far + [[1, 0]]
+    return [[half, half + 1]] + [near[0][:1]] + far + [near[0][1:]] + near[1:] + [[1, 0]]
 
 
 def on_device(

time: 44.2 us -> 42.6 us (0.964)
  waiting for transfers between devices: 13.1 us -> 11.3 us
  Pallas kernels: 9.28 us -> 10.3 us
  starting transfers between devices: 19.2 us -> 18.4 us
    ppermute x7, waiting for transfers between devices: 7.93 us -> 6.37 us  [on_device(): msgs[d] = lax.ppermute(sent[g], 'dst', over(blocks, d))]
    pallas_call x4 -> x5, Pallas kernels: 5.7 us -> 6.67 us  [edge_group(): pl.pallas_call(functools.partial(edge_kernel, ds, len(atoms)), out_shape=...]
    ppermute x7, starting transfers between devices: 11 us -> 10.2 us  [on_device(): msgs[d] = lax.ppermute(sent[g], 'dst', over(blocks, d))]
  transfers between devices with their start and end apart: 13 -> 13, of which waited for: 6 -> 8; matrix products, arithmetic and copies ran while one was open for 4% -> 4% of each run, Pallas kernels for 15% -> 18%
where the time goes in v5:
time: 42.6 us; the launch traced here: 42.5 us
  starting transfers between devices  18.4 us (43%)
  waiting for transfers between devices  11.3 us (27%)
  Pallas kernels  10.3 us (24%)
  other arithmetic  1.63 us (4%)
  between operations  0.8 us (2%)
    ppermute x7, starting transfers between devices, on_device(): msgs[d] = lax.ppermute(sent[g], 'dst', over(blocks, d))  10.2 us
    pallas_call x5, Pallas kernels, edge_group(): pl.pallas_call(functools.partial(edge_kernel, ds, len(atoms)), out_shape=...  6.67 us
    ppermute x7, waiting for transfers between devices, on_device(): msgs[d] = lax.ppermute(sent[g], 'dst', over(blocks, d))  6.37 us
    ppermute x3, starting transfers between devices, on_device(): held.append(lax.ppermute(atom_in, 'src', over(shards, p)))  4.63 us
    ppermute x3, starting transfers between devices, on_device(): parts.append(lax.ppermute(sums[p], 'src', over(shards, p)))  3.55 us
    ppermute x3, waiting for transfers between devices, on_device(): parts.append(lax.ppermute(sums[p], 'src', over(shards, p)))  2.65 us
    ppermute x3, waiting for transfers between devices, on_device(): held.append(lax.ppermute(atom_in, 'src', over(shards, p)))  2.32 us
    pallas_call x3, Pallas kernels, finish(): pl.pallas_call(functools.partial(finish_kernel, ds, [at for _, at in xs],...  2.1 us
  transfers between devices with their start and end apart: 13, of which 8 were waited for; matrix products, arithmetic and copies ran while one was open for 4% of the time, Pallas kernels for 18%

profile of v5, /device:TPU:0, one launch (start us, length us, event | category | flops | bytes accessed | tf_op | source)
XLA Modules:
  0.0 42.5 jit_solution(4756767406966942613)
XLA Ops:
  0.6 4.0 %collective-permute-start.2 = (bf16[64,256]{1,0:T(8,128)(2,1)}, bf16[64,256]{1,0:T(8,128)(2,1)S(1)}, u32[]{:S(2)}, u32[]{:S(2)}) collective-permute-start(bf16[64,256]{1,0:T(8,128)(2,1)} %atom_in.1), channel_id=1, source_target_pairs={{0,24},{8,16},{16,8},{24,0},{1,25},{9,17},{17,9},{25,1},{2,26},{10... | collective-permute-start | bytes 98312 | tf_op jit(solution)/shard_map/ppermute | solution.py:245
  4.6 0.5 %collective-permute-start.1 = (bf16[64,256]{1,0:T(8,128)(2,1)}, bf16[64,256]{1,0:T(8,128)(2,1)S(1)}, u32[]{:S(2)}, u32[]{:S(2)}) collective-permute-start(bf16[64,256]{1,0:T(8,128)(2,1)} %atom_in.1), channel_id=1, source_target_pairs={{0,16},{8,24},{16,0},{24,8},{1,17},{9,25},{17,1},{25,9},{2,18},{10... | collective-permute-start | bytes 98312 | tf_op jit(solution)/shard_map/ppermute | solution.py:245
  5.1 0.1 collective-permute-start
  5.3 0.0 copy-start
  5.3 0.0 copy-start.2
  5.3 0.0 copy-start.3
  5.3 0.0 copy-start.5
  5.3 0.0 copy-start.6
  5.3 0.0 copy-start.7
  5.3 1.6 %pad_maximum_fusion.refs_9_ = bf16[1792,512]{1,0:T(8,128)(2,1)S(1)} fusion(bf16[512,512]{1,0:T(8,128)(2,1)} %param.19, bf16[1024,512]{1,0:T(8,128)(2,1)} %bitcast.22, bf16[256,512]{1,0:T(8,128)(2,1)} %param.16), kind=kLoop, calls=%fused_computation | loop fusion | flops 5505024 | bytes 3670016 | tf_op jit(solution)/shard_map/concatenate | solution.py:246
  6.9 0.0 collective-permute-done.2.refs_4_
  6.9 1.8 %collective-permute-done.1.refs_3_ = bf16[64,256]{1,0:T(8,128)(2,1)S(1)} collective-permute-done((bf16[64,256]{1,0:T(8,128)(2,1)}, bf16[64,256]{1,0:T(8,128)(2,1)S(1)}, u32[]{:S(2)}, u32[]{:S(2)}) %collective-permute-start.1) | collective-permute-done | bytes 32800 | tf_op jit(solution)/shard_map/ppermute | solution.py:245
  8.7 0.5 %collective-permute-done.refs_2_ = bf16[64,256]{1,0:T(8,128)(2,1)S(1)} collective-permute-done((bf16[64,256]{1,0:T(8,128)(2,1)}, bf16[64,256]{1,0:T(8,128)(2,1)S(1)}, u32[]{:S(2)}, u32[]{:S(2)}) %collective-permute-start) | collective-permute-done | bytes 32800 | tf_op jit(solution)/shard_map/ppermute | solution.py:245
  9.3 0.0 copy-done
  9.3 0.0 copy-done.2
  9.3 0.0 copy-done.3
  9.3 0.0 copy-done.5
  9.3 0.0 copy-done.6
  9.3 0.0 copy-done.7
  9.3 1.4 %edge_group.5 = (f32[256,512]{1,0:T(8,128)S(1)}, bf16[128,512]{1,0:T(8,128)(2,1)S(1)}, bf16[128,512]{1,0:T(8,128)(2,1)S(1)}) custom-call(bf16[1024,512]{1,0:T(8,128)(2,1)S(1)} %copy-done, bf16[64,256]{1,0:T(8,128)(2,1)S(1)} %copy-done.2, bf16[64,256]{1,0:T(8,128)(2,1)S(1)} %collective-permute-done.refs_2_, ...), custom_call_target="tpu_custom_call" | custom-call | flops 536870912 | bytes 1048576 | tf_op jit(solution)/shard_map/edge_group/pallas_call | solution.py:89
  10.7 2.6 %collective-permute-start.8 = (bf16[128,512]{1,0:T(8,128)(2,1)S(1)}, bf16[128,512]{1,0:T(8,128)(2,1)S(1)}, u32[]{:S(2)}, u32[]{:S(2)}) collective-permute-start(bf16[128,512]{1,0:T(8,128)(2,1)S(1)} %get-tuple-element.35), channel_id=1, source_target_pairs={{0,4},{1,5},{2,6},{3,7},{4,0},{5,1},{6,2},{7,3},{8,12},{9,13},{10,... | collective-permute-start | bytes 393224 | tf_op jit(solution)/shard_map/ppermute | solution.py:255
  13.4 0.0 collective-permute-start.9
  13.4 1.2 %edge_group.6 = (f32[128,512]{1,0:T(8,128)S(1)}, bf16[128,512]{1,0:T(8,128)(2,1)S(1)}) custom-call(bf16[1024,512]{1,0:T(8,128)(2,1)S(1)} %copy-done, bf16[64,256]{1,0:T(8,128)(2,1)S(1)} %copy-done.2, bf16[64,256]{1,0:T(8,128)(2,1)S(1)} %collective-permute-done.refs_2_, bf16[64,256]{1,0:T(8,128)(2,1)S(1)} %collective-permute-done.1.refs_3_, ...), custom_call_target="tpu_custom_call" | custom-call | flops 268435456 | bytes 524288 | tf_op jit(solution)/shard_map/edge_group/pallas_call | solution.py:89
  14.6 1.4 %edge_group.7 = (f32[256,512]{1,0:T(8,128)S(1)}, bf16[128,512]{1,0:T(8,128)(2,1)S(1)}, bf16[128,512]{1,0:T(8,128)(2,1)S(1)}) custom-call(bf16[1024,512]{1,0:T(8,128)(2,1)S(1)} %copy-done, bf16[64,256]{1,0:T(8,128)(2,1)S(1)} %copy-done.2, bf16[64,256]{1,0:T(8,128)(2,1)S(1)} %collective-permute-done.refs_2_, ...), custom_call_target="tpu_custom_call" | custom-call | flops 536870912 | bytes 1048576 | tf_op jit(solution)/shard_map/edge_group/pallas_call | solution.py:89
  16.0 1.2 %edge_group.8 = (f32[128,512]{1,0:T(8,128)S(1)}, bf16[128,512]{1,0:T(8,128)(2,1)S(1)}) custom-call(bf16[1024,512]{1,0:T(8,128)(2,1)S(1)} %copy-done, bf16[64,256]{1,0:T(8,128)(2,1)S(1)} %copy-done.2, bf16[64,256]{1,0:T(8,128)(2,1)S(1)} %collective-permute-done.refs_2_, bf16[64,256]{1,0:T(8,128)(2,1)S(1)} %collective-permute-done.1.refs_3_, ...), custom_call_target="tpu_custom_call" | custom-call | flops 268435456 | bytes 524288 | tf_op jit(solution)/shard_map/edge_group/pallas_call | solution.py:89
  17.2 0.0 copy-start.1
  17.2 1.4 %edge_group.9 = (f32[256,512]{1,0:T(8,128)S(1)}, bf16[128,512]{1,0:T(8,128)(2,1)S(1)}, bf16[128,512]{1,0:T(8,128)(2,1)S(1)}) custom-call(bf16[1024,512]{1,0:T(8,128)(2,1)S(1)} %copy-done, bf16[64,256]{1,0:T(8,128)(2,1)S(1)} %copy-done.2, bf16[64,256]{1,0:T(8,128)(2,1)S(1)} %collective-permute-done.refs_2_, ...), custom_call_target="tpu_custom_call" | custom-call | flops 536870912 | bytes 1048576 | tf_op jit(solution)/shard_map/edge_group/pallas_call | solution.py:89
  18.7 0.5 %collective-permute-start.7 = (bf16[128,512]{1,0:T(8,128)(2,1)S(1)}, bf16[128,512]{1,0:T(8,128)(2,1)S(1)}, u32[]{:S(2)}, u32[]{:S(2)}) collective-permute-start(bf16[128,512]{1,0:T(8,128)(2,1)S(1)} %get-tuple-element.34), channel_id=1, source_target_pairs={{0,1},{1,0},{2,3},{3,2},{4,5},{5,4},{6,7},{7,6},{8,9},{9,8},{10,11... | collective-permute-start | bytes 393224 | tf_op jit(solution)/shard_map/ppermute | solution.py:255
  19.2 1.6 %collective-permute-start.5 = (bf16[128,512]{1,0:T(8,128)(2,1)S(1)}, bf16[128,512]{1,0:T(8,128)(2,1)S(1)}, u32[]{:S(2)}, u32[]{:S(2)}) collective-permute-start(bf16[128,512]{1,0:T(8,128)(2,1)S(1)} %get-tuple-element.30), channel_id=1, source_target_pairs={{0,2},{1,3},{2,0},{3,1},{4,6},{5,7},{6,4},{7,5},{8,10},{9,11},{10,... | collective-permute-start | bytes 393224 | tf_op jit(solution)/shard_map/ppermute | solution.py:255
  20.8 0.0 collective-permute-start.6
  20.8 0.5 %collective-permute-done.8.refs_6_ = bf16[128,512]{1,0:T(8,128)(2,1)S(1)} collective-permute-done((bf16[128,512]{1,0:T(8,128)(2,1)S(1)}, bf16[128,512]{1,0:T(8,128)(2,1)S(1)}, u32[]{:S(2)}, u32[]{:S(2)}) %collective-permute-start.8) | collective-permute-done | bytes 131104 | tf_op jit(solution)/shard_map/ppermute | solution.py:255
  21.2 4.4 %collective-permute-start.3 = (bf16[128,512]{1,0:T(8,128)(2,1)S(1)}, bf16[128,512]{1,0:T(8,128)(2,1)S(1)}, u32[]{:S(2)}, u32[]{:S(2)}) collective-permute-start(bf16[128,512]{1,0:T(8,128)(2,1)S(1)} %get-tuple-element.27), channel_id=1, source_target_pairs={{0,6},{1,7},{2,4},{3,5},{4,2},{5,3},{6,0},{7,1},{8,14},{9,15},{10,... | collective-permute-start | bytes 393224 | tf_op jit(solution)/shard_map/ppermute | solution.py:255
  25.7 0.0 collective-permute-done.9.refs_7_
  25.7 1.1 %collective-permute-start.4 = (bf16[128,512]{1,0:T(8,128)(2,1)S(1)}, bf16[128,512]{1,0:T(8,128)(2,1)S(1)}, u32[]{:S(2)}, u32[]{:S(2)}) collective-permute-start(bf16[128,512]{1,0:T(8,128)(2,1)S(1)} %get-tuple-element.28), channel_id=1, source_target_pairs={{0,7},{1,6},{2,5},{3,4},{4,3},{5,2},{6,1},{7,0},{8,15},{9,14},{10,... | collective-permute-start | bytes 393224 | tf_op jit(solution)/shard_map/ppermute | solution.py:255
  26.7 0.0 collective-permute-done.7.refs_5_
  26.7 0.0 copy-done.1
  26.7 0.9 %finish.3 = (bf16[1024,512]{1,0:T(8,128)(2,1)}, f32[256,256]{1,0:T(8,128)S(1)}) custom-call(f32[256,512]{1,0:T(8,128)S(1)} %get-tuple-element.32.refs_0_.refs_1_, f32[256,512]{1,0:T(8,128)S(1)} %get-tuple-element.32.refs_0_.refs_1_, f32[256,512]{1,0:T(8,128)S(1)} %get-tuple-element.24.refs_10_.refs_2_.refs_3_, ...), custom_call_target="tpu_custom_call" | custom-call | flops 268435456 | bytes 2097152 | tf_op jit(solution)/shard_map/finish/pallas_call | solution.py:189
  27.6 0.0 collective-permute-done.5.refs_2_
  27.6 2.2 %collective-permute-done.6.refs_3_ = bf16[128,512]{1,0:T(8,128)(2,1)S(1)} collective-permute-done((bf16[128,512]{1,0:T(8,128)(2,1)S(1)}, bf16[128,512]{1,0:T(8,128)(2,1)S(1)}, u32[]{:S(2)}, u32[]{:S(2)}) %collective-permute-start.6) | collective-permute-done | bytes 131104 | tf_op jit(solution)/shard_map/ppermute | solution.py:255
  29.9 0.8 %finish.4 = (bf16[1024,512]{1,0:T(8,128)(2,1)}, f32[256,256]{1,0:T(8,128)S(1)}) custom-call(f32[128,512]{1,0:T(8,128)S(1)} %get-tuple-element.25.refs_10_.refs_0_, f32[128,512]{1,0:T(8,128)S(1)} %get-tuple-element.29.refs_10_.refs_1_, bf16[128,512]{1,0:T(8,128)(2,1)S(1)} %collective-permute-done.5.refs_2_, ...), custom_call_target="tpu_custom_call", output_to_operand_aliasing={{0}: (7, {})} | custom-call | flops 134217728 | bytes 1048576 | tf_op jit(solution)/shard_map/finish/pallas_call | solution.py:189
  30.6 2.7 %collective-permute-done.3.refs_2_ = bf16[128,512]{1,0:T(8,128)(2,1)S(1)} collective-permute-done((bf16[128,512]{1,0:T(8,128)(2,1)S(1)}, bf16[128,512]{1,0:T(8,128)(2,1)S(1)}, u32[]{:S(2)}, u32[]{:S(2)}) %collective-permute-start.3) | collective-permute-done | bytes 131104 | tf_op jit(solution)/shard_map/ppermute | solution.py:255
  33.3 1.0 %collective-permute-done.4.refs_3_ = bf16[128,512]{1,0:T(8,128)(2,1)S(1)} collective-permute-done((bf16[128,512]{1,0:T(8,128)(2,1)S(1)}, bf16[128,512]{1,0:T(8,128)(2,1)S(1)}, u32[]{:S(2)}, u32[]{:S(2)}) %collective-permute-start.4) | collective-permute-done | bytes 131104 | tf_op jit(solution)/shard_map/ppermute | solution.py:255
  34.3 0.0 copy-start.4
  34.3 0.4 %finish.5 = (bf16[256,512]{1,0:T(8,128)(2,1)S(1)}, f32[64,256]{1,0:T(8,128)S(1)}, bf16[64,256]{1,0:T(8,128)(2,1)S(1)}, bf16[64,256]{1,0:T(8,128)(2,1)S(1)}, bf16[64,256]{1,0:T(8,128)(2,1)S(1)}) custom-call(f32[256,512]{1,0:T(8,128)S(1)} %get-tuple-element.26.refs_10_.refs_0_.refs_1_, f32[256,512]{1,0:T(8,128)S(1)} %get-tuple-element.26.refs_10_.refs_0_.refs_1_, ...), custom_call_target="tpu_custom_call" | custom-call | flops 134217728 | bytes 1048576 | tf_op jit(solution)/shard_map/finish/pallas_call | solution.py:189
  34.8 0.6 %collective-permute-start.10 = (bf16[64,256]{1,0:T(8,128)(2,1)S(1)}, bf16[64,256]{1,0:T(8,128)(2,1)S(1)}, u32[]{:S(2)}, u32[]{:S(2)}) collective-permute-start(bf16[64,256]{1,0:T(8,128)(2,1)S(1)} %get-tuple-element.43), channel_id=1, source_target_pairs={{0,8},{8,0},{16,24},{24,16},{1,9},{9,1},{17,25},{25,17},{2,10},{10... | collective-permute-start | bytes 98312 | tf_op jit(solution)/shard_map/ppermute | solution.py:272
  35.4 1.5 %collective-permute-start.11 = (bf16[64,256]{1,0:T(8,128)(2,1)S(1)}, bf16[64,256]{1,0:T(8,128)(2,1)S(1)}, u32[]{:S(2)}, u32[]{:S(2)}) collective-permute-start(bf16[64,256]{1,0:T(8,128)(2,1)S(1)} %get-tuple-element.44), channel_id=1, source_target_pairs={{0,16},{8,24},{16,0},{24,8},{1,17},{9,25},{17,1},{25,9},{2,18},{10... | collective-permute-start | bytes 98312 | tf_op jit(solution)/shard_map/ppermute | solution.py:272
  36.9 1.4 %collective-permute-start.12 = (bf16[64,256]{1,0:T(8,128)(2,1)S(1)}, bf16[64,256]{1,0:T(8,128)(2,1)S(1)}, u32[]{:S(2)}, u32[]{:S(2)}) collective-permute-start(bf16[64,256]{1,0:T(8,128)(2,1)S(1)} %get-tuple-element.45), channel_id=1, source_target_pairs={{0,24},{8,16},{16,8},{24,0},{1,25},{9,17},{17,9},{25,1},{2,26},{10... | collective-permute-start | bytes 98312 | tf_op jit(solution)/shard_map/ppermute | solution.py:272
  38.3 0.7 %store.1 = bf16[1024,512]{1,0:T(8,128)(2,1)} custom-call(bf16[256,512]{1,0:T(8,128)(2,1)S(1)} %get-tuple-element.40.stage, bf16[1024,512]{1,0:T(8,128)(2,1)} %get-tuple-element.41.old), custom_call_target="tpu_custom_call", output_to_operand_aliasing={{}: (1, {})} | custom-call | flops 100000000 | bytes 524288 | tf_op jit(solution)/shard_map/store/pallas_call | solution.py:122
  39.1 0.0 collective-permute-done.10.refs_1_
  39.1 0.2 collective-permute-done.11.refs_2_
  39.3 2.4 %collective-permute-done.12.refs_3_ = bf16[64,256]{1,0:T(8,128)(2,1)S(1)} collective-permute-done((bf16[64,256]{1,0:T(8,128)(2,1)S(1)}, bf16[64,256]{1,0:T(8,128)(2,1)S(1)}, u32[]{:S(2)}, u32[]{:S(2)}) %collective-permute-start.12) | collective-permute-done | bytes 32800 | tf_op jit(solution)/shard_map/ppermute | solution.py:272
  41.7 0.0 copy-done.4
  41.7 0.8 %atom_update.1 = bf16[64,256]{1,0:T(8,128)(2,1)} custom-call(bf16[64,256]{1,0:T(8,128)(2,1)S(1)} %copy-done.2, bf16[256,256]{1,0:T(8,128)(2,1)S(1)} %copy-done.4, f32[64,256]{1,0:T(8,128)S(1)} %get-tuple-element.42.refs_0_, bf16[64,256]{1,0:T(8,128)(2,1)S(1)} %collective-permute-done.10.refs_1_, bf16[64,256]{1,0:T(8,128)(2,1)S(1)} %collective-permute-done.11.refs_2_, ...), custom_call_target="tpu_custom_call" | custom-call | tf_op jit(solution)/shard_map/atom_update/pallas_call | solution.py:274
Async XLA Ops:
  0.6 6.3 %collective-permute-start.2 = (bf16[64,256]{1,0:T(8,128)(2,1)}, bf16[64,256]{1,0:T(8,128)(2,1)S(1)}, u32[]{:S(2)}, u32[]{:S(2)}) collective-permute-start(bf16[64,256]{1,0:T(8,128)(2,1)} %atom_in.1), channel_id=1, source_target_pairs={{0,24},{8,16},{16,8},{24,0},{1,25},{9,17},{17,9},{25,1},{2,26},{10... | collective-permute-start | bytes 98312 | tf_op jit(solution)/shard_map/ppermute | solution.py:245
  4.6 4.1 %collective-permute-start.1 = (bf16[64,256]{1,0:T(8,128)(2,1)}, bf16[64,256]{1,0:T(8,128)(2,1)S(1)}, u32[]{:S(2)}, u32[]{:S(2)}) collective-permute-start(bf16[64,256]{1,0:T(8,128)(2,1)} %atom_in.1), channel_id=1, source_target_pairs={{0,16},{8,24},{16,0},{24,8},{1,17},{9,25},{17,1},{25,9},{2,18},{10... | collective-permute-start | bytes 98312 | tf_op jit(solution)/shard_map/ppermute | solution.py:245
  5.1 4.1 %collective-permute-start = (bf16[64,256]{1,0:T(8,128)(2,1)}, bf16[64,256]{1,0:T(8,128)(2,1)S(1)}, u32[]{:S(2)}, u32[]{:S(2)}) collective-permute-start(bf16[64,256]{1,0:T(8,128)(2,1)} %atom_in.1), channel_id=1, source_target_pairs={{0,8},{8,0},{16,24},{24,16},{1,9},{9,1},{17,25},{25,17},{2,10},{10... | collective-permute-start | bytes 98312 | tf_op jit(solution)/shard_map/ppermute | solution.py:245
  5.3 4.0 %copy-start = (bf16[1024,512]{1,0:T(8,128)(2,1)S(1)}, bf16[1024,512]{1,0:T(8,128)(2,1)}, u32[]{:S(2)}) copy-start(bf16[1024,512]{1,0:T(8,128)(2,1)} %refs_0_.9) | copy-start | bytes 3145732
  5.3 4.0 %copy-start.2 = (bf16[64,256]{1,0:T(8,128)(2,1)S(1)}, bf16[64,256]{1,0:T(8,128)(2,1)}, u32[]{:S(2)}) copy-start(bf16[64,256]{1,0:T(8,128)(2,1)} %atom_in.1) | copy-start | bytes 98308
  5.3 4.0 %copy-start.3 = (s32[1024]{0:T(1024)S(1)}, s32[1024]{0:T(1024)}, u32[]{:S(2)}) copy-start(s32[1024]{0:T(1024)} %param.13) | copy-start | bytes 12292
  5.3 4.0 %copy-start.5 = (s32[1024]{0:T(1024)S(1)}, s32[1024]{0:T(1024)}, u32[]{:S(2)}) copy-start(s32[1024]{0:T(1024)} %param.14) | copy-start | bytes 12292
  5.3 4.0 %copy-start.6 = (f32[2,512]{1,0:T(2,128)S(1)}, f32[2,512]{1,0:T(2,128)}, u32[]{:S(2)}) copy-start(f32[2,512]{1,0:T(2,128)} %refs_8_.9) | copy-start | bytes 12292
  5.3 4.0 %copy-start.7 = (s32[1,1,8]{2,1,0:T(1,128)S(1)}, s32[1,1,8]{2,1,0:T(1,128)}, u32[]{:S(2)}) copy-start(s32[1,1,8]{2,1,0:T(1,128)} %param.15) | copy-start | bytes 100
  10.7 10.5 %collective-permute-start.8 = (bf16[128,512]{1,0:T(8,128)(2,1)S(1)}, bf16[128,512]{1,0:T(8,128)(2,1)S(1)}, u32[]{:S(2)}, u32[]{:S(2)}) collective-permute-start(bf16[128,512]{1,0:T(8,128)(2,1)S(1)} %get-tuple-element.35), channel_id=1, source_target_pairs={{0,4},{1,5},{2,6},{3,7},{4,0},{5,1},{6,2},{7,3},{8,12},{9,13},{10,... | collective-permute-start | bytes 393224 | tf_op jit(solution)/shard_map/ppermute | solution.py:255
  13.4 12.3 %collective-permute-start.9 = (bf16[128,512]{1,0:T(8,128)(2,1)S(1)}, bf16[128,512]{1,0:T(8,128)(2,1)S(1)}, u32[]{:S(2)}, u32[]{:S(2)}) collective-permute-start(bf16[128,512]{1,0:T(8,128)(2,1)S(1)} %get-tuple-element.36), channel_id=1, source_target_pairs={{0,5},{1,4},{2,7},{3,6},{4,1},{5,0},{6,3},{7,2},{8,13},{9,12},{10,... | collective-permute-start | bytes 393224 | tf_op jit(solution)/shard_map/ppermute | solution.py:255
  17.2 9.5 %copy-start.1 = (bf16[512,256]{1,0:T(8,128)(2,1)S(1)}, bf16[512,256]{1,0:T(8,128)(2,1)}, u32[]{:S(2)}) copy-start(bf16[512,256]{1,0:T(8,128)(2,1)} %refs_5_.3) | copy-start | bytes 786436
  18.7 8.1 %collective-permute-start.7 = (bf16[128,512]{1,0:T(8,128)(2,1)S(1)}, bf16[128,512]{1,0:T(8,128)(2,1)S(1)}, u32[]{:S(2)}, u32[]{:S(2)}) collective-permute-start(bf16[128,512]{1,0:T(8,128)(2,1)S(1)} %get-tuple-element.34), channel_id=1, source_target_pairs={{0,1},{1,0},{2,3},{3,2},{4,5},{5,4},{6,7},{7,6},{8,9},{9,8},{10,11... | collective-permute-start | bytes 393224 | tf_op jit(solution)/shard_map/ppermute | solution.py:255
  19.2 8.4 %collective-permute-start.5 = (bf16[128,512]{1,0:T(8,128)(2,1)S(1)}, bf16[128,512]{1,0:T(8,128)(2,1)S(1)}, u32[]{:S(2)}, u32[]{:S(2)}) collective-permute-start(bf16[128,512]{1,0:T(8,128)(2,1)S(1)} %get-tuple-element.30), channel_id=1, source_target_pairs={{0,2},{1,3},{2,0},{3,1},{4,6},{5,7},{6,4},{7,5},{8,10},{9,11},{10,... | collective-permute-start | bytes 393224 | tf_op jit(solution)/shard_map/ppermute | solution.py:255
  20.8 9.1 %collective-permute-start.6 = (bf16[128,512]{1,0:T(8,128)(2,1)S(1)}, bf16[128,512]{1,0:T(8,128)(2,1)S(1)}, u32[]{:S(2)}, u32[]{:S(2)}) collective-permute-start(bf16[128,512]{1,0:T(8,128)(2,1)S(1)} %get-tuple-element.31), channel_id=1, source_target_pairs={{0,3},{1,2},{2,1},{3,0},{4,7},{5,6},{6,5},{7,4},{8,11},{9,10},{10,... | collective-permute-start | bytes 393224 | tf_op jit(solution)/shard_map/ppermute | solution.py:255
  21.2 12.1 %collective-permute-start.3 = (bf16[128,512]{1,0:T(8,128)(2,1)S(1)}, bf16[128,512]{1,0:T(8,128)(2,1)S(1)}, u32[]{:S(2)}, u32[]{:S(2)}) collective-permute-start(bf16[128,512]{1,0:T(8,128)(2,1)S(1)} %get-tuple-element.27), channel_id=1, source_target_pairs={{0,6},{1,7},{2,4},{3,5},{4,2},{5,3},{6,0},{7,1},{8,14},{9,15},{10,... | collective-permute-start | bytes 393224 | tf_op jit(solution)/shard_map/ppermute | solution.py:255
  25.7 8.7 %collective-permute-start.4 = (bf16[128,512]{1,0:T(8,128)(2,1)S(1)}, bf16[128,512]{1,0:T(8,128)(2,1)S(1)}, u32[]{:S(2)}, u32[]{:S(2)}) collective-permute-start(bf16[128,512]{1,0:T(8,128)(2,1)S(1)} %get-tuple-element.28), channel_id=1, source_target_pairs={{0,7},{1,6},{2,5},{3,4},{4,3},{5,2},{6,1},{7,0},{8,15},{9,14},{10,... | collective-permute-start | bytes 393224 | tf_op jit(solution)/shard_map/ppermute | solution.py:255
  34.3 7.4 %copy-start.4 = (bf16[256,256]{1,0:T(8,128)(2,1)S(1)}, bf16[256,256]{1,0:T(8,128)(2,1)}, u32[]{:S(2)}) copy-start(bf16[256,256]{1,0:T(8,128)(2,1)} %w_atom.1) | copy-start | bytes 393220
  34.8 4.3 %collective-permute-start.10 = (bf16[64,256]{1,0:T(8,128)(2,1)S(1)}, bf16[64,256]{1,0:T(8,128)(2,1)S(1)}, u32[]{:S(2)}, u32[]{:S(2)}) collective-permute-start(bf16[64,256]{1,0:T(8,128)(2,1)S(1)} %get-tuple-element.43), channel_id=1, source_target_pairs={{0,8},{8,0},{16,24},{24,16},{1,9},{9,1},{17,25},{25,17},{2,10},{10... | collective-permute-start | bytes 98312 | tf_op jit(solution)/shard_map/ppermute | solution.py:272
  35.4 3.9 %collective-permute-start.11 = (bf16[64,256]{1,0:T(8,128)(2,1)S(1)}, bf16[64,256]{1,0:T(8,128)(2,1)S(1)}, u32[]{:S(2)}, u32[]{:S(2)}) collective-permute-start(bf16[64,256]{1,0:T(8,128)(2,1)S(1)} %get-tuple-element.44), channel_id=1, source_target_pairs={{0,16},{8,24},{16,0},{24,8},{1,17},{9,25},{17,1},{25,9},{2,18},{10... | collective-permute-start | bytes 98312 | tf_op jit(solution)/shard_map/ppermute | solution.py:272
  36.9 4.8 %collective-permute-start.12 = (bf16[64,256]{1,0:T(8,128)(2,1)S(1)}, bf16[64,256]{1,0:T(8,128)(2,1)S(1)}, u32[]{:S(2)}, u32[]{:S(2)}) collective-permute-start(bf16[64,256]{1,0:T(8,128)(2,1)S(1)} %get-tuple-element.45), channel_id=1, source_target_pairs={{0,24},{8,16},{16,8},{24,0},{1,25},{9,17},{17,9},{25,1},{2,26},{10... | collective-permute-start | bytes 98312 | tf_op jit(solution)/shard_map/ppermute | solution.py:272
